TPU v7x, 32 devices: a whole 2x2x4 slice. The times are simulated.
32 devices in a mesh: rows: 16 (over z, y, x), cent: 2 (over core).
Axes of the slice: x: 2, y: 2, z: 4, core: 2. Of those that a mesh axis runs over, the one named last changes fastest.
Arguments:
- points: bfloat16 [16384, 1024], P('rows'), may hold values from -8 to 8
- centroids: bfloat16 [4096, 1024], P('cent'), may hold values from -8 to 8
- assign: int32 [16384], P('rows'), may hold values from 0 to 4095, as said below
Outputs:
- nearest: float32 [2, 16384], P(None, 'rows')
- updated: bfloat16 [4096, 1024], P('cent')
Inputs may be any that keep to these rules, and one draw needn't show every extreme that they name: `assign`: split the points into aligned blocks of 1024 and the centroids into aligned groups of 128 consecutive ones: in each block at most 64 points are assigned into any one group, and in every block some group takes exactly 64 of them.
All inputs are finite; a program needn't handle non-finite values.
Results may differ from a plain program's by a relative error of at most 0.001.
Values may be sent and summed in bfloat16 or wider, within the bound.
No kernel may reach another device: no remote copies, remote signals or barrier semaphores. Data moves between devices by JAX's collectives and lax.ppermute only.
A program may use at most 64 MiB of HBM per device.

v0:
```python
import functools

import jax
import jax.numpy as jnp
from jax import lax
from jax.experimental import pallas as pl
from jax.experimental.pallas import tpu as pltpu
from jax.sharding import PartitionSpec as P


F32 = jnp.float32
BF16 = jnp.bfloat16
VMEM = pl.BlockSpec(memory_space=pltpu.VMEM)
ANY = pl.BlockSpec(memory_space=pl.ANY)
HBM = pl.BlockSpec(memory_space=pltpu.HBM)
LIMIT = 24 * 1024 * 1024
LABEL_ROWS = 8


def swap(value, mask, axis="rows"):
    size = lax.axis_size(axis)
    return lax.ppermute(value, axis, [(i, i ^ mask) for i in range(size)])


def block_min(values):
    size = lax.axis_size("cent")
    if size & (size - 1):
        return lax.pmin(values, "cent")
    mask = 1
    while mask < size:
        values = jnp.minimum(values, swap(values, mask, "cent"))
        mask *= 2
    return values


def cost(flops, moved):
    return pl.CostEstimate(flops=int(flops), bytes_accessed=int(moved), transcendentals=0)


def params():
    return pltpu.CompilerParams(vmem_limit_bytes=LIMIT)


def place_kernel(half, share, capacity, own, assign_ref, points_hbm, *refs):
    outs, (points_ref, sem) = refs[:-2], refs[-2:]
    copy = pltpu.make_async_copy(points_hbm, points_ref, sem)
    copy.start()
    me, cent = lax.axis_index("rows"), lax.axis_index("cent")
    count = assign_ref.shape[1]
    side = me // half if own else 1 - me // half
    owner = side * half + (
        lax.rem(me, half) ^ lax.broadcasted_iota(jnp.int32, (half, count), 0)
    )
    within = assign_ref[...] - (cent * 2 * half + owner) * share
    hot = (within >= 0) & (within < share)
    ones = jnp.where(hot, 1.0, 0.0).astype(F32)
    seg = 128
    upper = jnp.where(
        lax.broadcasted_iota(jnp.int32, (seg, seg), 0)
        < lax.broadcasted_iota(jnp.int32, (seg, seg), 1),
        1.0,
        0.0,
    ).astype(BF16)
    total = jnp.zeros((half, 1), F32)
    before = []
    for start in range(0, count, seg):
        piece = ones[:, start : start + seg]
        before.append(jnp.dot(piece.astype(BF16), upper, preferred_element_type=F32) + total)
        total = total + jnp.sum(piece, axis=1, keepdims=True)
    rank = jnp.where(hot, jnp.concatenate(before, axis=1), -1.0)
    label = jnp.sum(jnp.where(hot, within + 1, 0).astype(F32), axis=0, keepdims=True)
    label = jnp.transpose(jnp.broadcast_to(label, (8, count)))
    slots = lax.broadcasted_iota(jnp.int32, (capacity, count), 0).astype(F32)
    placing = jnp.concatenate(
        [jnp.where(slots == rank[m : m + 1], 1.0, 0.0).astype(BF16) for m in range(half)], axis=0
    )
    copy.wait()
    placed = jnp.dot(placing, points_ref[...], preferred_element_type=F32).astype(BF16)
    labels = jnp.dot(placing, label.astype(BF16), preferred_element_type=F32)
    labels = (jnp.transpose(labels) - 1.0).astype(BF16)
    for m in range(half):
        outs[m][:capacity, :] = placed[m * capacity : (m + 1) * capacity]
        outs[m][capacity:, :] = jnp.zeros((LABEL_ROWS, outs[m].shape[1]), BF16)
        outs[m][capacity:, :capacity] = labels[:, m * capacity : (m + 1) * capacity]


def place(own, points, assign_row, share, capacity):
    half = lax.axis_size("rows") // 2
    count, width = points.shape
    block = jax.ShapeDtypeStruct((capacity + LABEL_ROWS, width), BF16)
    return pl.pallas_call(
        functools.partial(place_kernel, half, share, capacity, own),
        out_shape=[block] * half,
        in_specs=[VMEM, HBM],
        out_specs=[VMEM] * half,
        scratch_shapes=[pltpu.VMEM((count, width), BF16), pltpu.SemaphoreType.DMA],
        compiler_params=params(),
        cost_estimate=cost(2 * half * capacity * count * width, 4 * count * width),
        name="place_own" if own else "place_other",
    )(assign_row, points)


def sum_kernel(share, capacity, *refs):
    blocks, sums_ref, counts_ref = refs[:-2], refs[-2], refs[-1]
    labels = jnp.concatenate(
        [r[capacity:, :capacity].astype(F32)[:1] for r in blocks], axis=1
    )
    chosen = jnp.where(
        lax.broadcasted_iota(jnp.int32, (share, labels.shape[1]), 0).astype(F32) == labels, 1.0, 0.0
    ).astype(F32)
    rows = jnp.concatenate([r[:capacity, :] for r in blocks], axis=0)
    sums_ref[...] = jnp.dot(chosen.astype(BF16), rows, preferred_element_type=F32)
    counts = jnp.broadcast_to(jnp.sum(chosen, axis=1, keepdims=True), (share, 8))
    counts_ref[...] = jnp.transpose(counts)


def add_up(blocks, share, capacity):
    width = blocks[0].shape[1]
    return pl.pallas_call(
        functools.partial(sum_kernel, share, capacity),
        out_shape=[jax.ShapeDtypeStruct((share, width), F32), jax.ShapeDtypeStruct((8, share), F32)],
        in_specs=[VMEM] * len(blocks),
        out_specs=[VMEM, VMEM],
        compiler_params=params(),
        cost_estimate=cost(2 * share * len(blocks) * capacity * width, 3 * share * width * 4),
    )(*blocks)


def renew_kernel(sums_ref, counts_ref, far_sums_ref, far_counts_ref, own_ref, out_ref):
    counts = jnp.transpose(counts_ref[...] + far_counts_ref[...])[:, :1]
    total = sums_ref[...] + far_sums_ref[...] + own_ref[...].astype(F32)
    out_ref[...] = (total / (counts + 1.0)).astype(BF16)


def renew(sums, counts, far_sums, far_counts, own):
    return pl.pallas_call(
        renew_kernel,
        out_shape=jax.ShapeDtypeStruct(own.shape, BF16),
        in_specs=[VMEM] * 5,
        out_specs=VMEM,
        compiler_params=params(),
        cost_estimate=cost(4 * own.size, 14 * own.size),
        name="renew",
    )(sums, counts, far_sums, far_counts, own)


def lowest(cents, columns):
    wide = cents.astype(F32)
    norms = jnp.sum(wide * wide, axis=1, keepdims=True)
    scores = norms - 2.0 * jnp.dot(cents, columns, preferred_element_type=F32)
    return jnp.min(scores.reshape(-1, 8, scores.shape[1]), axis=0)


def first_kernel(step, cents_ref, columns_ref, out_ref):
    out_ref[...] = jnp.full(out_ref.shape, jnp.inf, F32)

    @pl.loop(0, cents_ref.shape[0] // step)
    def _(i):
        start = pl.multiple_of(i * step, step)
        out_ref[...] = jnp.minimum(
            out_ref[...], lowest(cents_ref[pl.ds(start, step), :], columns_ref[...])
        )


def first_lowest(cents, columns):
    return pl.pallas_call(
        functools.partial(first_kernel, 256),
        out_shape=jax.ShapeDtypeStruct((8, columns.shape[1]), F32),
        in_specs=[VMEM, VMEM],
        out_specs=VMEM,
        compiler_params=params(),
        cost_estimate=cost(2 * cents.size * columns.shape[1], 2 * cents.size),
        name="first_lowest",
    )(cents, columns)


def arrive_kernel(share, places, fresh, *refs):
    count = len(places)
    pieces, columns_ref = refs[:count], refs[count]
    rest = refs[count + 1 :] if fresh else refs[count + 3 :]
    running_out, whole_out, sems = rest
    me = lax.axis_index("rows")
    copies = []
    for i, ((mask, row), ref) in enumerate(zip(places, pieces, strict=True)):
        start = pl.multiple_of((me ^ mask) * share + row, ref.shape[0])
        copy = pltpu.make_async_copy(
            ref, whole_out.at[pl.ds(start, ref.shape[0])], sems.at[i]
        )
        copy.start()
        copies.append(copy)
    found = lowest(jnp.concatenate([r[...] for r in pieces], axis=0), columns_ref[...])
    running_out[...] = found if fresh else jnp.minimum(refs[count + 1][...], found)
    for copy in copies:
        copy.wait()


def arrive(pieces, columns, running, whole, total, share):
    places = [(mask, row) for mask, row, _ in pieces]
    operands = [array for _, _, array in pieces]
    rows, width = sum(o.shape[0] for o in operands), operands[0].shape[1]
    fresh = running is None
    operands += [columns]
    specs = [VMEM] * len(operands)
    aliases = {}
    if not fresh:
        aliases = {len(operands) + 1: 1}
        operands += [running, whole]
        specs += [VMEM, ANY]
    return pl.pallas_call(
        functools.partial(arrive_kernel, share, places, fresh),
        out_shape=[
            jax.ShapeDtypeStruct((8, columns.shape[1]), F32),
            jax.ShapeDtypeStruct((total, width), BF16),
        ],
        in_specs=specs,
        out_specs=[VMEM, ANY],
        scratch_shapes=[pltpu.SemaphoreType.DMA((len(places),))],
        input_output_aliases=aliases,
        compiler_params=params(),
        cost_estimate=cost(2 * rows * width * columns.shape[1], 4 * rows * width),
    )(*operands)


def halves(points, centroids, assign, share, capacity):
    rows_count = lax.axis_size("rows")
    half = rows_count // 2
    me = lax.axis_index("rows")
    total = rows_count * share
    own = lax.dynamic_slice_in_dim(centroids, me * share, share, 0)
    assign_row = assign.reshape(1, -1)

    far = place(False, points, assign_row, share, capacity)
    far = [far[0]] + [swap(far[m], m) for m in range(1, half)]
    near = place(True, points, assign_row, share, capacity)
    near = [near[0]] + [swap(near[m], m) for m in range(1, half)]
    far_sums, far_counts = add_up(far, share, capacity)
    far_sums, late = lax.optimization_barrier((far_sums, points))
    far_sums = swap(far_sums, half)
    far_counts = swap(far_counts, half)
    columns = jnp.transpose(late)
    first = first_lowest(centroids, columns)
    near_sums, near_counts = add_up(near, share, capacity)
    pnorm = jnp.sum(jnp.square(late.astype(F32)), axis=1)
    first, pnorm, own, far_sums = lax.optimization_barrier((first, pnorm, own, far_sums))
    piece = renew(near_sums, near_counts, far_sums, far_counts, own)

    cut = share // 2
    running, whole = None, None
    columns_count = rows_count // 4
    for k in range(columns_count):
        one = piece if k == 0 else swap(piece, 4 * k)
        one_x, one_y = swap(one, 1), swap(one, 2)
        low = swap(one_y[:cut], 1)
        high = swap(one_x[cut:], 2)
        m = 4 * k
        sides = [(m, 0, one), (m ^ 1, 0, one_x), (m ^ 2, 0, one_y)]
        corner = [(m ^ 3, 0, low), (m ^ 3, cut, high)]
        if k == columns_count - 1:
            running, whole = arrive(sides, columns, running, whole, total, share)
            running, whole = arrive(corner, columns, running, whole, total, share)
        else:
            running, whole = arrive(sides + corner, columns, running, whole, total, share)
    both = jnp.stack([jnp.min(first, axis=0), jnp.min(running, axis=0)])
    nearest = block_min((pnorm[None, :] + both) / points.shape[1])
    return nearest, whole


def smallest(points, pnorm, cents):
    cnorm = jnp.sum(jnp.square(cents.astype(F32)), axis=1)
    dots = lax.dot_general(points, cents, (((1,), (1,)), ((), ())), preferred_element_type=F32)
    return jnp.min((pnorm[:, None] - 2.0 * dots + cnorm[None, :]) / points.shape[1], axis=1)


def plain(points, centroids, assign, share, capacity):
    blocksize = centroids.shape[0]
    count_pts = points.shape[0]
    pnorm = jnp.sum(jnp.square(points.astype(F32)), axis=1)
    first = smallest(points, pnorm, centroids)
    relative = assign - lax.axis_index("cent") * blocksize
    own = lax.dynamic_slice_in_dim(centroids, lax.axis_index("rows") * share, share, 0)
    rows_count = lax.axis_size("rows")
    inside = (relative >= 0) & (relative < blocksize)
    owners = jnp.where(inside, relative // share, rows_count)
    offsets = jnp.where(inside, relative - relative // share * share, 0)
    owner_hot = owners[:, None] == lax.broadcasted_iota(jnp.int32, (count_pts, rows_count), 1)
    earlier = lax.broadcasted_iota(jnp.int32, (count_pts, count_pts), 1) < lax.broadcasted_iota(
        jnp.int32, (count_pts, count_pts), 0
    )
    before = jnp.dot(earlier.astype(BF16), owner_hot.astype(BF16), preferred_element_type=F32)
    ranking = jnp.sum(jnp.where(owner_hot, before, 0.0), axis=1).astype(jnp.int32)
    slot_index = jnp.where(inside, owners * capacity + ranking, -1)
    placing = (
        lax.broadcasted_iota(jnp.int32, (rows_count * capacity, count_pts), 0)
        == slot_index[None, :]
    )
    outgoing = jnp.dot(placing.astype(BF16), points, preferred_element_type=F32).astype(BF16)
    labels = (jnp.sum(jnp.where(placing, offsets[None, :] + 1, 0), axis=1) - 1).astype(BF16)
    arrived = lax.all_to_all(outgoing, "rows", split_axis=0, concat_axis=0, tiled=True)
    arrived_labels = lax.all_to_all(labels, "rows", split_axis=0, concat_axis=0, tiled=True)
    chosen = (
        lax.broadcasted_iota(jnp.int32, (share, arrived.shape[0]), 0)
        == arrived_labels.astype(jnp.int32)[None, :]
    )
    sums = jnp.dot(chosen.astype(BF16), arrived, preferred_element_type=F32)
    counts = jnp.sum(chosen.astype(F32), axis=1)
    piece = ((sums + own.astype(F32)) / (counts[:, None] + 1.0)).astype(BF16)
    updated = lax.all_gather(piece, "rows", axis=0, tiled=True)
    second = smallest(points, pnorm, updated)
    return block_min(jnp.stack([first, second])), updated


def fits(rows_count, share, capacity, count, width, blocksize):
    return (
        rows_count >= 8
        and rows_count & (rows_count - 1) == 0
        and share % 128 == 0
        and share <= 256
        and capacity % 16 == 0
        and count % 128 == 0
        and width % 128 == 0
        and blocksize % 256 == 0
    )


def per_device(points, centroids, assign):
    rows_count = lax.axis_size("rows")
    share = centroids.shape[0] // rows_count
    groups = rows_count * lax.axis_size("cent")
    capacity = max(2, 2 * points.shape[0] // groups)
    good = fits(rows_count, share, capacity, *points.shape, centroids.shape[0])
    if not good:
        return plain(points, centroids, assign, share, capacity)
    return halves(points, centroids, assign, share, capacity)


def solution(mesh):
    return jax.shard_map(
        per_device,
        mesh=mesh,
        in_specs=(P("rows", None), P("cent", None), P("rows")),
        out_specs=(P(None, "rows"), P("cent", None)),
        check_vma=False,
    )
```

profile of v0, /device:TPU:0, one launch (start us, length us, event | category | flops | bytes accessed | tf_op | source)
XLA Modules:
  0.0 116.2 jit_solution(12753404811971490313)
XLA Ops:
  0.6 1.6 %copy-done = bf16[1024,1024]{1,0:T(8,128)(2,1)S(1)} copy-done((bf16[1024,1024]{1,0:T(8,128)(2,1)S(1)}, bf16[1024,1024]{1,0:T(8,128)(2,1)}, u32[]{:S(2)}) %copy-start) | copy-done | bytes 2097176
  2.9 2.0 %place_other.1 = (bf16[72,1024]{1,0:T(8,128)(2,1)S(1)}, bf16[72,1024]{1,0:T(8,128)(2,1)S(1)}, bf16[72,1024]{1,0:T(8,128)(2,1)S(1)}, bf16[72,1024]{1,0:T(8,128)(2...) custom-call(s32[1,1024]{1,0:T(1,128)S(1)} %bitcast.10, ...), custom_call_target="tpu_custom_call" | custom-call | flops 1073741824 | bytes 4194304 | tf_op jit(solution)/shard_map/place_other/pallas_call | solution.py:91
  4.9 3.0 %collective-permute-start = (bf16[72,1024]{1,0:T(8,128)(2,1)S(1)}, bf16[72,1024]{1,0:T(8,128)(2,1)S(1)}, u32[]{:S(2)}, u32[]{:S(2)}) collective-permute-start(bf16[72,1024]{1,0:T(8,128)(2,1)S(1)} %get-tuple-element.39), channel_id=1, source_target_pairs={{0,2},{2,0},{4,6},{6,4},{8,10},{10,8},{12,14},{14,12},{16,18},{18,... | collective-permute-start | bytes 442376 | tf_op jit(solution)/shard_map/ppermute | solution.py:22
  9.5 2.0 %collective-permute-start.3 = (bf16[72,1024]{1,0:T(8,128)(2,1)S(1)}, bf16[72,1024]{1,0:T(8,128)(2,1)S(1)}, u32[]{:S(2)}, u32[]{:S(2)}) collective-permute-start(bf16[72,1024]{1,0:T(8,128)(2,1)S(1)} %get-tuple-element.42), channel_id=1, source_target_pairs={{0,8},{2,10},{4,12},{6,14},{8,0},{10,2},{12,4},{14,6},{16,24},{18,... | collective-permute-start | bytes 442376 | tf_op jit(solution)/shard_map/ppermute | solution.py:22
  12.9 2.5 %collective-permute-start.5 = (bf16[72,1024]{1,0:T(8,128)(2,1)S(1)}, bf16[72,1024]{1,0:T(8,128)(2,1)}, u32[]{:S(2)}, u32[]{:S(2)}) collective-permute-start(bf16[72,1024]{1,0:T(8,128)(2,1)S(1)} %get-tuple-element.44), channel_id=1, source_target_pairs={{0,12},{2,14},{4,8},{6,10},{8,4},{10,6},{12,0},{14,2},{16,28},{18,... | collective-permute-start | bytes 442376 | tf_op jit(solution)/shard_map/ppermute | solution.py:22
  15.4 1.6 %collective-permute-start.6 = (bf16[72,1024]{1,0:T(8,128)(2,1)S(1)}, bf16[72,1024]{1,0:T(8,128)(2,1)}, u32[]{:S(2)}, u32[]{:S(2)}) collective-permute-start(bf16[72,1024]{1,0:T(8,128)(2,1)S(1)} %get-tuple-element.45), channel_id=1, source_target_pairs={{0,14},{2,12},{4,10},{6,8},{8,6},{10,4},{12,2},{14,0},{16,30},{18,... | collective-permute-start | bytes 442376 | tf_op jit(solution)/shard_map/ppermute | solution.py:22
  17.7 2.7 %place_own.1 = (bf16[72,1024]{1,0:T(8,128)(2,1)S(1)}, bf16[72,1024]{1,0:T(8,128)(2,1)S(1)}, bf16[72,1024]{1,0:T(8,128)(2,1)S(1)}, bf16[72,1024]{1,0:T(8,128)(2,1...) custom-call(s32[1,1024]{1,0:T(1,128)S(1)} %bitcast.11, ...), custom_call_target="tpu_custom_call" | custom-call | flops 1073741824 | bytes 4194304 | tf_op jit(solution)/shard_map/place_own/pallas_call | solution.py:91
  21.5 2.3 %collective-permute-start.10 = (bf16[72,1024]{1,0:T(8,128)(2,1)}, bf16[72,1024]{1,0:T(8,128)(2,1)S(1)}, u32[]{:S(2)}, u32[]{:S(2)}) collective-permute-start(bf16[72,1024]{1,0:T(8,128)(2,1)} %get-tuple-element.54), channel_id=1, source_target_pairs={{0,6},{2,4},{4,2},{6,0},{8,14},{10,12},{12,10},{14,8},{16,22},{18,... | collective-permute-start | bytes 442376 | tf_op jit(solution)/shard_map/ppermute | solution.py:22
  24.4 2.7 %collective-permute-start.12 = (bf16[72,1024]{1,0:T(8,128)(2,1)}, bf16[72,1024]{1,0:T(8,128)(2,1)}, u32[]{:S(2)}, u32[]{:S(2)}) collective-permute-start(bf16[72,1024]{1,0:T(8,128)(2,1)} %get-tuple-element.56), channel_id=1, source_target_pairs={{0,10},{2,8},{4,14},{6,12},{8,2},{10,0},{12,6},{14,4},{16,26},{18,... | collective-permute-start | bytes 442376 | tf_op jit(solution)/shard_map/ppermute | solution.py:22
  29.9 2.9 %copy.9 = bf16[1024,1024]{0,1:T(8,128)(2,1)S(1)} copy(bf16[1024,1024]{1,0:T(8,128)(2,1)} %points_hbm.3) | data formatting | bytes 4194304 | tf_op jit(solution)/shard_map/optimization_barrier | solution.py:237
  32.7 2.7 %collective-permute-start.7 = (f32[128,1024]{1,0:T(8,128)S(1)}, f32[128,1024]{1,0:T(8,128)S(1)}, u32[]{:S(2)}, u32[]{:S(2)}) collective-permute-start(f32[128,1024]{1,0:T(8,128)S(1)} %get-tuple-element.48), channel_id=1, source_target_pairs={{0,16},{2,18},{4,20},{6,22},{8,24},{10,26},{12,28},{14,30},{16,0},... | collective-permute-start | bytes 1572872 | tf_op jit(solution)/shard_map/ppermute | solution.py:22
  35.4 2.2 %copy-done.13 = bf16[2048,1024]{1,0:T(8,128)(2,1)S(1)} copy-done((bf16[2048,1024]{1,0:T(8,128)(2,1)S(1)}, bf16[2048,1024]{1,0:T(8,128)(2,1)}, u32[]{:S(2)}) %copy-start.13) | copy-done | bytes 4194328
  37.6 6.0 %first_lowest.1 = f32[8,1024]{1,0:T(8,128)S(1)} custom-call(bf16[2048,1024]{1,0:T(8,128)(2,1)S(1)} %copy-done.13, bf16[1024,1024]{1,0:T(8,128)(2,1)S(1)} %bitcast.4), custom_call_target="tpu_custom_call" | custom-call | flops 4294967296 | bytes 4194304 | tf_op jit(solution)/shard_map/first_lowest/pallas_call | solution.py:166
  45.3 1.8 %collective-permute-start.8 = (bf16[72,1024]{1,0:T(8,128)(2,1)S(1)}, bf16[72,1024]{1,0:T(8,128)(2,1)S(1)}, u32[]{:S(2)}, u32[]{:S(2)}) collective-permute-start(bf16[72,1024]{1,0:T(8,128)(2,1)S(1)} %get-tuple-element.52), channel_id=1, source_target_pairs={{0,2},{2,0},{4,6},{6,4},{8,10},{10,8},{12,14},{14,12},{16,18},{18,... | collective-permute-start | bytes 442376 | tf_op jit(solution)/shard_map/ppermute | solution.py:22
  49.5 8.2 %collective-permute-done.14.refs_7_ = bf16[72,1024]{1,0:T(8,128)(2,1)S(1)} collective-permute-done((bf16[72,1024]{1,0:T(8,128)(2,1)S(1)}, bf16[72,1024]{1,0:T(8,128)(2,1)S(1)}, u32[]{:S(2)}, u32[]{:S(2)}) %collective-permute-start.14) | collective-permute-done | bytes 147488 | tf_op jit(solution)/shard_map/ppermute | solution.py:22
  61.2 3.4 %collective-permute-start.21 = (bf16[128,1024]{1,0:T(8,128)(2,1)S(1)}, bf16[128,1024]{1,0:T(8,128)(2,1)S(1)}, u32[]{:S(2)}, u32[]{:S(2)}) collective-permute-start(bf16[128,1024]{1,0:T(8,128)(2,1)S(1)} %renew.1.refs_0_), channel_id=1, source_target_pairs={{0,16},{2,18},{4,20},{6,22},{8,24},{10,26},{12,28},{14,30},{16,0},... | collective-permute-start | bytes 786440 | tf_op jit(solution)/shard_map/ppermute | solution.py:22
  66.1 5.9 %collective-permute-start.28 = (bf16[128,1024]{1,0:T(8,128)(2,1)S(1)}, bf16[128,1024]{1,0:T(8,128)(2,1)S(1)}, u32[]{:S(2)}, u32[]{:S(2)}) collective-permute-start(bf16[128,1024]{1,0:T(8,128)(2,1)S(1)} %collective-permute-done.26.refs_0_), channel_id=1, source_target_pairs={{0,4},{2,6},{4,0},{6,2},{8,12},{10,14},{12,8},{14,10},{16,20},{18,... | collective-permute-start | bytes 786440 | tf_op jit(solution)/shard_map/ppermute | solution.py:22
  74.7 3.8 %collective-permute-done.21.refs_0_ = bf16[128,1024]{1,0:T(8,128)(2,1)S(1)} collective-permute-done((bf16[128,1024]{1,0:T(8,128)(2,1)S(1)}, bf16[128,1024]{1,0:T(8,128)(2,1)S(1)}, u32[]{:S(2)}, u32[]{:S(2)}) %collective-permute-start.21) | collective-permute-done | bytes 262176 | tf_op jit(solution)/shard_map/ppermute | solution.py:22
  83.9 1.9 %collective-permute-start.34 = (bf16[64,1024]{1,0:T(8,128)(2,1)}, bf16[64,1024]{1,0:T(8,128)(2,1)}, u32[]{:S(2)}, u32[]{:S(2)}) collective-permute-start(bf16[64,1024]{1,0:T(8,128)(2,1)} %slice.39), channel_id=1, source_target_pairs={{0,4},{2,6},{4,0},{6,2},{8,12},{10,14},{12,8},{14,10},{16,20},{18,... | collective-permute-start | bytes 393224 | tf_op jit(solution)/shard_map/ppermute | solution.py:22
  93.1 3.0 %collective-permute-start.24 = (bf16[64,1024]{1,0:T(8,128)(2,1)S(1)}, bf16[64,1024]{1,0:T(8,128)(2,1)S(1)}, u32[]{:S(2)}, u32[]{:S(2)}) collective-permute-start(bf16[64,1024]{1,0:T(8,128)(2,1)S(1)} %slice.34), channel_id=1, source_target_pairs={{0,2},{2,0},{4,6},{6,4},{8,10},{10,8},{12,14},{14,12},{16,18},{18,... | collective-permute-start | bytes 393224 | tf_op jit(solution)/shard_map/ppermute | solution.py:22
  100.4 2.8 %shard_map.52 = (f32[8,1024]{1,0:T(8,128)S(1)}, bf16[2048,1024]{1,0:T(8,128)(2,1)}) custom-call(bf16[128,1024]{1,0:T(8,128)(2,1)S(1)} %copy-done.7, bf16[128,1024]{1,0:T(8,128)(2,1)S(1)} %copy-done.11, bf16[128,1024]{1,0:T(8,128)(2,1)S(1)} %copy-done.9, bf16[64,1024]{1,0:T(8,128)(2,1)S(1)} %copy-done.17, bf16[64,1024]{1,0:T(8,128)(2,1)} %collective-permute-done.34.refs_4_, ...), custom_call_target="tpu_custom_call" | custom-call | flops 1073741824 | bytes 2097152 | tf_op jit(solution)/shard_map/pallas_call | solution.py:209
  105.0 2.8 %shard_map.53 = (f32[8,1024]{1,0:T(8,128)S(1)}, bf16[2048,1024]{1,0:T(8,128)(2,1)}) custom-call(bf16[128,1024]{1,0:T(8,128)(2,1)S(1)} %copy-done.5, bf16[128,1024]{1,0:T(8,128)(2,1)S(1)} %collective-permute-done.27.refs_1_, bf16[128,1024]{1,0:T(8,128)(2,1)S(1)} %collective-permute-done.28.refs_2_, ...), custom_call_target="tpu_custom_call", output_to_operand_aliasing={{1}: (7, {})} | custom-call | flops 1073741824 | bytes 2097152 | tf_op jit(solution)/shard_map/pallas_call | solution.py:209
  107.8 2.9 %shard_map.54 = (f32[8,1024]{1,0:T(8,128)S(1)}, bf16[2048,1024]{1,0:T(8,128)(2,1)}) custom-call(bf16[128,1024]{1,0:T(8,128)(2,1)S(1)} %copy-done.3, bf16[128,1024]{1,0:T(8,128)(2,1)} %collective-permute-done.22.refs_1_, bf16[128,1024]{1,0:T(8,128)(2,1)S(1)} %collective-permute-done.23.refs_2_, ...), custom_call_target="tpu_custom_call", output_to_operand_aliasing={{1}: (7, {})} | custom-call | flops 1073741824 | bytes 2097152 | tf_op jit(solution)/shard_map/pallas_call | solution.py:209
  110.7 2.6 %shard_map.55 = (f32[8,1024]{1,0:T(8,128)S(1)}, bf16[2048,1024]{1,0:T(8,128)(2,1)}) custom-call(bf16[128,1024]{1,0:T(8,128)(2,1)} %collective-permute-done.16.refs_0_, bf16[128,1024]{1,0:T(8,128)(2,1)S(1)} %collective-permute-done.19.refs_1_, bf16[128,1024]{1,0:T(8,128)(2,1)S(1)} %collective-permute-done.17.refs_2_, ...), custom_call_target="tpu_custom_call", output_to_operand_aliasing={{1}: (5, {})} | custom-call | flops 805306368 | bytes 1572864 | tf_op jit(solution)/shard_map/pallas_call | solution.py:209
  (114 shorter events, 42.1 us)
Async XLA Ops:
  9.5 12.0 %collective-permute-start.2 = (bf16[72,1024]{1,0:T(8,128)(2,1)S(1)}, bf16[72,1024]{1,0:T(8,128)(2,1)S(1)}, u32[]{:S(2)}, u32[]{:S(2)}) collective-permute-start(bf16[72,1024]{1,0:T(8,128)(2,1)S(1)} %get-tuple-element.41), channel_id=1, source_target_pairs={{0,6},{2,4},{4,2},{6,0},{8,14},{10,12},{12,10},{14,8},{16,22},{18,... | collective-permute-start | bytes 442376 | tf_op jit(solution)/shard_map/ppermute | solution.py:22
  9.5 14.3 %collective-permute-start.3 = (bf16[72,1024]{1,0:T(8,128)(2,1)S(1)}, bf16[72,1024]{1,0:T(8,128)(2,1)S(1)}, u32[]{:S(2)}, u32[]{:S(2)}) collective-permute-start(bf16[72,1024]{1,0:T(8,128)(2,1)S(1)} %get-tuple-element.42), channel_id=1, source_target_pairs={{0,8},{2,10},{4,12},{6,14},{8,0},{10,2},{12,4},{14,6},{16,24},{18,... | collective-permute-start | bytes 442376 | tf_op jit(solution)/shard_map/ppermute | solution.py:22
  11.5 12.8 %collective-permute-start.4 = (bf16[72,1024]{1,0:T(8,128)(2,1)S(1)}, bf16[72,1024]{1,0:T(8,128)(2,1)S(1)}, u32[]{:S(2)}, u32[]{:S(2)}) collective-permute-start(bf16[72,1024]{1,0:T(8,128)(2,1)S(1)} %get-tuple-element.43), channel_id=1, source_target_pairs={{0,10},{2,8},{4,14},{6,12},{8,2},{10,0},{12,6},{14,4},{16,26},{18,... | collective-permute-start | bytes 442376 | tf_op jit(solution)/shard_map/ppermute | solution.py:22
  12.9 14.2 %collective-permute-start.5 = (bf16[72,1024]{1,0:T(8,128)(2,1)S(1)}, bf16[72,1024]{1,0:T(8,128)(2,1)}, u32[]{:S(2)}, u32[]{:S(2)}) collective-permute-start(bf16[72,1024]{1,0:T(8,128)(2,1)S(1)} %get-tuple-element.44), channel_id=1, source_target_pairs={{0,12},{2,14},{4,8},{6,10},{8,4},{10,6},{12,0},{14,2},{16,28},{18,... | collective-permute-start | bytes 442376 | tf_op jit(solution)/shard_map/ppermute | solution.py:22
  15.4 13.1 %collective-permute-start.6 = (bf16[72,1024]{1,0:T(8,128)(2,1)S(1)}, bf16[72,1024]{1,0:T(8,128)(2,1)}, u32[]{:S(2)}, u32[]{:S(2)}) collective-permute-start(bf16[72,1024]{1,0:T(8,128)(2,1)S(1)} %get-tuple-element.45), channel_id=1, source_target_pairs={{0,14},{2,12},{4,10},{6,8},{8,6},{10,4},{12,2},{14,0},{16,30},{18,... | collective-permute-start | bytes 442376 | tf_op jit(solution)/shard_map/ppermute | solution.py:22
  21.5 22.7 %collective-permute-start.10 = (bf16[72,1024]{1,0:T(8,128)(2,1)}, bf16[72,1024]{1,0:T(8,128)(2,1)S(1)}, u32[]{:S(2)}, u32[]{:S(2)}) collective-permute-start(bf16[72,1024]{1,0:T(8,128)(2,1)} %get-tuple-element.54), channel_id=1, source_target_pairs={{0,6},{2,4},{4,2},{6,0},{8,14},{10,12},{12,10},{14,8},{16,22},{18,... | collective-permute-start | bytes 442376 | tf_op jit(solution)/shard_map/ppermute | solution.py:22
  23.8 21.5 %collective-permute-start.11 = (bf16[72,1024]{1,0:T(8,128)(2,1)}, bf16[72,1024]{1,0:T(8,128)(2,1)}, u32[]{:S(2)}, u32[]{:S(2)}) collective-permute-start(bf16[72,1024]{1,0:T(8,128)(2,1)} %get-tuple-element.55), channel_id=1, source_target_pairs={{0,8},{2,10},{4,12},{6,14},{8,0},{10,2},{12,4},{14,6},{16,24},{18,... | collective-permute-start | bytes 442376 | tf_op jit(solution)/shard_map/ppermute | solution.py:22
  24.4 22.8 %collective-permute-start.12 = (bf16[72,1024]{1,0:T(8,128)(2,1)}, bf16[72,1024]{1,0:T(8,128)(2,1)}, u32[]{:S(2)}, u32[]{:S(2)}) collective-permute-start(bf16[72,1024]{1,0:T(8,128)(2,1)} %get-tuple-element.56), channel_id=1, source_target_pairs={{0,10},{2,8},{4,14},{6,12},{8,2},{10,0},{12,6},{14,4},{16,26},{18,... | collective-permute-start | bytes 442376 | tf_op jit(solution)/shard_map/ppermute | solution.py:22
  27.1 22.0 %collective-permute-start.13 = (bf16[72,1024]{1,0:T(8,128)(2,1)}, bf16[72,1024]{1,0:T(8,128)(2,1)}, u32[]{:S(2)}, u32[]{:S(2)}) collective-permute-start(bf16[72,1024]{1,0:T(8,128)(2,1)} %get-tuple-element.57), channel_id=1, source_target_pairs={{0,12},{2,14},{4,8},{6,10},{8,4},{10,6},{12,0},{14,2},{16,28},{18,... | collective-permute-start | bytes 442376 | tf_op jit(solution)/shard_map/ppermute | solution.py:22
  32.7 26.4 %collective-permute-start.7 = (f32[128,1024]{1,0:T(8,128)S(1)}, f32[128,1024]{1,0:T(8,128)S(1)}, u32[]{:S(2)}, u32[]{:S(2)}) collective-permute-start(f32[128,1024]{1,0:T(8,128)S(1)} %get-tuple-element.48), channel_id=1, source_target_pairs={{0,16},{2,18},{4,20},{6,22},{8,24},{10,26},{12,28},{14,30},{16,0},... | collective-permute-start | bytes 1572872 | tf_op jit(solution)/shard_map/ppermute | solution.py:22
  44.2 13.5 %collective-permute-start.14 = (bf16[72,1024]{1,0:T(8,128)(2,1)S(1)}, bf16[72,1024]{1,0:T(8,128)(2,1)S(1)}, u32[]{:S(2)}, u32[]{:S(2)}) collective-permute-start(bf16[72,1024]{1,0:T(8,128)(2,1)S(1)} %copy-done.15), channel_id=1, source_target_pairs={{0,14},{2,12},{4,10},{6,8},{8,6},{10,4},{12,2},{14,0},{16,30},{18,... | collective-permute-start | bytes 442376 | tf_op jit(solution)/shard_map/ppermute | solution.py:22
  45.3 12.4 %collective-permute-start.8 = (bf16[72,1024]{1,0:T(8,128)(2,1)S(1)}, bf16[72,1024]{1,0:T(8,128)(2,1)S(1)}, u32[]{:S(2)}, u32[]{:S(2)}) collective-permute-start(bf16[72,1024]{1,0:T(8,128)(2,1)S(1)} %get-tuple-element.52), channel_id=1, source_target_pairs={{0,2},{2,0},{4,6},{6,4},{8,10},{10,8},{12,14},{14,12},{16,18},{18,... | collective-permute-start | bytes 442376 | tf_op jit(solution)/shard_map/ppermute | solution.py:22
  59.4 12.6 %collective-permute-start.32 = (bf16[128,1024]{1,0:T(8,128)(2,1)S(1)}, bf16[128,1024]{1,0:T(8,128)(2,1)S(1)}, u32[]{:S(2)}, u32[]{:S(2)}) collective-permute-start(bf16[128,1024]{1,0:T(8,128)(2,1)S(1)} %renew.1.refs_0_), channel_id=1, source_target_pairs={{0,4},{2,6},{4,0},{6,2},{8,12},{10,14},{12,8},{14,10},{16,20},{18,... | collective-permute-start | bytes 786440 | tf_op jit(solution)/shard_map/ppermute | solution.py:22
  60.1 13.7 %collective-permute-start.31 = (bf16[128,1024]{1,0:T(8,128)(2,1)S(1)}, bf16[128,1024]{1,0:T(8,128)(2,1)S(1)}, u32[]{:S(2)}, u32[]{:S(2)}) collective-permute-start(bf16[128,1024]{1,0:T(8,128)(2,1)S(1)} %renew.1.refs_0_), channel_id=1, source_target_pairs={{0,2},{2,0},{4,6},{6,4},{8,10},{10,8},{12,14},{14,12},{16,18},{18,... | collective-permute-start | bytes 786440 | tf_op jit(solution)/shard_map/ppermute | solution.py:22
  61.2 17.3 %collective-permute-start.21 = (bf16[128,1024]{1,0:T(8,128)(2,1)S(1)}, bf16[128,1024]{1,0:T(8,128)(2,1)S(1)}, u32[]{:S(2)}, u32[]{:S(2)}) collective-permute-start(bf16[128,1024]{1,0:T(8,128)(2,1)S(1)} %renew.1.refs_0_), channel_id=1, source_target_pairs={{0,16},{2,18},{4,20},{6,22},{8,24},{10,26},{12,28},{14,30},{16,0},... | collective-permute-start | bytes 786440 | tf_op jit(solution)/shard_map/ppermute | solution.py:22
  64.6 15.2 %collective-permute-start.16 = (bf16[128,1024]{1,0:T(8,128)(2,1)S(1)}, bf16[128,1024]{1,0:T(8,128)(2,1)}, u32[]{:S(2)}, u32[]{:S(2)}) collective-permute-start(bf16[128,1024]{1,0:T(8,128)(2,1)S(1)} %renew.1.refs_0_), channel_id=1, source_target_pairs={{0,24},{2,26},{4,28},{6,30},{8,16},{10,18},{12,20},{14,22},{16,8},... | collective-permute-start | bytes 786440 | tf_op jit(solution)/shard_map/ppermute | solution.py:22
  66.1 16.3 %collective-permute-start.28 = (bf16[128,1024]{1,0:T(8,128)(2,1)S(1)}, bf16[128,1024]{1,0:T(8,128)(2,1)S(1)}, u32[]{:S(2)}, u32[]{:S(2)}) collective-permute-start(bf16[128,1024]{1,0:T(8,128)(2,1)S(1)} %collective-permute-done.26.refs_0_), channel_id=1, source_target_pairs={{0,4},{2,6},{4,0},{6,2},{8,12},{10,14},{12,8},{14,10},{16,20},{18,... | collective-permute-start | bytes 786440 | tf_op jit(solution)/shard_map/ppermute | solution.py:22
  72.0 11.9 %collective-permute-start.27 = (bf16[128,1024]{1,0:T(8,128)(2,1)S(1)}, bf16[128,1024]{1,0:T(8,128)(2,1)S(1)}, u32[]{:S(2)}, u32[]{:S(2)}) collective-permute-start(bf16[128,1024]{1,0:T(8,128)(2,1)S(1)} %collective-permute-done.26.refs_0_), channel_id=1, source_target_pairs={{0,2},{2,0},{4,6},{6,4},{8,10},{10,8},{12,14},{14,12},{16,18},{18,... | collective-permute-start | bytes 786440 | tf_op jit(solution)/shard_map/ppermute | solution.py:22
  82.4 13.7 %collective-permute-start.17 = (bf16[128,1024]{1,0:T(8,128)(2,1)}, bf16[128,1024]{1,0:T(8,128)(2,1)S(1)}, u32[]{:S(2)}, u32[]{:S(2)}) collective-permute-start(bf16[128,1024]{1,0:T(8,128)(2,1)} %collective-permute-done.16.refs_0_), channel_id=1, source_target_pairs={{0,4},{2,6},{4,0},{6,2},{8,12},{10,14},{12,8},{14,10},{16,20},{18,... | collective-permute-start | bytes 786440 | tf_op jit(solution)/shard_map/ppermute | solution.py:22
  82.4 20.9 %collective-permute-start.19 = (bf16[128,1024]{1,0:T(8,128)(2,1)}, bf16[128,1024]{1,0:T(8,128)(2,1)S(1)}, u32[]{:S(2)}, u32[]{:S(2)}) collective-permute-start(bf16[128,1024]{1,0:T(8,128)(2,1)} %collective-permute-done.16.refs_0_), channel_id=1, source_target_pairs={{0,2},{2,0},{4,6},{6,4},{8,10},{10,8},{12,14},{14,12},{16,18},{18,... | collective-permute-start | bytes 786440 | tf_op jit(solution)/shard_map/ppermute | solution.py:22
  87.7 16.7 %collective-permute-start.29 = (bf16[64,1024]{1,0:T(8,128)(2,1)}, bf16[64,1024]{1,0:T(8,128)(2,1)S(1)}, u32[]{:S(2)}, u32[]{:S(2)}) collective-permute-start(bf16[64,1024]{1,0:T(8,128)(2,1)} %slice.36), channel_id=1, source_target_pairs={{0,2},{2,0},{4,6},{6,4},{8,10},{10,8},{12,14},{14,12},{16,18},{18,... | collective-permute-start | bytes 393224 | tf_op jit(solution)/shard_map/ppermute | solution.py:22
  89.1 15.9 %collective-permute-start.30 = (bf16[64,1024]{1,0:T(8,128)(2,1)}, bf16[64,1024]{1,0:T(8,128)(2,1)}, u32[]{:S(2)}, u32[]{:S(2)}) collective-permute-start(bf16[64,1024]{1,0:T(8,128)(2,1)} %slice.37), channel_id=1, source_target_pairs={{0,4},{2,6},{4,0},{6,2},{8,12},{10,14},{12,8},{14,10},{16,20},{18,... | collective-permute-start | bytes 393224 | tf_op jit(solution)/shard_map/ppermute | solution.py:22
  93.1 14.7 %collective-permute-start.24 = (bf16[64,1024]{1,0:T(8,128)(2,1)S(1)}, bf16[64,1024]{1,0:T(8,128)(2,1)S(1)}, u32[]{:S(2)}, u32[]{:S(2)}) collective-permute-start(bf16[64,1024]{1,0:T(8,128)(2,1)S(1)} %slice.34), channel_id=1, source_target_pairs={{0,2},{2,0},{4,6},{6,4},{8,10},{10,8},{12,14},{14,12},{16,18},{18,... | collective-permute-start | bytes 393224 | tf_op jit(solution)/shard_map/ppermute | solution.py:22
  96.1 11.7 %collective-permute-start.25 = (bf16[64,1024]{1,0:T(8,128)(2,1)S(1)}, bf16[64,1024]{1,0:T(8,128)(2,1)S(1)}, u32[]{:S(2)}, u32[]{:S(2)}) collective-permute-start(bf16[64,1024]{1,0:T(8,128)(2,1)S(1)} %slice.35), channel_id=1, source_target_pairs={{0,4},{2,6},{4,0},{6,2},{8,12},{10,14},{12,8},{14,10},{16,20},{18,... | collective-permute-start | bytes 393224 | tf_op jit(solution)/shard_map/ppermute | solution.py:22
  (32 other events, 225.6 us)
where the time goes:
time: 117 us; the launch traced here: 116 us
  starting transfers between devices  52.8 us (45%)
  Pallas kernels  25.7 us (22%)
  local copies, waits for them, and re-layouts  17.7 us (15%)
  waiting for transfers between devices  17.1 us (15%)
  other arithmetic  1.89 us (2%)
    ppermute x36, starting transfers between devices, swap(): return lax.ppermute(value, axis, [(i, i ^ mask) for i in range(size)])  52.8 us
    ppermute x36, waiting for transfers between devices, swap(): return lax.ppermute(value, axis, [(i, i ^ mask) for i in range(size)])  17.1 us
    pallas_call x5, Pallas kernels, arrive(): pl.pallas_call(functools.partial(arrive_kernel, share, places, fresh), ou...  12.1 us
    unnamed x40, local copies, waits for them, and re-layouts  10.9 us
    pallas_call x1, Pallas kernels, first_lowest(): pl.pallas_call(functools.partial(first_kernel, 256), out_shape=jax.ShapeD...  5.98 us
    pallas_call x2, Pallas kernels, place(): pl.pallas_call(functools.partial(place_kernel, half, share, capacity, own...  4.7 us
    optimization_barrier x1, local copies, waits for them, and re-layouts, halves(): far_sums, late = lax.optimization_barrier((far_sums, points))  2.86 us
    pallas_call x2, Pallas kernels, add_up(): pl.pallas_call(functools.partial(sum_kernel, share, capacity), out_shape=...  2.75 us
  transfers between devices with their start and end apart: 36, of which 8 were waited for; matrix products, arithmetic and copies ran while one was open for 7% of the time, Pallas kernels for 19%

commit v1 on v0

--- a/solution.py
+++ b/solution.py
@@ -41,19 +41,9 @@
     return pltpu.CompilerParams(vmem_limit_bytes=LIMIT)
 
 
-def place_kernel(half, share, capacity, own, assign_ref, points_hbm, *refs):
-    outs, (points_ref, sem) = refs[:-2], refs[-2:]
-    copy = pltpu.make_async_copy(points_hbm, points_ref, sem)
-    copy.start()
+def rank_kernel(half, share, assign_ref, far_ref, near_ref, far_label_ref, near_label_ref):
     me, cent = lax.axis_index("rows"), lax.axis_index("cent")
     count = assign_ref.shape[1]
-    side = me // half if own else 1 - me // half
-    owner = side * half + (
-        lax.rem(me, half) ^ lax.broadcasted_iota(jnp.int32, (half, count), 0)
-    )
-    within = assign_ref[...] - (cent * 2 * half + owner) * share
-    hot = (within >= 0) & (within < share)
-    ones = jnp.where(hot, 1.0, 0.0).astype(F32)
     seg = 128
     upper = jnp.where(
         lax.broadcasted_iota(jnp.int32, (seg, seg), 0)
@@ -61,22 +51,52 @@
         1.0,
         0.0,
     ).astype(BF16)
-    total = jnp.zeros((half, 1), F32)
-    before = []
-    for start in range(0, count, seg):
-        piece = ones[:, start : start + seg]
-        before.append(jnp.dot(piece.astype(BF16), upper, preferred_element_type=F32) + total)
-        total = total + jnp.sum(piece, axis=1, keepdims=True)
-    rank = jnp.where(hot, jnp.concatenate(before, axis=1), -1.0)
-    label = jnp.sum(jnp.where(hot, within + 1, 0).astype(F32), axis=0, keepdims=True)
-    label = jnp.transpose(jnp.broadcast_to(label, (8, count)))
+    low = lax.rem(me, half) ^ lax.broadcasted_iota(jnp.int32, (half, count), 0)
+    for side, rank_ref, label_ref in (
+        (1 - me // half, far_ref, far_label_ref),
+        (me // half, near_ref, near_label_ref),
+    ):
+        within = assign_ref[...] - (cent * 2 * half + side * half + low) * share
+        hot = (within >= 0) & (within < share)
+        ones = jnp.where(hot, 1.0, 0.0).astype(F32)
+        total = jnp.zeros((half, 1), F32)
+        before = []
+        for start in range(0, count, seg):
+            piece = ones[:, start : start + seg]
+            before.append(jnp.dot(piece.astype(BF16), upper, preferred_element_type=F32) + total)
+            total = total + jnp.sum(piece, axis=1, keepdims=True)
+        rank_ref[...] = jnp.where(hot, jnp.concatenate(before, axis=1), -1.0)
+        label = jnp.sum(jnp.where(hot, within + 1, 0).astype(F32), axis=0, keepdims=True)
+        label_ref[...] = jnp.transpose(jnp.broadcast_to(label, (8, count))).astype(BF16)
+
+
+def ranks(assign_row, half, share):
+    count = assign_row.shape[1]
+    rank = jax.ShapeDtypeStruct((half, count), F32)
+    label = jax.ShapeDtypeStruct((count, 8), BF16)
+    return pl.pallas_call(
+        functools.partial(rank_kernel, half, share),
+        out_shape=[rank, rank, label, label],
+        in_specs=[VMEM],
+        out_specs=[VMEM] * 4,
+        compiler_params=params(),
+        cost_estimate=cost(4 * half * count * 128, 64 * count),
+        name="ranks",
+    )(assign_row)
+
+
+def place_kernel(half, capacity, rank_ref, label_ref, points_ref, *outs):
+    count = points_ref.shape[0]
     slots = lax.broadcasted_iota(jnp.int32, (capacity, count), 0).astype(F32)
     placing = jnp.concatenate(
-        [jnp.where(slots == rank[m : m + 1], 1.0, 0.0).astype(BF16) for m in range(half)], axis=0
-    )
-    copy.wait()
+        [
+            jnp.where(slots == rank_ref[m : m + 1, :], 1.0, 0.0).astype(BF16)
+            for m in range(half)
+        ],
+        axis=0,
+    )
     placed = jnp.dot(placing, points_ref[...], preferred_element_type=F32).astype(BF16)
-    labels = jnp.dot(placing, label.astype(BF16), preferred_element_type=F32)
+    labels = jnp.dot(placing, label_ref[...], preferred_element_type=F32)
     labels = (jnp.transpose(labels) - 1.0).astype(BF16)
     for m in range(half):
         outs[m][:capacity, :] = placed[m * capacity : (m + 1) * capacity]
@@ -84,20 +104,18 @@
         outs[m][capacity:, :capacity] = labels[:, m * capacity : (m + 1) * capacity]
 
 
-def place(own, points, assign_row, share, capacity):
-    half = lax.axis_size("rows") // 2
+def place(rank, label, points, capacity):
+    half = rank.shape[0]
     count, width = points.shape
     block = jax.ShapeDtypeStruct((capacity + LABEL_ROWS, width), BF16)
     return pl.pallas_call(
-        functools.partial(place_kernel, half, share, capacity, own),
+        functools.partial(place_kernel, half, capacity),
         out_shape=[block] * half,
-        in_specs=[VMEM, HBM],
+        in_specs=[VMEM] * 3,
         out_specs=[VMEM] * half,
-        scratch_shapes=[pltpu.VMEM((count, width), BF16), pltpu.SemaphoreType.DMA],
         compiler_params=params(),
         cost_estimate=cost(2 * half * capacity * count * width, 4 * count * width),
-        name="place_own" if own else "place_other",
-    )(assign_row, points)
+    )(rank, label, points)
 
 
 def sum_kernel(share, capacity, *refs):
@@ -229,9 +247,10 @@
     own = lax.dynamic_slice_in_dim(centroids, me * share, share, 0)
     assign_row = assign.reshape(1, -1)
 
-    far = place(False, points, assign_row, share, capacity)
+    far_rank, near_rank, far_label, near_label = ranks(assign_row, half, share)
+    far = place(far_rank, far_label, points, capacity)
     far = [far[0]] + [swap(far[m], m) for m in range(1, half)]
-    near = place(True, points, assign_row, share, capacity)
+    near = place(near_rank, near_label, points, capacity)
     near = [near[0]] + [swap(near[m], m) for m in range(1, half)]
     far_sums, far_counts = add_up(far, share, capacity)
     far_sums, late = lax.optimization_barrier((far_sums, points))
@@ -244,25 +263,30 @@
     first, pnorm, own, far_sums = lax.optimization_barrier((first, pnorm, own, far_sums))
     piece = renew(near_sums, near_counts, far_sums, far_counts, own)
 
-    cut = share // 2
     running, whole = None, None
     columns_count = rows_count // 4
+    sets, corners = [], []
     for k in range(columns_count):
         one = piece if k == 0 else swap(piece, 4 * k)
         one_x, one_y = swap(one, 1), swap(one, 2)
-        low = swap(one_y[:cut], 1)
-        high = swap(one_x[cut:], 2)
+        corner = swap(one_y, 1) if k % 2 == 0 else swap(one_x, 2)
         m = 4 * k
-        sides = [(m, 0, one), (m ^ 1, 0, one_x), (m ^ 2, 0, one_y)]
-        corner = [(m ^ 3, 0, low), (m ^ 3, cut, high)]
-        if k == columns_count - 1:
-            running, whole = arrive(sides, columns, running, whole, total, share)
-            running, whole = arrive(corner, columns, running, whole, total, share)
-        else:
-            running, whole = arrive(sides + corner, columns, running, whole, total, share)
+        sets.append([(m, 0, one), (m ^ 1, 0, one_x), (m ^ 2, 0, one_y)])
+        corners.append((m ^ 3, 0, corner))
+    for name, group in groups_of(columns_count):
+        members = [p for k in group for p in sets[k]] if name != "last" else []
+        if name != "sides":
+            members += [corners[k] for k in group]
+        running, whole = arrive(members, columns, running, whole, total, share)
     both = jnp.stack([jnp.min(first, axis=0), jnp.min(running, axis=0)])
     nearest = block_min((pnorm[None, :] + both) / points.shape[1])
     return nearest, whole
+
+
+def groups_of(columns_count):
+    early = [("set", (k,)) for k in range(columns_count - 2)]
+    late = (columns_count - 2, columns_count - 1)
+    return early + [("sides", late), ("last", late)]
 
 
 def smallest(points, pnorm, cents):

time: 117 us -> 111 us (0.949)
  starting transfers between devices: 52.8 us -> 43.9 us
  local copies, waits for them, and re-layouts: 17.7 us -> 21.3 us
  waiting for transfers between devices: 17.1 us -> 20.6 us
  Pallas kernels: 25.7 us -> 22.8 us
    ppermute x36 -> x32, starting transfers between devices: 52.8 us -> 43.9 us  [swap(): return lax.ppermute(value, axis, [(i, i ^ mask) for i in range(size)])]
    unnamed x40 -> x50, local copies, waits for them, and re-layouts: 10.9 us -> 17.5 us
    ppermute x36 -> x32, waiting for transfers between devices: 17.1 us -> 20.6 us  [swap(): return lax.ppermute(value, axis, [(i, i ^ mask) for i in range(size)])]
    slice x8 -> x0, local copies, waits for them, and re-layouts: 2.96 us -> none  [the longest x4 2.27 us: halves(): high = swap(one_x[cut:], 2)]
    pallas_call x5 -> x4, Pallas kernels: 12.1 us -> 9.79 us  [arrive(): pl.pallas_call(functools.partial(arrive_kernel, share, places, fresh), ou...]
    pallas_call x2 -> x3, Pallas kernels: 4.7 us -> 4.27 us  [the longest x2 4 us: place(): pl.pallas_call(functools.partial(place_kernel, half, capacity), out_shape...]
  transfers between devices with their start and end apart: 36 -> 32, of which waited for: 8 -> 6; matrix products, arithmetic and copies ran while one was open for 7% -> 4% of each run, Pallas kernels for 19% -> 17%
where the time goes in v1:
time: 111 us
  starting transfers between devices  43.9 us (40%)
  Pallas kernels  22.8 us (21%)
  local copies, waits for them, and re-layouts  21.3 us (19%)
  waiting for transfers between devices  20.6 us (19%)
  other arithmetic  1.13 us (1%)
    ppermute x32, starting transfers between devices, swap(): return lax.ppermute(value, axis, [(i, i ^ mask) for i in range(size)])  43.9 us
    ppermute x32, waiting for transfers between devices, swap(): return lax.ppermute(value, axis, [(i, i ^ mask) for i in range(size)])  20.6 us
    unnamed x50, local copies, waits for them, and re-layouts  17.5 us
    pallas_call x4, Pallas kernels, arrive(): pl.pallas_call(functools.partial(arrive_kernel, share, places, fresh), ou...  9.79 us
    pallas_call x1, Pallas kernels, first_lowest(): pl.pallas_call(functools.partial(first_kernel, 256), out_shape=jax.ShapeD...  5.8 us
    pallas_call x2, Pallas kernels, place(): pl.pallas_call(functools.partial(place_kernel, half, capacity), out_shape...  4 us
    optimization_barrier x1, local copies, waits for them, and re-layouts, halves(): far_sums, late = lax.optimization_barrier((far_sums, points))  2.85 us
    pallas_call x2, Pallas kernels, add_up(): pl.pallas_call(functools.partial(sum_kernel, share, capacity), out_shape=...  2.75 us
  transfers between devices with their start and end apart: 32, of which 6 were waited for; matrix products, arithmetic and copies ran while one was open for 4% of the time, Pallas kernels for 17%

profile of v1, /device:TPU:0, one launch (start us, length us, event | category | flops | bytes accessed | tf_op | source)
XLA Modules:
  0.0 110.7 jit_solution(7887557674738449456)
XLA Ops:
  3.2 2.4 %shard_map.50 = (bf16[72,1024]{1,0:T(8,128)(2,1)S(1)}, bf16[72,1024]{1,0:T(8,128)(2,1)S(1)}, bf16[72,1024]{1,0:T(8,128)(2,1)S(1)}, bf16[72,1024]{1,0:T(8,128)(2,...) custom-call(f32[8,1024]{1,0:T(8,128)S(1)} %get-tuple-element.40.rank, ...), custom_call_target="tpu_custom_call" | custom-call | flops 1073741824 | bytes 4194304 | tf_op jit(solution)/shard_map/pallas_call | solution.py:111
  5.6 3.0 %collective-permute-start = (bf16[72,1024]{1,0:T(8,128)(2,1)S(1)}, bf16[72,1024]{1,0:T(8,128)(2,1)S(1)}, u32[]{:S(2)}, u32[]{:S(2)}) collective-permute-start(bf16[72,1024]{1,0:T(8,128)(2,1)S(1)} %get-tuple-element.43), channel_id=1, source_target_pairs={{0,2},{2,0},{4,6},{6,4},{8,10},{10,8},{12,14},{14,12},{16,18},{18,... | collective-permute-start | bytes 442376 | tf_op jit(solution)/shard_map/ppermute | solution.py:22
  10.1 2.1 %collective-permute-start.3 = (bf16[72,1024]{1,0:T(8,128)(2,1)}, bf16[72,1024]{1,0:T(8,128)(2,1)S(1)}, u32[]{:S(2)}, u32[]{:S(2)}) collective-permute-start(bf16[72,1024]{1,0:T(8,128)(2,1)} %get-tuple-element.46), channel_id=1, source_target_pairs={{0,8},{2,10},{4,12},{6,14},{8,0},{10,2},{12,4},{14,6},{16,24},{18,... | collective-permute-start | bytes 442376 | tf_op jit(solution)/shard_map/ppermute | solution.py:22
  13.5 2.5 %collective-permute-start.5 = (bf16[72,1024]{1,0:T(8,128)(2,1)}, bf16[72,1024]{1,0:T(8,128)(2,1)}, u32[]{:S(2)}, u32[]{:S(2)}) collective-permute-start(bf16[72,1024]{1,0:T(8,128)(2,1)} %get-tuple-element.48), channel_id=1, source_target_pairs={{0,12},{2,14},{4,8},{6,10},{8,4},{10,6},{12,0},{14,2},{16,28},{18,... | collective-permute-start | bytes 442376 | tf_op jit(solution)/shard_map/ppermute | solution.py:22
  16.1 1.6 %collective-permute-start.6 = (bf16[72,1024]{1,0:T(8,128)(2,1)}, bf16[72,1024]{1,0:T(8,128)(2,1)}, u32[]{:S(2)}, u32[]{:S(2)}) collective-permute-start(bf16[72,1024]{1,0:T(8,128)(2,1)} %get-tuple-element.49), channel_id=1, source_target_pairs={{0,14},{2,12},{4,10},{6,8},{8,6},{10,4},{12,2},{14,0},{16,30},{18,... | collective-permute-start | bytes 442376 | tf_op jit(solution)/shard_map/ppermute | solution.py:22
  17.7 1.6 %shard_map.52 = (bf16[72,1024]{1,0:T(8,128)(2,1)S(1)}, bf16[72,1024]{1,0:T(8,128)(2,1)S(1)}, bf16[72,1024]{1,0:T(8,128)(2,1)S(1)}, bf16[72,1024]{1,0:T(8,128)(2,...) custom-call(f32[8,1024]{1,0:T(8,128)S(1)} %get-tuple-element.55.rank, ...), custom_call_target="tpu_custom_call" | custom-call | flops 1073741824 | bytes 4194304 | tf_op jit(solution)/shard_map/pallas_call | solution.py:111
  24.3 2.4 %collective-permute-start.10 = (bf16[72,1024]{1,0:T(8,128)(2,1)}, bf16[72,1024]{1,0:T(8,128)(2,1)S(1)}, u32[]{:S(2)}, u32[]{:S(2)}) collective-permute-start(bf16[72,1024]{1,0:T(8,128)(2,1)} %copy-done.23), channel_id=1, source_target_pairs={{0,6},{2,4},{4,2},{6,0},{8,14},{10,12},{12,10},{14,8},{16,22},{18,... | collective-permute-start | bytes 442376 | tf_op jit(solution)/shard_map/ppermute | solution.py:22
  27.2 2.4 %collective-permute-start.12 = (bf16[72,1024]{1,0:T(8,128)(2,1)}, bf16[72,1024]{1,0:T(8,128)(2,1)}, u32[]{:S(2)}, u32[]{:S(2)}) collective-permute-start(bf16[72,1024]{1,0:T(8,128)(2,1)} %copy-done.21), channel_id=1, source_target_pairs={{0,10},{2,8},{4,14},{6,12},{8,2},{10,0},{12,6},{14,4},{16,26},{18,... | collective-permute-start | bytes 442376 | tf_op jit(solution)/shard_map/ppermute | solution.py:22
  33.2 2.9 %copy.8 = bf16[1024,1024]{0,1:T(8,128)(2,1)S(1)} copy(bf16[1024,1024]{1,0:T(8,128)(2,1)} %points_ref.3) | data formatting | bytes 4194304 | tf_op jit(solution)/shard_map/optimization_barrier | solution.py:256
  36.1 2.7 %collective-permute-start.7 = (f32[128,1024]{1,0:T(8,128)}, f32[128,1024]{1,0:T(8,128)S(1)}, u32[]{:S(2)}, u32[]{:S(2)}) collective-permute-start(f32[128,1024]{1,0:T(8,128)} %copy-done.7), channel_id=1, source_target_pairs={{0,16},{2,18},{4,20},{6,22},{8,24},{10,26},{12,28},{14,30},{16,0},... | collective-permute-start | bytes 1572872 | tf_op jit(solution)/shard_map/ppermute | solution.py:22
  38.8 2.2 %copy-done.6 = bf16[2048,1024]{1,0:T(8,128)(2,1)S(1)} copy-done((bf16[2048,1024]{1,0:T(8,128)(2,1)S(1)}, bf16[2048,1024]{1,0:T(8,128)(2,1)}, u32[]{:S(2)}) %copy-start.6) | copy-done | bytes 4194328
  41.0 5.8 %first_lowest.1 = f32[8,1024]{1,0:T(8,128)S(1)} custom-call(bf16[2048,1024]{1,0:T(8,128)(2,1)S(1)} %copy-done.6, bf16[1024,1024]{1,0:T(8,128)(2,1)S(1)} %bitcast.4), custom_call_target="tpu_custom_call" | custom-call | flops 4294967296 | bytes 4194304 | tf_op jit(solution)/shard_map/first_lowest/pallas_call | solution.py:184
  52.2 9.6 %collective-permute-done.14.refs_7_ = bf16[72,1024]{1,0:T(8,128)(2,1)S(1)} collective-permute-done((bf16[72,1024]{1,0:T(8,128)(2,1)S(1)}, bf16[72,1024]{1,0:T(8,128)(2,1)S(1)}, u32[]{:S(2)}, u32[]{:S(2)}) %collective-permute-start.14) | collective-permute-done | bytes 147488 | tf_op jit(solution)/shard_map/ppermute | solution.py:22
  65.3 1.8 %collective-permute-start.16 = (bf16[128,1024]{1,0:T(8,128)(2,1)S(1)}, bf16[128,1024]{1,0:T(8,128)(2,1)S(1)}, u32[]{:S(2)}, u32[]{:S(2)}) collective-permute-start(bf16[128,1024]{1,0:T(8,128)(2,1)S(1)} %renew.1.refs_0_), channel_id=1, source_target_pairs={{0,16},{2,18},{4,20},{6,22},{8,24},{10,26},{12,28},{14,30},{16,0},... | collective-permute-start | bytes 786440 | tf_op jit(solution)/shard_map/ppermute | solution.py:22
  67.2 2.5 %collective-permute-start.19 = (bf16[128,1024]{1,0:T(8,128)(2,1)S(1)}, bf16[128,1024]{1,0:T(8,128)(2,1)S(1)}, u32[]{:S(2)}, u32[]{:S(2)}) collective-permute-start(bf16[128,1024]{1,0:T(8,128)(2,1)S(1)} %renew.1.refs_0_), channel_id=1, source_target_pairs={{0,24},{2,26},{4,28},{6,30},{8,16},{10,18},{12,20},{14,22},{16,8},... | collective-permute-start | bytes 786440 | tf_op jit(solution)/shard_map/ppermute | solution.py:22
  70.4 3.2 %collective-permute-done.24.refs_0_ = bf16[128,1024]{1,0:T(8,128)(2,1)S(1)} collective-permute-done((bf16[128,1024]{1,0:T(8,128)(2,1)S(1)}, bf16[128,1024]{1,0:T(8,128)(2,1)S(1)}, u32[]{:S(2)}, u32[]{:S(2)}) %collective-permute-start.24) | collective-permute-done | bytes 262176 | tf_op jit(solution)/shard_map/ppermute | solution.py:22
  77.0 2.3 %collective-permute-start.26 = (bf16[128,1024]{1,0:T(8,128)(2,1)S(1)}, bf16[128,1024]{1,0:T(8,128)(2,1)S(1)}, u32[]{:S(2)}, u32[]{:S(2)}) collective-permute-start(bf16[128,1024]{1,0:T(8,128)(2,1)S(1)} %collective-permute-done.24.refs_0_), channel_id=1, source_target_pairs={{0,4},{2,6},{4,0},{6,2},{8,12},{10,14},{12,8},{14,10},{16,20},{18,... | collective-permute-start | bytes 786440 | tf_op jit(solution)/shard_map/ppermute | solution.py:22
  79.3 3.1 %collective-permute-done.16.refs_0_ = bf16[128,1024]{1,0:T(8,128)(2,1)S(1)} collective-permute-done((bf16[128,1024]{1,0:T(8,128)(2,1)S(1)}, bf16[128,1024]{1,0:T(8,128)(2,1)S(1)}, u32[]{:S(2)}, u32[]{:S(2)}) %collective-permute-start.16) | collective-permute-done | bytes 262176 | tf_op jit(solution)/shard_map/ppermute | solution.py:22
  85.0 3.4 %collective-permute-done.30.refs_3_ = bf16[128,1024]{1,0:T(8,128)(2,1)S(1)} collective-permute-done((bf16[128,1024]{1,0:T(8,128)(2,1)S(1)}, bf16[128,1024]{1,0:T(8,128)(2,1)S(1)}, u32[]{:S(2)}, u32[]{:S(2)}) %collective-permute-start.30) | collective-permute-done | bytes 262176 | tf_op jit(solution)/shard_map/ppermute | solution.py:22
  90.7 1.7 %collective-permute-start.23 = (bf16[128,1024]{1,0:T(8,128)(2,1)S(1)}, bf16[128,1024]{1,0:T(8,128)(2,1)}, u32[]{:S(2)}, u32[]{:S(2)}) collective-permute-start(bf16[128,1024]{1,0:T(8,128)(2,1)S(1)} %collective-permute-done.19.refs_3_), channel_id=1, source_target_pairs={{0,4},{2,6},{4,0},{6,2},{8,12},{10,14},{12,8},{14,10},{16,20},{18,... | collective-permute-start | bytes 786440 | tf_op jit(solution)/shard_map/ppermute | solution.py:22
  92.4 1.7 %collective-permute-start.18 = (bf16[128,1024]{1,0:T(8,128)(2,1)S(1)}, bf16[128,1024]{1,0:T(8,128)(2,1)S(1)}, u32[]{:S(2)}, u32[]{:S(2)}) collective-permute-start(bf16[128,1024]{1,0:T(8,128)(2,1)S(1)} %collective-permute-done.17.refs_2_), channel_id=1, source_target_pairs={{0,2},{2,0},{4,6},{6,4},{8,10},{10,8},{12,14},{14,12},{16,18},{18,... | collective-permute-start | bytes 786440 | tf_op jit(solution)/shard_map/ppermute | solution.py:22
  98.0 1.9 %shard_map.54 = (f32[8,1024]{1,0:T(8,128)S(1)}, bf16[2048,1024]{1,0:T(8,128)(2,1)}) custom-call(bf16[128,1024]{1,0:T(8,128)(2,1)S(1)} %copy-done.5, bf16[128,1024]{1,0:T(8,128)(2,1)S(1)} %copy-done.11, bf16[128,1024]{1,0:T(8,128)(2,1)S(1)} %copy-done.9, bf16[128,1024]{1,0:T(8,128)(2,1)S(1)} %copy-done.13, bf16[1024,1024]{1,0:T(8,128)(2,1)S(1)} %bitcast.5), custom_call_target="tpu_custom_call" | custom-call | flops 1073741824 | bytes 2097152 | tf_op jit(solution)/shard_map/pallas_call | solution.py:227
  100.9 2.9 %shard_map.55 = (f32[8,1024]{1,0:T(8,128)S(1)}, bf16[2048,1024]{1,0:T(8,128)(2,1)}) custom-call(bf16[128,1024]{1,0:T(8,128)(2,1)S(1)} %collective-permute-done.24.refs_0_, bf16[128,1024]{1,0:T(8,128)(2,1)S(1)} %collective-permute-done.25.refs_1_, bf16[128,1024]{1,0:T(8,128)(2,1)S(1)} %copy-done.3, ...), custom_call_target="tpu_custom_call", output_to_operand_aliasing={{1}: (6, {})} | custom-call | flops 1073741824 | bytes 2097152 | tf_op jit(solution)/shard_map/pallas_call | solution.py:227
  103.8 3.7 %shard_map.56 = (f32[8,1024]{1,0:T(8,128)S(1)}, bf16[2048,1024]{1,0:T(8,128)(2,1)}) custom-call(bf16[128,1024]{1,0:T(8,128)(2,1)S(1)} %collective-permute-done.16.refs_0_, bf16[128,1024]{1,0:T(8,128)(2,1)} %collective-permute-done.22.refs_1_, bf16[128,1024]{1,0:T(8,128)(2,1)S(1)} %collective-permute-done.17.refs_2_, ...), custom_call_target="tpu_custom_call", output_to_operand_aliasing={{1}: (8, {})} | custom-call | flops 1610612736 | bytes 3145728 | tf_op jit(solution)/shard_map/pallas_call | solution.py:227
  (108 shorter events, 40.5 us)
Async XLA Ops:
  10.1 14.3 %collective-permute-start.2 = (bf16[72,1024]{1,0:T(8,128)(2,1)}, bf16[72,1024]{1,0:T(8,128)(2,1)S(1)}, u32[]{:S(2)}, u32[]{:S(2)}) collective-permute-start(bf16[72,1024]{1,0:T(8,128)(2,1)} %get-tuple-element.45), channel_id=1, source_target_pairs={{0,6},{2,4},{4,2},{6,0},{8,14},{10,12},{12,10},{14,8},{16,22},{18,... | collective-permute-start | bytes 442376 | tf_op jit(solution)/shard_map/ppermute | solution.py:22
  10.1 16.7 %collective-permute-start.3 = (bf16[72,1024]{1,0:T(8,128)(2,1)}, bf16[72,1024]{1,0:T(8,128)(2,1)S(1)}, u32[]{:S(2)}, u32[]{:S(2)}) collective-permute-start(bf16[72,1024]{1,0:T(8,128)(2,1)} %get-tuple-element.46), channel_id=1, source_target_pairs={{0,8},{2,10},{4,12},{6,14},{8,0},{10,2},{12,4},{14,6},{16,24},{18,... | collective-permute-start | bytes 442376 | tf_op jit(solution)/shard_map/ppermute | solution.py:22
  12.1 15.1 %collective-permute-start.4 = (bf16[72,1024]{1,0:T(8,128)(2,1)}, bf16[72,1024]{1,0:T(8,128)(2,1)S(1)}, u32[]{:S(2)}, u32[]{:S(2)}) collective-permute-start(bf16[72,1024]{1,0:T(8,128)(2,1)} %get-tuple-element.47), channel_id=1, source_target_pairs={{0,10},{2,8},{4,14},{6,12},{8,2},{10,0},{12,6},{14,4},{16,26},{18,... | collective-permute-start | bytes 442376 | tf_op jit(solution)/shard_map/ppermute | solution.py:22
  13.5 16.2 %collective-permute-start.5 = (bf16[72,1024]{1,0:T(8,128)(2,1)}, bf16[72,1024]{1,0:T(8,128)(2,1)}, u32[]{:S(2)}, u32[]{:S(2)}) collective-permute-start(bf16[72,1024]{1,0:T(8,128)(2,1)} %get-tuple-element.48), channel_id=1, source_target_pairs={{0,12},{2,14},{4,8},{6,10},{8,4},{10,6},{12,0},{14,2},{16,28},{18,... | collective-permute-start | bytes 442376 | tf_op jit(solution)/shard_map/ppermute | solution.py:22
  16.1 15.0 %collective-permute-start.6 = (bf16[72,1024]{1,0:T(8,128)(2,1)}, bf16[72,1024]{1,0:T(8,128)(2,1)}, u32[]{:S(2)}, u32[]{:S(2)}) collective-permute-start(bf16[72,1024]{1,0:T(8,128)(2,1)} %get-tuple-element.49), channel_id=1, source_target_pairs={{0,14},{2,12},{4,10},{6,8},{8,6},{10,4},{12,2},{14,0},{16,30},{18,... | collective-permute-start | bytes 442376 | tf_op jit(solution)/shard_map/ppermute | solution.py:22
  24.3 22.4 %collective-permute-start.10 = (bf16[72,1024]{1,0:T(8,128)(2,1)}, bf16[72,1024]{1,0:T(8,128)(2,1)S(1)}, u32[]{:S(2)}, u32[]{:S(2)}) collective-permute-start(bf16[72,1024]{1,0:T(8,128)(2,1)} %copy-done.23), channel_id=1, source_target_pairs={{0,6},{2,4},{4,2},{6,0},{8,14},{10,12},{12,10},{14,8},{16,22},{18,... | collective-permute-start | bytes 442376 | tf_op jit(solution)/shard_map/ppermute | solution.py:22
  26.8 21.6 %collective-permute-start.11 = (bf16[72,1024]{1,0:T(8,128)(2,1)}, bf16[72,1024]{1,0:T(8,128)(2,1)}, u32[]{:S(2)}, u32[]{:S(2)}) collective-permute-start(bf16[72,1024]{1,0:T(8,128)(2,1)} %copy-done.22), channel_id=1, source_target_pairs={{0,8},{2,10},{4,12},{6,14},{8,0},{10,2},{12,4},{14,6},{16,24},{18,... | collective-permute-start | bytes 442376 | tf_op jit(solution)/shard_map/ppermute | solution.py:22
  27.2 22.6 %collective-permute-start.12 = (bf16[72,1024]{1,0:T(8,128)(2,1)}, bf16[72,1024]{1,0:T(8,128)(2,1)}, u32[]{:S(2)}, u32[]{:S(2)}) collective-permute-start(bf16[72,1024]{1,0:T(8,128)(2,1)} %copy-done.21), channel_id=1, source_target_pairs={{0,10},{2,8},{4,14},{6,12},{8,2},{10,0},{12,6},{14,4},{16,26},{18,... | collective-permute-start | bytes 442376 | tf_op jit(solution)/shard_map/ppermute | solution.py:22
  29.6 22.1 %collective-permute-start.13 = (bf16[72,1024]{1,0:T(8,128)(2,1)}, bf16[72,1024]{1,0:T(8,128)(2,1)}, u32[]{:S(2)}, u32[]{:S(2)}) collective-permute-start(bf16[72,1024]{1,0:T(8,128)(2,1)} %copy-done.20), channel_id=1, source_target_pairs={{0,12},{2,14},{4,8},{6,10},{8,4},{10,6},{12,0},{14,2},{16,28},{18,... | collective-permute-start | bytes 442376 | tf_op jit(solution)/shard_map/ppermute | solution.py:22
  36.1 27.1 %collective-permute-start.7 = (f32[128,1024]{1,0:T(8,128)}, f32[128,1024]{1,0:T(8,128)S(1)}, u32[]{:S(2)}, u32[]{:S(2)}) collective-permute-start(f32[128,1024]{1,0:T(8,128)} %copy-done.7), channel_id=1, source_target_pairs={{0,16},{2,18},{4,20},{6,22},{8,24},{10,26},{12,28},{14,30},{16,0},... | collective-permute-start | bytes 1572872 | tf_op jit(solution)/shard_map/ppermute | solution.py:22
  46.8 15.0 %collective-permute-start.14 = (bf16[72,1024]{1,0:T(8,128)(2,1)S(1)}, bf16[72,1024]{1,0:T(8,128)(2,1)S(1)}, u32[]{:S(2)}, u32[]{:S(2)}) collective-permute-start(bf16[72,1024]{1,0:T(8,128)(2,1)S(1)} %copy-done.19), channel_id=1, source_target_pairs={{0,14},{2,12},{4,10},{6,8},{8,6},{10,4},{12,2},{14,0},{16,30},{18,... | collective-permute-start | bytes 442376 | tf_op jit(solution)/shard_map/ppermute | solution.py:22
  48.4 13.4 %collective-permute-start.8 = (bf16[72,1024]{1,0:T(8,128)(2,1)S(1)}, bf16[72,1024]{1,0:T(8,128)(2,1)S(1)}, u32[]{:S(2)}, u32[]{:S(2)}) collective-permute-start(bf16[72,1024]{1,0:T(8,128)(2,1)S(1)} %copy-done.17), channel_id=1, source_target_pairs={{0,2},{2,0},{4,6},{6,4},{8,10},{10,8},{12,14},{14,12},{16,18},{18,... | collective-permute-start | bytes 442376 | tf_op jit(solution)/shard_map/ppermute | solution.py:22
  49.8 12.0 %collective-permute-start.9 = (bf16[72,1024]{1,0:T(8,128)(2,1)S(1)}, bf16[72,1024]{1,0:T(8,128)(2,1)S(1)}, u32[]{:S(2)}, u32[]{:S(2)}) collective-permute-start(bf16[72,1024]{1,0:T(8,128)(2,1)S(1)} %copy-done.15), channel_id=1, source_target_pairs={{0,4},{2,6},{4,0},{6,2},{8,12},{10,14},{12,8},{14,10},{16,20},{18,... | collective-permute-start | bytes 442376 | tf_op jit(solution)/shard_map/ppermute | solution.py:22
  51.8 11.5 %collective-permute-start.15 = (f32[8,128]{1,0:T(8,128)S(1)}, f32[8,128]{1,0:T(8,128)S(1)}, u32[]{:S(2)}, u32[]{:S(2)}) collective-permute-start(f32[8,128]{1,0:T(8,128)S(1)} %get-tuple-element.68), channel_id=1, source_target_pairs={{0,16},{2,18},{4,20},{6,22},{8,24},{10,26},{12,28},{14,30},{16,0},... | collective-permute-start | bytes 12296 | tf_op jit(solution)/shard_map/ppermute | solution.py:22
  64.6 11.8 %collective-permute-start.28 = (bf16[128,1024]{1,0:T(8,128)(2,1)S(1)}, bf16[128,1024]{1,0:T(8,128)(2,1)S(1)}, u32[]{:S(2)}, u32[]{:S(2)}) collective-permute-start(bf16[128,1024]{1,0:T(8,128)(2,1)S(1)} %renew.1.refs_0_), channel_id=1, source_target_pairs={{0,2},{2,0},{4,6},{6,4},{8,10},{10,8},{12,14},{14,12},{16,18},{18,... | collective-permute-start | bytes 786440 | tf_op jit(solution)/shard_map/ppermute | solution.py:22
  65.3 17.0 %collective-permute-start.16 = (bf16[128,1024]{1,0:T(8,128)(2,1)S(1)}, bf16[128,1024]{1,0:T(8,128)(2,1)S(1)}, u32[]{:S(2)}, u32[]{:S(2)}) collective-permute-start(bf16[128,1024]{1,0:T(8,128)(2,1)S(1)} %renew.1.refs_0_), channel_id=1, source_target_pairs={{0,16},{2,18},{4,20},{6,22},{8,24},{10,26},{12,28},{14,30},{16,0},... | collective-permute-start | bytes 786440 | tf_op jit(solution)/shard_map/ppermute | solution.py:22
  67.2 16.7 %collective-permute-start.19 = (bf16[128,1024]{1,0:T(8,128)(2,1)S(1)}, bf16[128,1024]{1,0:T(8,128)(2,1)S(1)}, u32[]{:S(2)}, u32[]{:S(2)}) collective-permute-start(bf16[128,1024]{1,0:T(8,128)(2,1)S(1)} %renew.1.refs_0_), channel_id=1, source_target_pairs={{0,24},{2,26},{4,28},{6,30},{8,16},{10,18},{12,20},{14,22},{16,8},... | collective-permute-start | bytes 786440 | tf_op jit(solution)/shard_map/ppermute | solution.py:22
  74.4 13.9 %collective-permute-start.30 = (bf16[128,1024]{1,0:T(8,128)(2,1)S(1)}, bf16[128,1024]{1,0:T(8,128)(2,1)S(1)}, u32[]{:S(2)}, u32[]{:S(2)}) collective-permute-start(bf16[128,1024]{1,0:T(8,128)(2,1)S(1)} %collective-permute-done.29.refs_2_), channel_id=1, source_target_pairs={{0,2},{2,0},{4,6},{6,4},{8,10},{10,8},{12,14},{14,12},{16,18},{18,... | collective-permute-start | bytes 786440 | tf_op jit(solution)/shard_map/ppermute | solution.py:22
  77.0 12.9 %collective-permute-start.26 = (bf16[128,1024]{1,0:T(8,128)(2,1)S(1)}, bf16[128,1024]{1,0:T(8,128)(2,1)S(1)}, u32[]{:S(2)}, u32[]{:S(2)}) collective-permute-start(bf16[128,1024]{1,0:T(8,128)(2,1)S(1)} %collective-permute-done.24.refs_0_), channel_id=1, source_target_pairs={{0,4},{2,6},{4,0},{6,2},{8,12},{10,14},{12,8},{14,10},{16,20},{18,... | collective-permute-start | bytes 786440 | tf_op jit(solution)/shard_map/ppermute | solution.py:22
  84.3 15.6 %collective-permute-start.27 = (bf16[128,1024]{1,0:T(8,128)(2,1)S(1)}, bf16[128,1024]{1,0:T(8,128)(2,1)}, u32[]{:S(2)}, u32[]{:S(2)}) collective-permute-start(bf16[128,1024]{1,0:T(8,128)(2,1)S(1)} %collective-permute-done.25.refs_1_), channel_id=1, source_target_pairs={{0,4},{2,6},{4,0},{6,2},{8,12},{10,14},{12,8},{14,10},{16,20},{18,... | collective-permute-start | bytes 786440 | tf_op jit(solution)/shard_map/ppermute | solution.py:22
  89.1 14.7 %collective-permute-start.22 = (bf16[128,1024]{1,0:T(8,128)(2,1)S(1)}, bf16[128,1024]{1,0:T(8,128)(2,1)}, u32[]{:S(2)}, u32[]{:S(2)}) collective-permute-start(bf16[128,1024]{1,0:T(8,128)(2,1)S(1)} %collective-permute-done.16.refs_0_), channel_id=1, source_target_pairs={{0,2},{2,0},{4,6},{6,4},{8,10},{10,8},{12,14},{14,12},{16,18},{18,... | collective-permute-start | bytes 786440 | tf_op jit(solution)/shard_map/ppermute | solution.py:22
  90.7 13.1 %collective-permute-start.23 = (bf16[128,1024]{1,0:T(8,128)(2,1)S(1)}, bf16[128,1024]{1,0:T(8,128)(2,1)}, u32[]{:S(2)}, u32[]{:S(2)}) collective-permute-start(bf16[128,1024]{1,0:T(8,128)(2,1)S(1)} %collective-permute-done.19.refs_3_), channel_id=1, source_target_pairs={{0,4},{2,6},{4,0},{6,2},{8,12},{10,14},{12,8},{14,10},{16,20},{18,... | collective-permute-start | bytes 786440 | tf_op jit(solution)/shard_map/ppermute | solution.py:22
  92.4 15.0 %collective-permute-start.18 = (bf16[128,1024]{1,0:T(8,128)(2,1)S(1)}, bf16[128,1024]{1,0:T(8,128)(2,1)S(1)}, u32[]{:S(2)}, u32[]{:S(2)}) collective-permute-start(bf16[128,1024]{1,0:T(8,128)(2,1)S(1)} %collective-permute-done.17.refs_2_), channel_id=1, source_target_pairs={{0,2},{2,0},{4,6},{6,4},{8,10},{10,8},{12,14},{14,12},{16,18},{18,... | collective-permute-start | bytes 786440 | tf_op jit(solution)/shard_map/ppermute | solution.py:22
  94.2 13.3 %collective-permute-start.21 = (bf16[128,1024]{1,0:T(8,128)(2,1)}, bf16[128,1024]{1,0:T(8,128)(2,1)S(1)}, u32[]{:S(2)}, u32[]{:S(2)}) collective-permute-start(bf16[128,1024]{1,0:T(8,128)(2,1)} %collective-permute-done.20.refs_4_), channel_id=1, source_target_pairs={{0,4},{2,6},{4,0},{6,2},{8,12},{10,14},{12,8},{14,10},{16,20},{18,... | collective-permute-start | bytes 786440 | tf_op jit(solution)/shard_map/ppermute | solution.py:22
  (33 other events, 119.9 us)

commit v2 on v1

--- a/solution.py
+++ b/solution.py
@@ -80,7 +80,7 @@
         in_specs=[VMEM],
         out_specs=[VMEM] * 4,
         compiler_params=params(),
-        cost_estimate=cost(4 * half * count * 128, 64 * count),
+        cost_estimate=cost(2e9, 64 * count),
         name="ranks",
     )(assign_row)
 
@@ -182,7 +182,7 @@
 
 def first_lowest(cents, columns):
     return pl.pallas_call(
-        functools.partial(first_kernel, 256),
+        functools.partial(first_kernel, 512),
         out_shape=jax.ShapeDtypeStruct((8, columns.shape[1]), F32),
         in_specs=[VMEM, VMEM],
         out_specs=VMEM,
@@ -253,7 +253,7 @@
     near = place(near_rank, near_label, points, capacity)
     near = [near[0]] + [swap(near[m], m) for m in range(1, half)]
     far_sums, far_counts = add_up(far, share, capacity)
-    far_sums, late = lax.optimization_barrier((far_sums, points))
+    near[1], late = lax.optimization_barrier((near[1], points))
     far_sums = swap(far_sums, half)
     far_counts = swap(far_counts, half)
     columns = jnp.transpose(late)
@@ -268,7 +268,8 @@
     sets, corners = [], []
     for k in range(columns_count):
         one = piece if k == 0 else swap(piece, 4 * k)
-        one_x, one_y = swap(one, 1), swap(one, 2)
+        one_y = swap(one, 2)
+        one_x = swap(one, 1)
         corner = swap(one_y, 1) if k % 2 == 0 else swap(one_x, 2)
         m = 4 * k
         sets.append([(m, 0, one), (m ^ 1, 0, one_x), (m ^ 2, 0, one_y)])

time: 111 us -> 104 us (0.937)
  waiting for transfers between devices: 20.6 us -> 10.7 us
  starting transfers between devices: 43.9 us -> 52.6 us
  local copies, waits for them, and re-layouts: 21.3 us -> 16.3 us
    ppermute x32, waiting for transfers between devices: 20.6 us -> 10.7 us  [swap(): return lax.ppermute(value, axis, [(i, i ^ mask) for i in range(size)])]
    ppermute x32, starting transfers between devices: 43.9 us -> 52.6 us  [swap(): return lax.ppermute(value, axis, [(i, i ^ mask) for i in range(size)])]
    unnamed x50 -> x36, local copies, waits for them, and re-layouts: 17.5 us -> 12.4 us
  transfers between devices with their start and end apart: 32 -> 32, of which waited for: 6 -> 6; matrix products, arithmetic and copies ran while one was open for 4% -> 4% of each run, Pallas kernels for 17% -> 18%
where the time goes in v2:
time: 104 us; the launch traced here: 103 us
  starting transfers between devices  52.6 us (51%)
  Pallas kernels  21.8 us (21%)
  local copies, waits for them, and re-layouts  16.3 us (16%)
  waiting for transfers between devices  10.7 us (10%)
  other arithmetic  1.13 us (1%)
    ppermute x32, starting transfers between devices, swap(): return lax.ppermute(value, axis, [(i, i ^ mask) for i in range(size)])  52.6 us
    unnamed x36, local copies, waits for them, and re-layouts  12.4 us
    ppermute x32, waiting for transfers between devices, swap(): return lax.ppermute(value, axis, [(i, i ^ mask) for i in range(size)])  10.7 us
    pallas_call x4, Pallas kernels, arrive(): pl.pallas_call(functools.partial(arrive_kernel, share, places, fresh), ou...  9.79 us
    pallas_call x1, Pallas kernels, first_lowest(): pl.pallas_call(functools.partial(first_kernel, 512), out_shape=jax.ShapeD...  5.1 us
    pallas_call x2, Pallas kernels, place(): pl.pallas_call(functools.partial(place_kernel, half, capacity), out_shape...  3.99 us
    optimization_barrier x1, local copies, waits for them, and re-layouts, halves(): near[1], late = lax.optimization_barrier((near[1], points))  2.85 us
    pallas_call x2, Pallas kernels, add_up(): pl.pallas_call(functools.partial(sum_kernel, share, capacity), out_shape=...  2.5 us
  transfers between devices with their start and end apart: 32, of which 6 were waited for; matrix products, arithmetic and copies ran while one was open for 4% of the time, Pallas kernels for 18%

profile of v2, /device:TPU:0, one launch (start us, length us, event | category | flops | bytes accessed | tf_op | source)
XLA Modules:
  0.0 103.4 jit_solution(14251127459545842228)
XLA Ops:
  2.2 1.6 %shard_map.51 = (bf16[72,1024]{1,0:T(8,128)(2,1)S(1)}, bf16[72,1024]{1,0:T(8,128)(2,1)S(1)}, bf16[72,1024]{1,0:T(8,128)(2,1)S(1)}, bf16[72,1024]{1,0:T(8,128)(2,...) custom-call(f32[8,1024]{1,0:T(8,128)S(1)} %get-tuple-element.44.rank, ...), custom_call_target="tpu_custom_call" | custom-call | flops 1073741824 | bytes 4194304 | tf_op jit(solution)/shard_map/pallas_call | solution.py:111
  3.9 3.0 %collective-permute-start.1 = (bf16[72,1024]{1,0:T(8,128)(2,1)S(1)}, bf16[72,1024]{1,0:T(8,128)(2,1)S(1)}, u32[]{:S(2)}, u32[]{:S(2)}) collective-permute-start(bf16[72,1024]{1,0:T(8,128)(2,1)S(1)} %get-tuple-element.47), channel_id=1, source_target_pairs={{0,2},{2,0},{4,6},{6,4},{8,10},{10,8},{12,14},{14,12},{16,18},{18,... | collective-permute-start | bytes 442376 | tf_op jit(solution)/shard_map/ppermute | solution.py:22
  8.4 2.0 %collective-permute-start.4 = (bf16[72,1024]{1,0:T(8,128)(2,1)S(1)}, bf16[72,1024]{1,0:T(8,128)(2,1)S(1)}, u32[]{:S(2)}, u32[]{:S(2)}) collective-permute-start(bf16[72,1024]{1,0:T(8,128)(2,1)S(1)} %get-tuple-element.50), channel_id=1, source_target_pairs={{0,8},{2,10},{4,12},{6,14},{8,0},{10,2},{12,4},{14,6},{16,24},{18,... | collective-permute-start | bytes 442376 | tf_op jit(solution)/shard_map/ppermute | solution.py:22
  11.8 2.5 %collective-permute-start.6 = (bf16[72,1024]{1,0:T(8,128)(2,1)S(1)}, bf16[72,1024]{1,0:T(8,128)(2,1)S(1)}, u32[]{:S(2)}, u32[]{:S(2)}) collective-permute-start(bf16[72,1024]{1,0:T(8,128)(2,1)S(1)} %get-tuple-element.52), channel_id=1, source_target_pairs={{0,12},{2,14},{4,8},{6,10},{8,4},{10,6},{12,0},{14,2},{16,28},{18,... | collective-permute-start | bytes 442376 | tf_op jit(solution)/shard_map/ppermute | solution.py:22
  14.3 1.6 %collective-permute-start.7 = (bf16[72,1024]{1,0:T(8,128)(2,1)S(1)}, bf16[72,1024]{1,0:T(8,128)(2,1)S(1)}, u32[]{:S(2)}, u32[]{:S(2)}) collective-permute-start(bf16[72,1024]{1,0:T(8,128)(2,1)S(1)} %get-tuple-element.53), channel_id=1, source_target_pairs={{0,14},{2,12},{4,10},{6,8},{8,6},{10,4},{12,2},{14,0},{16,30},{18,... | collective-permute-start | bytes 442376 | tf_op jit(solution)/shard_map/ppermute | solution.py:22
  15.9 2.4 %shard_map.50 = (bf16[72,1024]{1,0:T(8,128)(2,1)S(1)}, bf16[72,1024]{1,0:T(8,128)(2,1)S(1)}, bf16[72,1024]{1,0:T(8,128)(2,1)S(1)}, bf16[72,1024]{1,0:T(8,128)(2,...) custom-call(f32[8,1024]{1,0:T(8,128)S(1)} %get-tuple-element.40.rank, ...), custom_call_target="tpu_custom_call" | custom-call | flops 1073741824 | bytes 4194304 | tf_op jit(solution)/shard_map/pallas_call | solution.py:111
  19.0 4.0 %collective-permute-start = (bf16[72,1024]{1,0:T(8,128)(2,1)S(1)}, bf16[72,1024]{1,0:T(8,128)(2,1)S(1)}, u32[]{:S(2)}, u32[]{:S(2)}) collective-permute-start(bf16[72,1024]{1,0:T(8,128)(2,1)S(1)} %get-tuple-element.42), channel_id=1, source_target_pairs={{0,2},{2,0},{4,6},{6,4},{8,10},{10,8},{12,14},{14,12},{16,18},{18,... | collective-permute-start | bytes 442376 | tf_op jit(solution)/shard_map/ppermute | solution.py:22
  25.7 2.7 %collective-permute-start.13 = (bf16[72,1024]{1,0:T(8,128)(2,1)}, bf16[72,1024]{1,0:T(8,128)(2,1)}, u32[]{:S(2)}, u32[]{:S(2)}) collective-permute-start(bf16[72,1024]{1,0:T(8,128)(2,1)} %get-tuple-element.63), channel_id=1, source_target_pairs={{0,12},{2,14},{4,8},{6,10},{8,4},{10,6},{12,0},{14,2},{16,28},{18,... | collective-permute-start | bytes 442376 | tf_op jit(solution)/shard_map/ppermute | solution.py:22
  29.6 2.6 %collective-permute-start.8 = (f32[128,1024]{1,0:T(8,128)}, f32[128,1024]{1,0:T(8,128)S(1)}, u32[]{:S(2)}, u32[]{:S(2)}) collective-permute-start(f32[128,1024]{1,0:T(8,128)} %get-tuple-element.54), channel_id=1, source_target_pairs={{0,16},{2,18},{4,20},{6,22},{8,24},{10,26},{12,28},{14,30},{16,0},... | collective-permute-start | bytes 1572872 | tf_op jit(solution)/shard_map/ppermute | solution.py:22
  32.2 2.9 %copy.8 = bf16[1024,1024]{0,1:T(8,128)(2,1)S(1)} copy(bf16[1024,1024]{1,0:T(8,128)(2,1)} %points_ref.3) | data formatting | bytes 4194304 | tf_op jit(solution)/shard_map/optimization_barrier | solution.py:256
  35.1 2.2 %copy-done.6 = bf16[2048,1024]{1,0:T(8,128)(2,1)S(1)} copy-done((bf16[2048,1024]{1,0:T(8,128)(2,1)S(1)}, bf16[2048,1024]{1,0:T(8,128)(2,1)}, u32[]{:S(2)}) %copy-start.6) | copy-done | bytes 4194328
  37.3 5.1 %first_lowest.1 = f32[8,1024]{1,0:T(8,128)S(1)} custom-call(bf16[2048,1024]{1,0:T(8,128)(2,1)S(1)} %copy-done.6, bf16[1024,1024]{1,0:T(8,128)(2,1)S(1)} %bitcast.4), custom_call_target="tpu_custom_call" | custom-call | flops 4294967296 | bytes 4194304 | tf_op jit(solution)/shard_map/first_lowest/pallas_call | solution.py:184
  46.3 3.2 %collective-permute-done.14.refs_7_ = bf16[72,1024]{1,0:T(8,128)(2,1)S(1)} collective-permute-done((bf16[72,1024]{1,0:T(8,128)(2,1)S(1)}, bf16[72,1024]{1,0:T(8,128)(2,1)S(1)}, u32[]{:S(2)}, u32[]{:S(2)}) %collective-permute-start.14) | collective-permute-done | bytes 147488 | tf_op jit(solution)/shard_map/ppermute | solution.py:22
  53.4 3.8 %collective-permute-start.29 = (bf16[128,1024]{1,0:T(8,128)(2,1)S(1)}, bf16[128,1024]{1,0:T(8,128)(2,1)S(1)}, u32[]{:S(2)}, u32[]{:S(2)}) collective-permute-start(bf16[128,1024]{1,0:T(8,128)(2,1)S(1)} %renew.1.refs_0_), channel_id=1, source_target_pairs={{0,4},{2,6},{4,0},{6,2},{8,12},{10,14},{12,8},{14,10},{16,20},{18,... | collective-permute-start | bytes 786440 | tf_op jit(solution)/shard_map/ppermute | solution.py:22
  57.1 2.9 %collective-permute-start.16 = (bf16[128,1024]{1,0:T(8,128)(2,1)S(1)}, bf16[128,1024]{1,0:T(8,128)(2,1)S(1)}, u32[]{:S(2)}, u32[]{:S(2)}) collective-permute-start(bf16[128,1024]{1,0:T(8,128)(2,1)S(1)} %renew.1.refs_0_), channel_id=1, source_target_pairs={{0,16},{2,18},{4,20},{6,22},{8,24},{10,26},{12,28},{14,30},{16,0},... | collective-permute-start | bytes 786440 | tf_op jit(solution)/shard_map/ppermute | solution.py:22
  62.2 3.5 %collective-permute-start.25 = (bf16[128,1024]{1,0:T(8,128)(2,1)S(1)}, bf16[128,1024]{1,0:T(8,128)(2,1)S(1)}, u32[]{:S(2)}, u32[]{:S(2)}) collective-permute-start(bf16[128,1024]{1,0:T(8,128)(2,1)S(1)} %collective-permute-done.24.refs_0_), channel_id=1, source_target_pairs={{0,2},{2,0},{4,6},{6,4},{8,10},{10,8},{12,14},{14,12},{16,18},{18,... | collective-permute-start | bytes 786440 | tf_op jit(solution)/shard_map/ppermute | solution.py:22
  67.1 5.0 %collective-permute-start.26 = (bf16[128,1024]{1,0:T(8,128)(2,1)S(1)}, bf16[128,1024]{1,0:T(8,128)(2,1)S(1)}, u32[]{:S(2)}, u32[]{:S(2)}) collective-permute-start(bf16[128,1024]{1,0:T(8,128)(2,1)S(1)} %collective-permute-done.24.refs_0_), channel_id=1, source_target_pairs={{0,4},{2,6},{4,0},{6,2},{8,12},{10,14},{12,8},{14,10},{16,20},{18,... | collective-permute-start | bytes 786440 | tf_op jit(solution)/shard_map/ppermute | solution.py:22
  72.1 2.5 %collective-permute-done.16.refs_0_ = bf16[128,1024]{1,0:T(8,128)(2,1)S(1)} collective-permute-done((bf16[128,1024]{1,0:T(8,128)(2,1)S(1)}, bf16[128,1024]{1,0:T(8,128)(2,1)S(1)}, u32[]{:S(2)}, u32[]{:S(2)}) %collective-permute-start.16) | collective-permute-done | bytes 262176 | tf_op jit(solution)/shard_map/ppermute | solution.py:22
  80.1 1.9 %collective-permute-start.23 = (bf16[128,1024]{1,0:T(8,128)(2,1)S(1)}, bf16[128,1024]{1,0:T(8,128)(2,1)}, u32[]{:S(2)}, u32[]{:S(2)}) collective-permute-start(bf16[128,1024]{1,0:T(8,128)(2,1)S(1)} %collective-permute-done.19.refs_3_), channel_id=1, source_target_pairs={{0,4},{2,6},{4,0},{6,2},{8,12},{10,14},{12,8},{14,10},{16,20},{18,... | collective-permute-start | bytes 786440 | tf_op jit(solution)/shard_map/ppermute | solution.py:22
  82.0 2.4 %collective-permute-done.17.refs_2_ = bf16[128,1024]{1,0:T(8,128)(2,1)S(1)} collective-permute-done((bf16[128,1024]{1,0:T(8,128)(2,1)S(1)}, bf16[128,1024]{1,0:T(8,128)(2,1)S(1)}, u32[]{:S(2)}, u32[]{:S(2)}) %collective-permute-start.17) | collective-permute-done | bytes 262176 | tf_op jit(solution)/shard_map/ppermute | solution.py:22
  85.1 1.8 %collective-permute-start.21 = (bf16[128,1024]{1,0:T(8,128)(2,1)}, bf16[128,1024]{1,0:T(8,128)(2,1)S(1)}, u32[]{:S(2)}, u32[]{:S(2)}) collective-permute-start(bf16[128,1024]{1,0:T(8,128)(2,1)} %collective-permute-done.20.refs_4_), channel_id=1, source_target_pairs={{0,4},{2,6},{4,0},{6,2},{8,12},{10,14},{12,8},{14,10},{16,20},{18,... | collective-permute-start | bytes 786440 | tf_op jit(solution)/shard_map/ppermute | solution.py:22
  90.7 1.9 %shard_map.54 = (f32[8,1024]{1,0:T(8,128)S(1)}, bf16[2048,1024]{1,0:T(8,128)(2,1)}) custom-call(bf16[128,1024]{1,0:T(8,128)(2,1)S(1)} %copy-done.5, bf16[128,1024]{1,0:T(8,128)(2,1)S(1)} %copy-done.10, bf16[128,1024]{1,0:T(8,128)(2,1)S(1)} %copy-done.8, bf16[128,1024]{1,0:T(8,128)(2,1)S(1)} %copy-done.12, bf16[1024,1024]{1,0:T(8,128)(2,1)S(1)} %bitcast.5), custom_call_target="tpu_custom_call" | custom-call | flops 1073741824 | bytes 2097152 | tf_op jit(solution)/shard_map/pallas_call | solution.py:227
  93.6 2.9 %shard_map.55 = (f32[8,1024]{1,0:T(8,128)S(1)}, bf16[2048,1024]{1,0:T(8,128)(2,1)}) custom-call(bf16[128,1024]{1,0:T(8,128)(2,1)S(1)} %collective-permute-done.24.refs_0_, bf16[128,1024]{1,0:T(8,128)(2,1)S(1)} %collective-permute-done.25.refs_1_, bf16[128,1024]{1,0:T(8,128)(2,1)S(1)} %copy-done.3, ...), custom_call_target="tpu_custom_call", output_to_operand_aliasing={{1}: (6, {})} | custom-call | flops 1073741824 | bytes 2097152 | tf_op jit(solution)/shard_map/pallas_call | solution.py:227
  96.5 3.7 %shard_map.56 = (f32[8,1024]{1,0:T(8,128)S(1)}, bf16[2048,1024]{1,0:T(8,128)(2,1)}) custom-call(bf16[128,1024]{1,0:T(8,128)(2,1)S(1)} %collective-permute-done.16.refs_0_, bf16[128,1024]{1,0:T(8,128)(2,1)} %collective-permute-done.22.refs_1_, bf16[128,1024]{1,0:T(8,128)(2,1)S(1)} %collective-permute-done.17.refs_2_, ...), custom_call_target="tpu_custom_call", output_to_operand_aliasing={{1}: (8, {})} | custom-call | flops 1610612736 | bytes 3145728 | tf_op jit(solution)/shard_map/pallas_call | solution.py:227
  (94 shorter events, 34.5 us)
Async XLA Ops:
  8.4 10.6 %collective-permute-start.3 = (bf16[72,1024]{1,0:T(8,128)(2,1)S(1)}, bf16[72,1024]{1,0:T(8,128)(2,1)S(1)}, u32[]{:S(2)}, u32[]{:S(2)}) collective-permute-start(bf16[72,1024]{1,0:T(8,128)(2,1)S(1)} %get-tuple-element.49), channel_id=1, source_target_pairs={{0,6},{2,4},{4,2},{6,0},{8,14},{10,12},{12,10},{14,8},{16,22},{18,... | collective-permute-start | bytes 442376 | tf_op jit(solution)/shard_map/ppermute | solution.py:22
  8.4 15.6 %collective-permute-start.4 = (bf16[72,1024]{1,0:T(8,128)(2,1)S(1)}, bf16[72,1024]{1,0:T(8,128)(2,1)S(1)}, u32[]{:S(2)}, u32[]{:S(2)}) collective-permute-start(bf16[72,1024]{1,0:T(8,128)(2,1)S(1)} %get-tuple-element.50), channel_id=1, source_target_pairs={{0,8},{2,10},{4,12},{6,14},{8,0},{10,2},{12,4},{14,6},{16,24},{18,... | collective-permute-start | bytes 442376 | tf_op jit(solution)/shard_map/ppermute | solution.py:22
  10.4 13.6 %collective-permute-start.5 = (bf16[72,1024]{1,0:T(8,128)(2,1)S(1)}, bf16[72,1024]{1,0:T(8,128)(2,1)S(1)}, u32[]{:S(2)}, u32[]{:S(2)}) collective-permute-start(bf16[72,1024]{1,0:T(8,128)(2,1)S(1)} %get-tuple-element.51), channel_id=1, source_target_pairs={{0,10},{2,8},{4,14},{6,12},{8,2},{10,0},{12,6},{14,4},{16,26},{18,... | collective-permute-start | bytes 442376 | tf_op jit(solution)/shard_map/ppermute | solution.py:22
  11.8 12.8 %collective-permute-start.6 = (bf16[72,1024]{1,0:T(8,128)(2,1)S(1)}, bf16[72,1024]{1,0:T(8,128)(2,1)S(1)}, u32[]{:S(2)}, u32[]{:S(2)}) collective-permute-start(bf16[72,1024]{1,0:T(8,128)(2,1)S(1)} %get-tuple-element.52), channel_id=1, source_target_pairs={{0,12},{2,14},{4,8},{6,10},{8,4},{10,6},{12,0},{14,2},{16,28},{18,... | collective-permute-start | bytes 442376 | tf_op jit(solution)/shard_map/ppermute | solution.py:22
  14.3 11.4 %collective-permute-start.7 = (bf16[72,1024]{1,0:T(8,128)(2,1)S(1)}, bf16[72,1024]{1,0:T(8,128)(2,1)S(1)}, u32[]{:S(2)}, u32[]{:S(2)}) collective-permute-start(bf16[72,1024]{1,0:T(8,128)(2,1)S(1)} %get-tuple-element.53), channel_id=1, source_target_pairs={{0,14},{2,12},{4,10},{6,8},{8,6},{10,4},{12,2},{14,0},{16,30},{18,... | collective-permute-start | bytes 442376 | tf_op jit(solution)/shard_map/ppermute | solution.py:22
  19.0 10.6 %collective-permute-start = (bf16[72,1024]{1,0:T(8,128)(2,1)S(1)}, bf16[72,1024]{1,0:T(8,128)(2,1)S(1)}, u32[]{:S(2)}, u32[]{:S(2)}) collective-permute-start(bf16[72,1024]{1,0:T(8,128)(2,1)S(1)} %get-tuple-element.42), channel_id=1, source_target_pairs={{0,2},{2,0},{4,6},{6,4},{8,10},{10,8},{12,14},{14,12},{16,18},{18,... | collective-permute-start | bytes 442376 | tf_op jit(solution)/shard_map/ppermute | solution.py:22
  23.9 18.4 %collective-permute-start.10 = (bf16[72,1024]{1,0:T(8,128)(2,1)}, bf16[72,1024]{1,0:T(8,128)(2,1)S(1)}, u32[]{:S(2)}, u32[]{:S(2)}) collective-permute-start(bf16[72,1024]{1,0:T(8,128)(2,1)} %get-tuple-element.60), channel_id=1, source_target_pairs={{0,6},{2,4},{4,2},{6,0},{8,14},{10,12},{12,10},{14,8},{16,22},{18,... | collective-permute-start | bytes 442376 | tf_op jit(solution)/shard_map/ppermute | solution.py:22
  24.0 19.9 %collective-permute-start.11 = (bf16[72,1024]{1,0:T(8,128)(2,1)}, bf16[72,1024]{1,0:T(8,128)(2,1)S(1)}, u32[]{:S(2)}, u32[]{:S(2)}) collective-permute-start(bf16[72,1024]{1,0:T(8,128)(2,1)} %get-tuple-element.61), channel_id=1, source_target_pairs={{0,8},{2,10},{4,12},{6,14},{8,0},{10,2},{12,4},{14,6},{16,24},{18,... | collective-permute-start | bytes 442376 | tf_op jit(solution)/shard_map/ppermute | solution.py:22
  24.6 21.3 %collective-permute-start.12 = (bf16[72,1024]{1,0:T(8,128)(2,1)}, bf16[72,1024]{1,0:T(8,128)(2,1)}, u32[]{:S(2)}, u32[]{:S(2)}) collective-permute-start(bf16[72,1024]{1,0:T(8,128)(2,1)} %get-tuple-element.62), channel_id=1, source_target_pairs={{0,10},{2,8},{4,14},{6,12},{8,2},{10,0},{12,6},{14,4},{16,26},{18,... | collective-permute-start | bytes 442376 | tf_op jit(solution)/shard_map/ppermute | solution.py:22
  25.7 20.6 %collective-permute-start.13 = (bf16[72,1024]{1,0:T(8,128)(2,1)}, bf16[72,1024]{1,0:T(8,128)(2,1)}, u32[]{:S(2)}, u32[]{:S(2)}) collective-permute-start(bf16[72,1024]{1,0:T(8,128)(2,1)} %get-tuple-element.63), channel_id=1, source_target_pairs={{0,12},{2,14},{4,8},{6,10},{8,4},{10,6},{12,0},{14,2},{16,28},{18,... | collective-permute-start | bytes 442376 | tf_op jit(solution)/shard_map/ppermute | solution.py:22
  29.6 22.5 %collective-permute-start.8 = (f32[128,1024]{1,0:T(8,128)}, f32[128,1024]{1,0:T(8,128)S(1)}, u32[]{:S(2)}, u32[]{:S(2)}) collective-permute-start(f32[128,1024]{1,0:T(8,128)} %get-tuple-element.54), channel_id=1, source_target_pairs={{0,16},{2,18},{4,20},{6,22},{8,24},{10,26},{12,28},{14,30},{16,0},... | collective-permute-start | bytes 1572872 | tf_op jit(solution)/shard_map/ppermute | solution.py:22
  52.4 9.8 %collective-permute-start.24 = (bf16[128,1024]{1,0:T(8,128)(2,1)S(1)}, bf16[128,1024]{1,0:T(8,128)(2,1)S(1)}, u32[]{:S(2)}, u32[]{:S(2)}) collective-permute-start(bf16[128,1024]{1,0:T(8,128)(2,1)S(1)} %renew.1.refs_0_), channel_id=1, source_target_pairs={{0,8},{2,10},{4,12},{6,14},{8,0},{10,2},{12,4},{14,6},{16,24},{18,... | collective-permute-start | bytes 786440 | tf_op jit(solution)/shard_map/ppermute | solution.py:22
  53.4 12.3 %collective-permute-start.29 = (bf16[128,1024]{1,0:T(8,128)(2,1)S(1)}, bf16[128,1024]{1,0:T(8,128)(2,1)S(1)}, u32[]{:S(2)}, u32[]{:S(2)}) collective-permute-start(bf16[128,1024]{1,0:T(8,128)(2,1)S(1)} %renew.1.refs_0_), channel_id=1, source_target_pairs={{0,4},{2,6},{4,0},{6,2},{8,12},{10,14},{12,8},{14,10},{16,20},{18,... | collective-permute-start | bytes 786440 | tf_op jit(solution)/shard_map/ppermute | solution.py:22
  57.1 17.5 %collective-permute-start.16 = (bf16[128,1024]{1,0:T(8,128)(2,1)S(1)}, bf16[128,1024]{1,0:T(8,128)(2,1)S(1)}, u32[]{:S(2)}, u32[]{:S(2)}) collective-permute-start(bf16[128,1024]{1,0:T(8,128)(2,1)S(1)} %renew.1.refs_0_), channel_id=1, source_target_pairs={{0,16},{2,18},{4,20},{6,22},{8,24},{10,26},{12,28},{14,30},{16,0},... | collective-permute-start | bytes 786440 | tf_op jit(solution)/shard_map/ppermute | solution.py:22
  60.0 15.2 %collective-permute-start.19 = (bf16[128,1024]{1,0:T(8,128)(2,1)S(1)}, bf16[128,1024]{1,0:T(8,128)(2,1)S(1)}, u32[]{:S(2)}, u32[]{:S(2)}) collective-permute-start(bf16[128,1024]{1,0:T(8,128)(2,1)S(1)} %renew.1.refs_0_), channel_id=1, source_target_pairs={{0,24},{2,26},{4,28},{6,30},{8,16},{10,18},{12,20},{14,22},{16,8},... | collective-permute-start | bytes 786440 | tf_op jit(solution)/shard_map/ppermute | solution.py:22
  62.2 14.7 %collective-permute-start.25 = (bf16[128,1024]{1,0:T(8,128)(2,1)S(1)}, bf16[128,1024]{1,0:T(8,128)(2,1)S(1)}, u32[]{:S(2)}, u32[]{:S(2)}) collective-permute-start(bf16[128,1024]{1,0:T(8,128)(2,1)S(1)} %collective-permute-done.24.refs_0_), channel_id=1, source_target_pairs={{0,2},{2,0},{4,6},{6,4},{8,10},{10,8},{12,14},{14,12},{16,18},{18,... | collective-permute-start | bytes 786440 | tf_op jit(solution)/shard_map/ppermute | solution.py:22
  65.6 12.3 %collective-permute-start.30 = (bf16[128,1024]{1,0:T(8,128)(2,1)S(1)}, bf16[128,1024]{1,0:T(8,128)(2,1)S(1)}, u32[]{:S(2)}, u32[]{:S(2)}) collective-permute-start(bf16[128,1024]{1,0:T(8,128)(2,1)S(1)} %collective-permute-done.29.refs_2_), channel_id=1, source_target_pairs={{0,2},{2,0},{4,6},{6,4},{8,10},{10,8},{12,14},{14,12},{16,18},{18,... | collective-permute-start | bytes 786440 | tf_op jit(solution)/shard_map/ppermute | solution.py:22
  67.1 12.3 %collective-permute-start.26 = (bf16[128,1024]{1,0:T(8,128)(2,1)S(1)}, bf16[128,1024]{1,0:T(8,128)(2,1)S(1)}, u32[]{:S(2)}, u32[]{:S(2)}) collective-permute-start(bf16[128,1024]{1,0:T(8,128)(2,1)S(1)} %collective-permute-done.24.refs_0_), channel_id=1, source_target_pairs={{0,4},{2,6},{4,0},{6,2},{8,12},{10,14},{12,8},{14,10},{16,20},{18,... | collective-permute-start | bytes 786440 | tf_op jit(solution)/shard_map/ppermute | solution.py:22
  75.3 9.8 %collective-permute-start.20 = (bf16[128,1024]{1,0:T(8,128)(2,1)S(1)}, bf16[128,1024]{1,0:T(8,128)(2,1)}, u32[]{:S(2)}, u32[]{:S(2)}) collective-permute-start(bf16[128,1024]{1,0:T(8,128)(2,1)S(1)} %collective-permute-done.19.refs_3_), channel_id=1, source_target_pairs={{0,2},{2,0},{4,6},{6,4},{8,10},{10,8},{12,14},{14,12},{16,18},{18,... | collective-permute-start | bytes 786440 | tf_op jit(solution)/shard_map/ppermute | solution.py:22
  76.9 15.8 %collective-permute-start.27 = (bf16[128,1024]{1,0:T(8,128)(2,1)S(1)}, bf16[128,1024]{1,0:T(8,128)(2,1)}, u32[]{:S(2)}, u32[]{:S(2)}) collective-permute-start(bf16[128,1024]{1,0:T(8,128)(2,1)S(1)} %collective-permute-done.25.refs_1_), channel_id=1, source_target_pairs={{0,4},{2,6},{4,0},{6,2},{8,12},{10,14},{12,8},{14,10},{16,20},{18,... | collective-permute-start | bytes 786440 | tf_op jit(solution)/shard_map/ppermute | solution.py:22
  78.7 17.8 %collective-permute-start.22 = (bf16[128,1024]{1,0:T(8,128)(2,1)S(1)}, bf16[128,1024]{1,0:T(8,128)(2,1)}, u32[]{:S(2)}, u32[]{:S(2)}) collective-permute-start(bf16[128,1024]{1,0:T(8,128)(2,1)S(1)} %collective-permute-done.16.refs_0_), channel_id=1, source_target_pairs={{0,2},{2,0},{4,6},{6,4},{8,10},{10,8},{12,14},{14,12},{16,18},{18,... | collective-permute-start | bytes 786440 | tf_op jit(solution)/shard_map/ppermute | solution.py:22
  80.1 16.4 %collective-permute-start.23 = (bf16[128,1024]{1,0:T(8,128)(2,1)S(1)}, bf16[128,1024]{1,0:T(8,128)(2,1)}, u32[]{:S(2)}, u32[]{:S(2)}) collective-permute-start(bf16[128,1024]{1,0:T(8,128)(2,1)S(1)} %collective-permute-done.19.refs_3_), channel_id=1, source_target_pairs={{0,4},{2,6},{4,0},{6,2},{8,12},{10,14},{12,8},{14,10},{16,20},{18,... | collective-permute-start | bytes 786440 | tf_op jit(solution)/shard_map/ppermute | solution.py:22
  84.4 15.8 %collective-permute-start.18 = (bf16[128,1024]{1,0:T(8,128)(2,1)S(1)}, bf16[128,1024]{1,0:T(8,128)(2,1)S(1)}, u32[]{:S(2)}, u32[]{:S(2)}) collective-permute-start(bf16[128,1024]{1,0:T(8,128)(2,1)S(1)} %collective-permute-done.17.refs_2_), channel_id=1, source_target_pairs={{0,2},{2,0},{4,6},{6,4},{8,10},{10,8},{12,14},{14,12},{16,18},{18,... | collective-permute-start | bytes 786440 | tf_op jit(solution)/shard_map/ppermute | solution.py:22
  85.1 15.1 %collective-permute-start.21 = (bf16[128,1024]{1,0:T(8,128)(2,1)}, bf16[128,1024]{1,0:T(8,128)(2,1)S(1)}, u32[]{:S(2)}, u32[]{:S(2)}) collective-permute-start(bf16[128,1024]{1,0:T(8,128)(2,1)} %collective-permute-done.20.refs_4_), channel_id=1, source_target_pairs={{0,4},{2,6},{4,0},{6,2},{8,12},{10,14},{12,8},{14,10},{16,20},{18,... | collective-permute-start | bytes 786440 | tf_op jit(solution)/shard_map/ppermute | solution.py:22
  (26 other events, 96.1 us)

commit v3 on v2

--- a/solution.py
+++ b/solution.py
@@ -212,11 +212,68 @@
         copy.wait()
 
 
-def arrive(pieces, columns, running, whole, total, share):
+def low_kernel(*refs):
+    pieces, (columns_ref, running_ref, out_ref) = refs[:-3], refs[-3:]
+    found = lowest(jnp.concatenate([r[...] for r in pieces], axis=0), columns_ref[...])
+    out_ref[...] = jnp.minimum(running_ref[...], found)
+
+
+def write_kernel(share, places, *refs):
+    count = len(places)
+    pieces, (whole_out, held, in_sems, out_sems) = refs[:count], refs[count + 1 :]
+    me = lax.axis_index("rows")
+    moves, at = [], 0
+    for i, ((mask, row), ref) in enumerate(zip(places, pieces, strict=True)):
+        rows = ref.shape[0]
+        slot = held.at[pl.ds(at, rows)]
+        start = pl.multiple_of((me ^ mask) * share + row, rows)
+        inward = pltpu.make_async_copy(ref, slot, in_sems.at[i])
+        outward = pltpu.make_async_copy(slot, whole_out.at[pl.ds(start, rows)], out_sems.at[i])
+        inward.start()
+        moves.append((inward, outward))
+        at += rows
+    for inward, outward in moves:
+        inward.wait()
+        outward.start()
+    for _, outward in moves:
+        outward.wait()
+
+
+def write(pieces, whole, share):
+    places = [(mask, row) for mask, row, _ in pieces]
+    operands = [array for _, _, array in pieces]
+    rows, width = sum(o.shape[0] for o in operands), operands[0].shape[1]
+    return pl.pallas_call(
+        functools.partial(write_kernel, share, places),
+        out_shape=jax.ShapeDtypeStruct(whole.shape, whole.dtype),
+        in_specs=[ANY] * (len(operands) + 1),
+        out_specs=ANY,
+        scratch_shapes=[
+            pltpu.VMEM((rows, width), BF16),
+            pltpu.SemaphoreType.DMA((len(places),)),
+            pltpu.SemaphoreType.DMA((len(places),)),
+        ],
+        input_output_aliases={len(operands): 0},
+        compiler_params=params(),
+        cost_estimate=cost(rows * width, 4 * rows * width),
+        name="write_last",
+    )(*operands, whole)
+
+
+def arrive(pieces, columns, running, whole, total, share, writes=True):
     places = [(mask, row) for mask, row, _ in pieces]
     operands = [array for _, _, array in pieces]
     rows, width = sum(o.shape[0] for o in operands), operands[0].shape[1]
     fresh = running is None
+    if not writes:
+        return pl.pallas_call(
+            low_kernel,
+            out_shape=jax.ShapeDtypeStruct((8, columns.shape[1]), F32),
+            in_specs=[VMEM] * (len(operands) + 2),
+            out_specs=VMEM,
+            compiler_params=params(),
+            cost_estimate=cost(2 * rows * width * columns.shape[1], 2 * rows * width),
+        )(*operands, columns, running), whole
     operands += [columns]
     specs = [VMEM] * len(operands)
     aliases = {}
@@ -275,10 +332,17 @@
         sets.append([(m, 0, one), (m ^ 1, 0, one_x), (m ^ 2, 0, one_y)])
         corners.append((m ^ 3, 0, corner))
     for name, group in groups_of(columns_count):
-        members = [p for k in group for p in sets[k]] if name != "last" else []
-        if name != "sides":
+        members = [p for k in group for p in sets[k]] if name == "set" else []
+        if name == "set":
             members += [corners[k] for k in group]
-        running, whole = arrive(members, columns, running, whole, total, share)
+            if group[0] == columns_count - 3:
+                members += [sets[k][0] for k in range(columns_count - 2, columns_count)]
+        elif name == "sides":
+            members = [p for k in group for p in sets[k][1:]]
+        else:
+            members = [corners[k] for k in group]
+        running, whole = arrive(members, columns, running, whole, total, share, name != "last")
+    whole = write([corners[k] for k in group], whole, share)
     both = jnp.stack([jnp.min(first, axis=0), jnp.min(running, axis=0)])
     nearest = block_min((pnorm[None, :] + both) / points.shape[1])
     return nearest, whole

time: 104 us -> 104 us (level)
    pallas_call x0 -> x2, Pallas kernels: none -> 1.6 us  [the longest x1 0.88 us: write(): pl.pallas_call(functools.partial(write_kernel, share, places), out_shape=...]
    pallas_call x4 -> x3, Pallas kernels: 9.79 us -> 8.63 us  [arrive(): pl.pallas_call(functools.partial(arrive_kernel, share, places, fresh), ou...]
  transfers between devices with their start and end apart: 32 -> 32, of which waited for: 6 -> 6; matrix products, arithmetic and copies ran while one was open for 4% -> 4% of each run, Pallas kernels for 18% -> 19%
where the time goes in v3:
time: 104 us; the launch traced here: 103 us
  starting transfers between devices  52.8 us (51%)
  Pallas kernels  22.2 us (21%)
  local copies, waits for them, and re-layouts  16.3 us (16%)
  waiting for transfers between devices  9.83 us (9%)
  other arithmetic  1.13 us (1%)
    ppermute x32, starting transfers between devices, swap(): return lax.ppermute(value, axis, [(i, i ^ mask) for i in range(size)])  52.8 us
    unnamed x36, local copies, waits for them, and re-layouts  12.5 us
    ppermute x32, waiting for transfers between devices, swap(): return lax.ppermute(value, axis, [(i, i ^ mask) for i in range(size)])  9.83 us
    pallas_call x3, Pallas kernels, arrive(): pl.pallas_call(functools.partial(arrive_kernel, share, places, fresh), ou...  8.63 us
    pallas_call x1, Pallas kernels, first_lowest(): pl.pallas_call(functools.partial(first_kernel, 512), out_shape=jax.ShapeD...  5.1 us
    pallas_call x2, Pallas kernels, place(): pl.pallas_call(functools.partial(place_kernel, half, capacity), out_shape...  3.97 us
    optimization_barrier x1, local copies, waits for them, and re-layouts, halves(): near[1], late = lax.optimization_barrier((near[1], points))  2.85 us
    pallas_call x2, Pallas kernels, add_up(): pl.pallas_call(functools.partial(sum_kernel, share, capacity), out_shape=...  2.5 us
  transfers between devices with their start and end apart: 32, of which 6 were waited for; matrix products, arithmetic and copies ran while one was open for 4% of the time, Pallas kernels for 19%

profile of v3, /device:TPU:0, one launch (start us, length us, event | category | flops | bytes accessed | tf_op | source)
XLA Modules:
  0.0 103.2 jit_solution(13199735318187036965)
XLA Ops:
  2.2 1.6 %shard_map.51 = (bf16[72,1024]{1,0:T(8,128)(2,1)S(1)}, bf16[72,1024]{1,0:T(8,128)(2,1)S(1)}, bf16[72,1024]{1,0:T(8,128)(2,1)S(1)}, bf16[72,1024]{1,0:T(8,128)(2,...) custom-call(f32[8,1024]{1,0:T(8,128)S(1)} %get-tuple-element.42.rank, ...), custom_call_target="tpu_custom_call" | custom-call | flops 1073741824 | bytes 4194304 | tf_op jit(solution)/shard_map/pallas_call | solution.py:111
  3.9 3.0 %collective-permute-start.1 = (bf16[72,1024]{1,0:T(8,128)(2,1)S(1)}, bf16[72,1024]{1,0:T(8,128)(2,1)S(1)}, u32[]{:S(2)}, u32[]{:S(2)}) collective-permute-start(bf16[72,1024]{1,0:T(8,128)(2,1)S(1)} %get-tuple-element.45), channel_id=1, source_target_pairs={{0,2},{2,0},{4,6},{6,4},{8,10},{10,8},{12,14},{14,12},{16,18},{18,... | collective-permute-start | bytes 442376 | tf_op jit(solution)/shard_map/ppermute | solution.py:22
  8.4 2.0 %collective-permute-start.4 = (bf16[72,1024]{1,0:T(8,128)(2,1)S(1)}, bf16[72,1024]{1,0:T(8,128)(2,1)S(1)}, u32[]{:S(2)}, u32[]{:S(2)}) collective-permute-start(bf16[72,1024]{1,0:T(8,128)(2,1)S(1)} %get-tuple-element.48), channel_id=1, source_target_pairs={{0,8},{2,10},{4,12},{6,14},{8,0},{10,2},{12,4},{14,6},{16,24},{18,... | collective-permute-start | bytes 442376 | tf_op jit(solution)/shard_map/ppermute | solution.py:22
  11.8 2.5 %collective-permute-start.6 = (bf16[72,1024]{1,0:T(8,128)(2,1)S(1)}, bf16[72,1024]{1,0:T(8,128)(2,1)S(1)}, u32[]{:S(2)}, u32[]{:S(2)}) collective-permute-start(bf16[72,1024]{1,0:T(8,128)(2,1)S(1)} %get-tuple-element.50), channel_id=1, source_target_pairs={{0,12},{2,14},{4,8},{6,10},{8,4},{10,6},{12,0},{14,2},{16,28},{18,... | collective-permute-start | bytes 442376 | tf_op jit(solution)/shard_map/ppermute | solution.py:22
  14.3 1.6 %collective-permute-start.7 = (bf16[72,1024]{1,0:T(8,128)(2,1)S(1)}, bf16[72,1024]{1,0:T(8,128)(2,1)S(1)}, u32[]{:S(2)}, u32[]{:S(2)}) collective-permute-start(bf16[72,1024]{1,0:T(8,128)(2,1)S(1)} %get-tuple-element.51), channel_id=1, source_target_pairs={{0,14},{2,12},{4,10},{6,8},{8,6},{10,4},{12,2},{14,0},{16,30},{18,... | collective-permute-start | bytes 442376 | tf_op jit(solution)/shard_map/ppermute | solution.py:22
  15.9 2.4 %shard_map.50 = (bf16[72,1024]{1,0:T(8,128)(2,1)S(1)}, bf16[72,1024]{1,0:T(8,128)(2,1)S(1)}, bf16[72,1024]{1,0:T(8,128)(2,1)S(1)}, bf16[72,1024]{1,0:T(8,128)(2,...) custom-call(f32[8,1024]{1,0:T(8,128)S(1)} %get-tuple-element.38.rank, ...), custom_call_target="tpu_custom_call" | custom-call | flops 1073741824 | bytes 4194304 | tf_op jit(solution)/shard_map/pallas_call | solution.py:111
  19.0 4.0 %collective-permute-start = (bf16[72,1024]{1,0:T(8,128)(2,1)S(1)}, bf16[72,1024]{1,0:T(8,128)(2,1)S(1)}, u32[]{:S(2)}, u32[]{:S(2)}) collective-permute-start(bf16[72,1024]{1,0:T(8,128)(2,1)S(1)} %get-tuple-element.40), channel_id=1, source_target_pairs={{0,2},{2,0},{4,6},{6,4},{8,10},{10,8},{12,14},{14,12},{16,18},{18,... | collective-permute-start | bytes 442376 | tf_op jit(solution)/shard_map/ppermute | solution.py:22
  25.7 2.7 %collective-permute-start.13 = (bf16[72,1024]{1,0:T(8,128)(2,1)}, bf16[72,1024]{1,0:T(8,128)(2,1)}, u32[]{:S(2)}, u32[]{:S(2)}) collective-permute-start(bf16[72,1024]{1,0:T(8,128)(2,1)} %get-tuple-element.61), channel_id=1, source_target_pairs={{0,12},{2,14},{4,8},{6,10},{8,4},{10,6},{12,0},{14,2},{16,28},{18,... | collective-permute-start | bytes 442376 | tf_op jit(solution)/shard_map/ppermute | solution.py:22
  29.6 2.6 %collective-permute-start.8 = (f32[128,1024]{1,0:T(8,128)}, f32[128,1024]{1,0:T(8,128)S(1)}, u32[]{:S(2)}, u32[]{:S(2)}) collective-permute-start(f32[128,1024]{1,0:T(8,128)} %get-tuple-element.52), channel_id=1, source_target_pairs={{0,16},{2,18},{4,20},{6,22},{8,24},{10,26},{12,28},{14,30},{16,0},... | collective-permute-start | bytes 1572872 | tf_op jit(solution)/shard_map/ppermute | solution.py:22
  32.2 2.9 %copy.8 = bf16[1024,1024]{0,1:T(8,128)(2,1)S(1)} copy(bf16[1024,1024]{1,0:T(8,128)(2,1)} %points_ref.3) | data formatting | bytes 4194304 | tf_op jit(solution)/shard_map/optimization_barrier | solution.py:313
  35.0 2.2 %copy-done.6 = bf16[2048,1024]{1,0:T(8,128)(2,1)S(1)} copy-done((bf16[2048,1024]{1,0:T(8,128)(2,1)S(1)}, bf16[2048,1024]{1,0:T(8,128)(2,1)}, u32[]{:S(2)}) %copy-start.6) | copy-done | bytes 4194328
  37.2 5.1 %first_lowest.1 = f32[8,1024]{1,0:T(8,128)S(1)} custom-call(bf16[2048,1024]{1,0:T(8,128)(2,1)S(1)} %copy-done.6, bf16[1024,1024]{1,0:T(8,128)(2,1)S(1)} %bitcast.4), custom_call_target="tpu_custom_call" | custom-call | flops 4294967296 | bytes 4194304 | tf_op jit(solution)/shard_map/first_lowest/pallas_call | solution.py:184
  46.3 3.2 %collective-permute-done.14.refs_7_ = bf16[72,1024]{1,0:T(8,128)(2,1)S(1)} collective-permute-done((bf16[72,1024]{1,0:T(8,128)(2,1)S(1)}, bf16[72,1024]{1,0:T(8,128)(2,1)S(1)}, u32[]{:S(2)}, u32[]{:S(2)}) %collective-permute-start.14) | collective-permute-done | bytes 147488 | tf_op jit(solution)/shard_map/ppermute | solution.py:22
  53.4 3.9 %collective-permute-start.29 = (bf16[128,1024]{1,0:T(8,128)(2,1)S(1)}, bf16[128,1024]{1,0:T(8,128)(2,1)S(1)}, u32[]{:S(2)}, u32[]{:S(2)}) collective-permute-start(bf16[128,1024]{1,0:T(8,128)(2,1)S(1)} %renew.1.refs_0_), channel_id=1, source_target_pairs={{0,4},{2,6},{4,0},{6,2},{8,12},{10,14},{12,8},{14,10},{16,20},{18,... | collective-permute-start | bytes 786440 | tf_op jit(solution)/shard_map/ppermute | solution.py:22
  57.2 2.9 %collective-permute-start.16 = (bf16[128,1024]{1,0:T(8,128)(2,1)S(1)}, bf16[128,1024]{1,0:T(8,128)(2,1)S(1)}, u32[]{:S(2)}, u32[]{:S(2)}) collective-permute-start(bf16[128,1024]{1,0:T(8,128)(2,1)S(1)} %renew.1.refs_0_), channel_id=1, source_target_pairs={{0,16},{2,18},{4,20},{6,22},{8,24},{10,26},{12,28},{14,30},{16,0},... | collective-permute-start | bytes 786440 | tf_op jit(solution)/shard_map/ppermute | solution.py:22
  62.3 3.5 %collective-permute-start.25 = (bf16[128,1024]{1,0:T(8,128)(2,1)S(1)}, bf16[128,1024]{1,0:T(8,128)(2,1)}, u32[]{:S(2)}, u32[]{:S(2)}) collective-permute-start(bf16[128,1024]{1,0:T(8,128)(2,1)S(1)} %collective-permute-done.24.refs_0_), channel_id=1, source_target_pairs={{0,2},{2,0},{4,6},{6,4},{8,10},{10,8},{12,14},{14,12},{16,18},{18,... | collective-permute-start | bytes 786440 | tf_op jit(solution)/shard_map/ppermute | solution.py:22
  67.2 5.0 %collective-permute-start.26 = (bf16[128,1024]{1,0:T(8,128)(2,1)S(1)}, bf16[128,1024]{1,0:T(8,128)(2,1)S(1)}, u32[]{:S(2)}, u32[]{:S(2)}) collective-permute-start(bf16[128,1024]{1,0:T(8,128)(2,1)S(1)} %collective-permute-done.24.refs_0_), channel_id=1, source_target_pairs={{0,4},{2,6},{4,0},{6,2},{8,12},{10,14},{12,8},{14,10},{16,20},{18,... | collective-permute-start | bytes 786440 | tf_op jit(solution)/shard_map/ppermute | solution.py:22
  72.2 2.5 %collective-permute-done.16.refs_4_ = bf16[128,1024]{1,0:T(8,128)(2,1)S(1)} collective-permute-done((bf16[128,1024]{1,0:T(8,128)(2,1)S(1)}, bf16[128,1024]{1,0:T(8,128)(2,1)S(1)}, u32[]{:S(2)}, u32[]{:S(2)}) %collective-permute-start.16) | collective-permute-done | bytes 262176 | tf_op jit(solution)/shard_map/ppermute | solution.py:22
  80.2 1.8 %collective-permute-start.23 = (bf16[128,1024]{1,0:T(8,128)(2,1)S(1)}, bf16[128,1024]{1,0:T(8,128)(2,1)}, u32[]{:S(2)}, u32[]{:S(2)}) collective-permute-start(bf16[128,1024]{1,0:T(8,128)(2,1)S(1)} %collective-permute-done.19.refs_5_), channel_id=1, source_target_pairs={{0,4},{2,6},{4,0},{6,2},{8,12},{10,14},{12,8},{14,10},{16,20},{18,... | collective-permute-start | bytes 786440 | tf_op jit(solution)/shard_map/ppermute | solution.py:22
  82.1 2.4 %collective-permute-done.17.refs_1_ = bf16[128,1024]{1,0:T(8,128)(2,1)} collective-permute-done((bf16[128,1024]{1,0:T(8,128)(2,1)S(1)}, bf16[128,1024]{1,0:T(8,128)(2,1)}, u32[]{:S(2)}, u32[]{:S(2)}) %collective-permute-start.17) | collective-permute-done | bytes 262176 | tf_op jit(solution)/shard_map/ppermute | solution.py:22
  85.3 1.8 %collective-permute-start.21 = (bf16[128,1024]{1,0:T(8,128)(2,1)}, bf16[128,1024]{1,0:T(8,128)(2,1)S(1)}, u32[]{:S(2)}, u32[]{:S(2)}) collective-permute-start(bf16[128,1024]{1,0:T(8,128)(2,1)} %collective-permute-done.20.refs_2_), channel_id=1, source_target_pairs={{0,4},{2,6},{4,0},{6,2},{8,12},{10,14},{12,8},{14,10},{16,20},{18,... | collective-permute-start | bytes 786440 | tf_op jit(solution)/shard_map/ppermute | solution.py:22
  90.9 1.9 %shard_map.54 = (f32[8,1024]{1,0:T(8,128)S(1)}, bf16[2048,1024]{1,0:T(8,128)(2,1)}) custom-call(bf16[128,1024]{1,0:T(8,128)(2,1)S(1)} %copy-done.5, bf16[128,1024]{1,0:T(8,128)(2,1)S(1)} %copy-done.10, bf16[128,1024]{1,0:T(8,128)(2,1)S(1)} %copy-done.8, bf16[128,1024]{1,0:T(8,128)(2,1)S(1)} %copy-done.12, bf16[1024,1024]{1,0:T(8,128)(2,1)S(1)} %bitcast.5), custom_call_target="tpu_custom_call" | custom-call | flops 1073741824 | bytes 2097152 | tf_op jit(solution)/shard_map/pallas_call | solution.py:284
  93.8 3.6 %shard_map.55 = (f32[8,1024]{1,0:T(8,128)S(1)}, bf16[2048,1024]{1,0:T(8,128)(2,1)}) custom-call(bf16[128,1024]{1,0:T(8,128)(2,1)S(1)} %collective-permute-done.24.refs_0_, bf16[128,1024]{1,0:T(8,128)(2,1)} %collective-permute-done.25.refs_1_, bf16[128,1024]{1,0:T(8,128)(2,1)S(1)} %copy-done.3, ...), custom_call_target="tpu_custom_call", output_to_operand_aliasing={{1}: (8, {})} | custom-call | flops 1610612736 | bytes 3145728 | tf_op jit(solution)/shard_map/pallas_call | solution.py:284
  97.4 3.1 %shard_map.56 = (f32[8,1024]{1,0:T(8,128)S(1)}, bf16[2048,1024]{1,0:T(8,128)(2,1)}) custom-call(bf16[128,1024]{1,0:T(8,128)(2,1)} %collective-permute-done.22.refs_0_, bf16[128,1024]{1,0:T(8,128)(2,1)} %collective-permute-done.17.refs_1_, bf16[128,1024]{1,0:T(8,128)(2,1)} %collective-permute-done.20.refs_2_, ...), custom_call_target="tpu_custom_call", output_to_operand_aliasing={{1}: (6, {})} | custom-call | flops 1073741824 | bytes 2097152 | tf_op jit(solution)/shard_map/pallas_call | solution.py:284
  (95 shorter events, 34.1 us)
Async XLA Ops:
  8.4 10.6 %collective-permute-start.3 = (bf16[72,1024]{1,0:T(8,128)(2,1)S(1)}, bf16[72,1024]{1,0:T(8,128)(2,1)S(1)}, u32[]{:S(2)}, u32[]{:S(2)}) collective-permute-start(bf16[72,1024]{1,0:T(8,128)(2,1)S(1)} %get-tuple-element.47), channel_id=1, source_target_pairs={{0,6},{2,4},{4,2},{6,0},{8,14},{10,12},{12,10},{14,8},{16,22},{18,... | collective-permute-start | bytes 442376 | tf_op jit(solution)/shard_map/ppermute | solution.py:22
  8.4 15.5 %collective-permute-start.4 = (bf16[72,1024]{1,0:T(8,128)(2,1)S(1)}, bf16[72,1024]{1,0:T(8,128)(2,1)S(1)}, u32[]{:S(2)}, u32[]{:S(2)}) collective-permute-start(bf16[72,1024]{1,0:T(8,128)(2,1)S(1)} %get-tuple-element.48), channel_id=1, source_target_pairs={{0,8},{2,10},{4,12},{6,14},{8,0},{10,2},{12,4},{14,6},{16,24},{18,... | collective-permute-start | bytes 442376 | tf_op jit(solution)/shard_map/ppermute | solution.py:22
  10.4 13.6 %collective-permute-start.5 = (bf16[72,1024]{1,0:T(8,128)(2,1)S(1)}, bf16[72,1024]{1,0:T(8,128)(2,1)S(1)}, u32[]{:S(2)}, u32[]{:S(2)}) collective-permute-start(bf16[72,1024]{1,0:T(8,128)(2,1)S(1)} %get-tuple-element.49), channel_id=1, source_target_pairs={{0,10},{2,8},{4,14},{6,12},{8,2},{10,0},{12,6},{14,4},{16,26},{18,... | collective-permute-start | bytes 442376 | tf_op jit(solution)/shard_map/ppermute | solution.py:22
  11.8 12.8 %collective-permute-start.6 = (bf16[72,1024]{1,0:T(8,128)(2,1)S(1)}, bf16[72,1024]{1,0:T(8,128)(2,1)S(1)}, u32[]{:S(2)}, u32[]{:S(2)}) collective-permute-start(bf16[72,1024]{1,0:T(8,128)(2,1)S(1)} %get-tuple-element.50), channel_id=1, source_target_pairs={{0,12},{2,14},{4,8},{6,10},{8,4},{10,6},{12,0},{14,2},{16,28},{18,... | collective-permute-start | bytes 442376 | tf_op jit(solution)/shard_map/ppermute | solution.py:22
  14.3 11.4 %collective-permute-start.7 = (bf16[72,1024]{1,0:T(8,128)(2,1)S(1)}, bf16[72,1024]{1,0:T(8,128)(2,1)S(1)}, u32[]{:S(2)}, u32[]{:S(2)}) collective-permute-start(bf16[72,1024]{1,0:T(8,128)(2,1)S(1)} %get-tuple-element.51), channel_id=1, source_target_pairs={{0,14},{2,12},{4,10},{6,8},{8,6},{10,4},{12,2},{14,0},{16,30},{18,... | collective-permute-start | bytes 442376 | tf_op jit(solution)/shard_map/ppermute | solution.py:22
  19.0 10.6 %collective-permute-start = (bf16[72,1024]{1,0:T(8,128)(2,1)S(1)}, bf16[72,1024]{1,0:T(8,128)(2,1)S(1)}, u32[]{:S(2)}, u32[]{:S(2)}) collective-permute-start(bf16[72,1024]{1,0:T(8,128)(2,1)S(1)} %get-tuple-element.40), channel_id=1, source_target_pairs={{0,2},{2,0},{4,6},{6,4},{8,10},{10,8},{12,14},{14,12},{16,18},{18,... | collective-permute-start | bytes 442376 | tf_op jit(solution)/shard_map/ppermute | solution.py:22
  23.9 18.4 %collective-permute-start.10 = (bf16[72,1024]{1,0:T(8,128)(2,1)}, bf16[72,1024]{1,0:T(8,128)(2,1)S(1)}, u32[]{:S(2)}, u32[]{:S(2)}) collective-permute-start(bf16[72,1024]{1,0:T(8,128)(2,1)} %get-tuple-element.58), channel_id=1, source_target_pairs={{0,6},{2,4},{4,2},{6,0},{8,14},{10,12},{12,10},{14,8},{16,22},{18,... | collective-permute-start | bytes 442376 | tf_op jit(solution)/shard_map/ppermute | solution.py:22
  24.0 19.9 %collective-permute-start.11 = (bf16[72,1024]{1,0:T(8,128)(2,1)}, bf16[72,1024]{1,0:T(8,128)(2,1)S(1)}, u32[]{:S(2)}, u32[]{:S(2)}) collective-permute-start(bf16[72,1024]{1,0:T(8,128)(2,1)} %get-tuple-element.59), channel_id=1, source_target_pairs={{0,8},{2,10},{4,12},{6,14},{8,0},{10,2},{12,4},{14,6},{16,24},{18,... | collective-permute-start | bytes 442376 | tf_op jit(solution)/shard_map/ppermute | solution.py:22
  24.6 21.3 %collective-permute-start.12 = (bf16[72,1024]{1,0:T(8,128)(2,1)}, bf16[72,1024]{1,0:T(8,128)(2,1)}, u32[]{:S(2)}, u32[]{:S(2)}) collective-permute-start(bf16[72,1024]{1,0:T(8,128)(2,1)} %get-tuple-element.60), channel_id=1, source_target_pairs={{0,10},{2,8},{4,14},{6,12},{8,2},{10,0},{12,6},{14,4},{16,26},{18,... | collective-permute-start | bytes 442376 | tf_op jit(solution)/shard_map/ppermute | solution.py:22
  25.7 20.6 %collective-permute-start.13 = (bf16[72,1024]{1,0:T(8,128)(2,1)}, bf16[72,1024]{1,0:T(8,128)(2,1)}, u32[]{:S(2)}, u32[]{:S(2)}) collective-permute-start(bf16[72,1024]{1,0:T(8,128)(2,1)} %get-tuple-element.61), channel_id=1, source_target_pairs={{0,12},{2,14},{4,8},{6,10},{8,4},{10,6},{12,0},{14,2},{16,28},{18,... | collective-permute-start | bytes 442376 | tf_op jit(solution)/shard_map/ppermute | solution.py:22
  29.6 22.5 %collective-permute-start.8 = (f32[128,1024]{1,0:T(8,128)}, f32[128,1024]{1,0:T(8,128)S(1)}, u32[]{:S(2)}, u32[]{:S(2)}) collective-permute-start(f32[128,1024]{1,0:T(8,128)} %get-tuple-element.52), channel_id=1, source_target_pairs={{0,16},{2,18},{4,20},{6,22},{8,24},{10,26},{12,28},{14,30},{16,0},... | collective-permute-start | bytes 1572872 | tf_op jit(solution)/shard_map/ppermute | solution.py:22
  52.3 9.9 %collective-permute-start.24 = (bf16[128,1024]{1,0:T(8,128)(2,1)S(1)}, bf16[128,1024]{1,0:T(8,128)(2,1)S(1)}, u32[]{:S(2)}, u32[]{:S(2)}) collective-permute-start(bf16[128,1024]{1,0:T(8,128)(2,1)S(1)} %renew.1.refs_0_), channel_id=1, source_target_pairs={{0,8},{2,10},{4,12},{6,14},{8,0},{10,2},{12,4},{14,6},{16,24},{18,... | collective-permute-start | bytes 786440 | tf_op jit(solution)/shard_map/ppermute | solution.py:22
  53.4 12.4 %collective-permute-start.29 = (bf16[128,1024]{1,0:T(8,128)(2,1)S(1)}, bf16[128,1024]{1,0:T(8,128)(2,1)S(1)}, u32[]{:S(2)}, u32[]{:S(2)}) collective-permute-start(bf16[128,1024]{1,0:T(8,128)(2,1)S(1)} %renew.1.refs_0_), channel_id=1, source_target_pairs={{0,4},{2,6},{4,0},{6,2},{8,12},{10,14},{12,8},{14,10},{16,20},{18,... | collective-permute-start | bytes 786440 | tf_op jit(solution)/shard_map/ppermute | solution.py:22
  57.2 17.5 %collective-permute-start.16 = (bf16[128,1024]{1,0:T(8,128)(2,1)S(1)}, bf16[128,1024]{1,0:T(8,128)(2,1)S(1)}, u32[]{:S(2)}, u32[]{:S(2)}) collective-permute-start(bf16[128,1024]{1,0:T(8,128)(2,1)S(1)} %renew.1.refs_0_), channel_id=1, source_target_pairs={{0,16},{2,18},{4,20},{6,22},{8,24},{10,26},{12,28},{14,30},{16,0},... | collective-permute-start | bytes 786440 | tf_op jit(solution)/shard_map/ppermute | solution.py:22
  60.1 15.2 %collective-permute-start.19 = (bf16[128,1024]{1,0:T(8,128)(2,1)S(1)}, bf16[128,1024]{1,0:T(8,128)(2,1)S(1)}, u32[]{:S(2)}, u32[]{:S(2)}) collective-permute-start(bf16[128,1024]{1,0:T(8,128)(2,1)S(1)} %renew.1.refs_0_), channel_id=1, source_target_pairs={{0,24},{2,26},{4,28},{6,30},{8,16},{10,18},{12,20},{14,22},{16,8},... | collective-permute-start | bytes 786440 | tf_op jit(solution)/shard_map/ppermute | solution.py:22
  62.3 14.6 %collective-permute-start.25 = (bf16[128,1024]{1,0:T(8,128)(2,1)S(1)}, bf16[128,1024]{1,0:T(8,128)(2,1)}, u32[]{:S(2)}, u32[]{:S(2)}) collective-permute-start(bf16[128,1024]{1,0:T(8,128)(2,1)S(1)} %collective-permute-done.24.refs_0_), channel_id=1, source_target_pairs={{0,2},{2,0},{4,6},{6,4},{8,10},{10,8},{12,14},{14,12},{16,18},{18,... | collective-permute-start | bytes 786440 | tf_op jit(solution)/shard_map/ppermute | solution.py:22
  65.7 12.3 %collective-permute-start.30 = (bf16[128,1024]{1,0:T(8,128)(2,1)S(1)}, bf16[128,1024]{1,0:T(8,128)(2,1)S(1)}, u32[]{:S(2)}, u32[]{:S(2)}) collective-permute-start(bf16[128,1024]{1,0:T(8,128)(2,1)S(1)} %collective-permute-done.29.refs_2_), channel_id=1, source_target_pairs={{0,2},{2,0},{4,6},{6,4},{8,10},{10,8},{12,14},{14,12},{16,18},{18,... | collective-permute-start | bytes 786440 | tf_op jit(solution)/shard_map/ppermute | solution.py:22
  67.2 12.3 %collective-permute-start.26 = (bf16[128,1024]{1,0:T(8,128)(2,1)S(1)}, bf16[128,1024]{1,0:T(8,128)(2,1)S(1)}, u32[]{:S(2)}, u32[]{:S(2)}) collective-permute-start(bf16[128,1024]{1,0:T(8,128)(2,1)S(1)} %collective-permute-done.24.refs_0_), channel_id=1, source_target_pairs={{0,4},{2,6},{4,0},{6,2},{8,12},{10,14},{12,8},{14,10},{16,20},{18,... | collective-permute-start | bytes 786440 | tf_op jit(solution)/shard_map/ppermute | solution.py:22
  75.3 10.0 %collective-permute-start.20 = (bf16[128,1024]{1,0:T(8,128)(2,1)S(1)}, bf16[128,1024]{1,0:T(8,128)(2,1)}, u32[]{:S(2)}, u32[]{:S(2)}) collective-permute-start(bf16[128,1024]{1,0:T(8,128)(2,1)S(1)} %collective-permute-done.19.refs_5_), channel_id=1, source_target_pairs={{0,2},{2,0},{4,6},{6,4},{8,10},{10,8},{12,14},{14,12},{16,18},{18,... | collective-permute-start | bytes 786440 | tf_op jit(solution)/shard_map/ppermute | solution.py:22
  76.9 15.9 %collective-permute-start.27 = (bf16[128,1024]{1,0:T(8,128)(2,1)}, bf16[128,1024]{1,0:T(8,128)(2,1)}, u32[]{:S(2)}, u32[]{:S(2)}) collective-permute-start(bf16[128,1024]{1,0:T(8,128)(2,1)} %collective-permute-done.25.refs_1_), channel_id=1, source_target_pairs={{0,4},{2,6},{4,0},{6,2},{8,12},{10,14},{12,8},{14,10},{16,20},{18,... | collective-permute-start | bytes 786440 | tf_op jit(solution)/shard_map/ppermute | solution.py:22
  78.8 18.6 %collective-permute-start.22 = (bf16[128,1024]{1,0:T(8,128)(2,1)S(1)}, bf16[128,1024]{1,0:T(8,128)(2,1)}, u32[]{:S(2)}, u32[]{:S(2)}) collective-permute-start(bf16[128,1024]{1,0:T(8,128)(2,1)S(1)} %collective-permute-done.16.refs_4_), channel_id=1, source_target_pairs={{0,2},{2,0},{4,6},{6,4},{8,10},{10,8},{12,14},{14,12},{16,18},{18,... | collective-permute-start | bytes 786440 | tf_op jit(solution)/shard_map/ppermute | solution.py:22
  80.2 17.2 %collective-permute-start.23 = (bf16[128,1024]{1,0:T(8,128)(2,1)S(1)}, bf16[128,1024]{1,0:T(8,128)(2,1)}, u32[]{:S(2)}, u32[]{:S(2)}) collective-permute-start(bf16[128,1024]{1,0:T(8,128)(2,1)S(1)} %collective-permute-done.19.refs_5_), channel_id=1, source_target_pairs={{0,4},{2,6},{4,0},{6,2},{8,12},{10,14},{12,8},{14,10},{16,20},{18,... | collective-permute-start | bytes 786440 | tf_op jit(solution)/shard_map/ppermute | solution.py:22
  84.5 16.1 %collective-permute-start.18 = (bf16[128,1024]{1,0:T(8,128)(2,1)}, bf16[128,1024]{1,0:T(8,128)(2,1)S(1)}, u32[]{:S(2)}, u32[]{:S(2)}) collective-permute-start(bf16[128,1024]{1,0:T(8,128)(2,1)} %collective-permute-done.17.refs_1_), channel_id=1, source_target_pairs={{0,2},{2,0},{4,6},{6,4},{8,10},{10,8},{12,14},{14,12},{16,18},{18,... | collective-permute-start | bytes 786440 | tf_op jit(solution)/shard_map/ppermute | solution.py:22
  85.3 15.3 %collective-permute-start.21 = (bf16[128,1024]{1,0:T(8,128)(2,1)}, bf16[128,1024]{1,0:T(8,128)(2,1)S(1)}, u32[]{:S(2)}, u32[]{:S(2)}) collective-permute-start(bf16[128,1024]{1,0:T(8,128)(2,1)} %collective-permute-done.20.refs_2_), channel_id=1, source_target_pairs={{0,4},{2,6},{4,0},{6,2},{8,12},{10,14},{12,8},{14,10},{16,20},{18,... | collective-permute-start | bytes 786440 | tf_op jit(solution)/shard_map/ppermute | solution.py:22
  (26 other events, 96.1 us)

commit v4 on v3

--- a/solution.py
+++ b/solution.py
@@ -14,6 +14,7 @@
 ANY = pl.BlockSpec(memory_space=pl.ANY)
 HBM = pl.BlockSpec(memory_space=pltpu.HBM)
 LIMIT = 24 * 1024 * 1024
+WIDE = 58 * 1024 * 1024
 LABEL_ROWS = 8
 
 
@@ -85,37 +86,38 @@
     )(assign_row)
 
 
-def place_kernel(half, capacity, rank_ref, label_ref, points_ref, *outs):
+def place_kernel(masks, capacity, rank_ref, label_ref, points_ref, *outs):
     count = points_ref.shape[0]
     slots = lax.broadcasted_iota(jnp.int32, (capacity, count), 0).astype(F32)
     placing = jnp.concatenate(
         [
             jnp.where(slots == rank_ref[m : m + 1, :], 1.0, 0.0).astype(BF16)
-            for m in range(half)
+            for m in masks
         ],
         axis=0,
     )
     placed = jnp.dot(placing, points_ref[...], preferred_element_type=F32).astype(BF16)
     labels = jnp.dot(placing, label_ref[...], preferred_element_type=F32)
     labels = (jnp.transpose(labels) - 1.0).astype(BF16)
-    for m in range(half):
+    for m in range(len(masks)):
         outs[m][:capacity, :] = placed[m * capacity : (m + 1) * capacity]
         outs[m][capacity:, :] = jnp.zeros((LABEL_ROWS, outs[m].shape[1]), BF16)
         outs[m][capacity:, :capacity] = labels[:, m * capacity : (m + 1) * capacity]
 
 
-def place(rank, label, points, capacity):
-    half = rank.shape[0]
+def place(rank, label, points, capacity, masks):
+    half = len(masks)
     count, width = points.shape
     block = jax.ShapeDtypeStruct((capacity + LABEL_ROWS, width), BF16)
-    return pl.pallas_call(
-        functools.partial(place_kernel, half, capacity),
+    blocks = pl.pallas_call(
+        functools.partial(place_kernel, masks, capacity),
         out_shape=[block] * half,
         in_specs=[VMEM] * 3,
         out_specs=[VMEM] * half,
         compiler_params=params(),
         cost_estimate=cost(2 * half * capacity * count * width, 4 * count * width),
     )(rank, label, points)
+    return dict(zip(masks, blocks, strict=True))
 
 
 def sum_kernel(share, capacity, *refs):
@@ -169,24 +171,29 @@
     return jnp.min(scores.reshape(-1, 8, scores.shape[1]), axis=0)
 
 
-def first_kernel(step, cents_ref, columns_ref, out_ref):
-    out_ref[...] = jnp.full(out_ref.shape, jnp.inf, F32)
-
-    @pl.loop(0, cents_ref.shape[0] // step)
-    def _(i):
-        start = pl.multiple_of(i * step, step)
-        out_ref[...] = jnp.minimum(
-            out_ref[...], lowest(cents_ref[pl.ds(start, step), :], columns_ref[...])
-        )
+def first_kernel(cents_ref, columns_ref, out_ref):
+    found = lowest(cents_ref[...], columns_ref[...])
+
+    @pl.when(pl.program_id(0) == 0)
+    def _():
+        out_ref[...] = found
+
+    @pl.when(pl.program_id(0) > 0)
+    def _():
+        out_ref[...] = jnp.minimum(out_ref[...], found)
 
 
 def first_lowest(cents, columns):
-    return pl.pallas_call(
-        functools.partial(first_kernel, 512),
-        out_shape=jax.ShapeDtypeStruct((8, columns.shape[1]), F32),
-        in_specs=[VMEM, VMEM],
-        out_specs=VMEM,
-        compiler_params=params(),
+    count, width = cents.shape
+    step = 512 if count % 512 == 0 else 256
+    out = jax.ShapeDtypeStruct((8, columns.shape[1]), F32)
+    return pl.pallas_call(
+        first_kernel,
+        grid=(count // step,),
+        out_shape=out,
+        in_specs=[pl.BlockSpec((step, width), lambda i: (i, 0)), VMEM],
+        out_specs=pl.BlockSpec(out.shape, lambda i: (0, 0)),
+        compiler_params=pltpu.CompilerParams(vmem_limit_bytes=WIDE),
         cost_estimate=cost(2 * cents.size * columns.shape[1], 2 * cents.size),
         name="first_lowest",
     )(cents, columns)
@@ -305,9 +312,12 @@
     assign_row = assign.reshape(1, -1)
 
     far_rank, near_rank, far_label, near_label = ranks(assign_row, half, share)
-    far = place(far_rank, far_label, points, capacity)
+    powers = [m for m in range(half) if m and m & (m - 1) == 0]
+    others = [m for m in range(half) if m not in powers]
+    far = place(far_rank, far_label, points, capacity, powers)
+    far |= place(far_rank, far_label, points, capacity, others)
     far = [far[0]] + [swap(far[m], m) for m in range(1, half)]
-    near = place(near_rank, near_label, points, capacity)
+    near = place(near_rank, near_label, points, capacity, range(half))
     near = [near[0]] + [swap(near[m], m) for m in range(1, half)]
     far_sums, far_counts = add_up(far, share, capacity)
     near[1], late = lax.optimization_barrier((near[1], points))

time: 104 us -> 107 us (1.029)
  Pallas kernels: 22.2 us -> 27.8 us
  starting transfers between devices: 52.8 us -> 47.6 us
  waiting for transfers between devices: 9.83 us -> 13.7 us
  local copies, waits for them, and re-layouts: 16.3 us -> 15.1 us
    ppermute x32, starting transfers between devices: 52.8 us -> 47.6 us  [swap(): return lax.ppermute(value, axis, [(i, i ^ mask) for i in range(size)])]
    pallas_call x3 -> x4, Pallas kernels: 9.08 us -> 13.4 us  [the longest x1 7.83 us: first_lowest(): pl.pallas_call(first_kernel, grid=(count // step,), out_shape=out, in_spe...]
    ppermute x32, waiting for transfers between devices: 9.83 us -> 13.7 us  [swap(): return lax.ppermute(value, axis, [(i, i ^ mask) for i in range(size)])]
    pallas_call x2, Pallas kernels: 2.5 us -> 3.69 us  [add_up(): pl.pallas_call(functools.partial(sum_kernel, share, capacity), out_shape=...]
    unnamed x36 -> x46, local copies, waits for them, and re-layouts: 12.5 us -> 11.6 us
  transfers between devices with their start and end apart: 32 -> 32, of which waited for: 6 -> 4; matrix products, arithmetic and copies ran while one was open for 4% -> 4% of each run, Pallas kernels for 19% -> 23%
where the time goes in v4:
time: 107 us; the launch traced here: 106 us
  starting transfers between devices  47.6 us (44%)
  Pallas kernels  27.8 us (26%)
  local copies, waits for them, and re-layouts  15.1 us (14%)
  waiting for transfers between devices  13.7 us (13%)
  other arithmetic  1.13 us (1%)
    ppermute x32, starting transfers between devices, swap(): return lax.ppermute(value, axis, [(i, i ^ mask) for i in range(size)])  47.6 us
    ppermute x32, waiting for transfers between devices, swap(): return lax.ppermute(value, axis, [(i, i ^ mask) for i in range(size)])  13.7 us
    unnamed x46, local copies, waits for them, and re-layouts  11.6 us
    pallas_call x3, Pallas kernels, arrive(): pl.pallas_call(functools.partial(arrive_kernel, share, places, fresh), ou...  8.63 us
    pallas_call x1, Pallas kernels, first_lowest(): pl.pallas_call(first_kernel, grid=(count // step,), out_shape=out, in_spe...  7.83 us
    pallas_call x3, Pallas kernels, place(): pl.pallas_call(functools.partial(place_kernel, masks, capacity), out_shap...  5.56 us
    pallas_call x2, Pallas kernels, add_up(): pl.pallas_call(functools.partial(sum_kernel, share, capacity), out_shape=...  3.69 us
    optimization_barrier x1, local copies, waits for them, and re-layouts, halves(): near[1], late = lax.optimization_barrier((near[1], points))  2.54 us
  transfers between devices with their start and end apart: 32, of which 4 were waited for; matrix products, arithmetic and copies ran while one was open for 4% of the time, Pallas kernels for 23%

profile of v4, /device:TPU:0, one launch (start us, length us, event | category | flops | bytes accessed | tf_op | source)
XLA Modules:
  0.0 106.3 jit_solution(4982494871535495373)
XLA Ops:
  2.2 1.8 %shard_map.51 = (bf16[72,1024]{1,0:T(8,128)(2,1)S(1)}, bf16[72,1024]{1,0:T(8,128)(2,1)S(1)}, bf16[72,1024]{1,0:T(8,128)(2,1)S(1)}, bf16[72,1024]{1,0:T(8,128)(2,1)S(1)}, bf16[72,1024]{1,0:T(8,128)(2,1)}) custom-call(f32[8,1024]{1,0:T(8,128)S(1)} %get-tuple-element.42.rank_ref, bf16[1024,8]{1,0:T(8,128)(2,1)S(1)} %get-tuple-element.43.label_ref, ...), custom_call_target="tpu_custom_call" | custom-call | flops 671088640 | bytes 4194304 | tf_op jit(solution)/shard_map/pallas_call | solution.py:112
  4.0 3.9 %collective-permute-start.3 = (bf16[72,1024]{1,0:T(8,128)(2,1)S(1)}, bf16[72,1024]{1,0:T(8,128)(2,1)S(1)}, u32[]{:S(2)}, u32[]{:S(2)}) collective-permute-start(bf16[72,1024]{1,0:T(8,128)(2,1)S(1)} %get-tuple-element.47), channel_id=1, source_target_pairs={{0,6},{2,4},{4,2},{6,0},{8,14},{10,12},{12,10},{14,8},{16,22},{18,... | collective-permute-start | bytes 442376 | tf_op jit(solution)/shard_map/ppermute | solution.py:23
  8.0 1.5 %collective-permute-start.5 = (bf16[72,1024]{1,0:T(8,128)(2,1)S(1)}, bf16[72,1024]{1,0:T(8,128)(2,1)S(1)}, u32[]{:S(2)}, u32[]{:S(2)}) collective-permute-start(bf16[72,1024]{1,0:T(8,128)(2,1)S(1)} %get-tuple-element.49), channel_id=1, source_target_pairs={{0,10},{2,8},{4,14},{6,12},{8,2},{10,0},{12,6},{14,4},{16,26},{18,... | collective-permute-start | bytes 442376 | tf_op jit(solution)/shard_map/ppermute | solution.py:23
  9.5 3.9 %collective-permute-start.7 = (bf16[72,1024]{1,0:T(8,128)(2,1)}, bf16[72,1024]{1,0:T(8,128)(2,1)S(1)}, u32[]{:S(2)}, u32[]{:S(2)}) collective-permute-start(bf16[72,1024]{1,0:T(8,128)(2,1)} %get-tuple-element.51), channel_id=1, source_target_pairs={{0,14},{2,12},{4,10},{6,8},{8,6},{10,4},{12,2},{14,0},{16,30},{18,... | collective-permute-start | bytes 442376 | tf_op jit(solution)/shard_map/ppermute | solution.py:23
  13.4 1.5 %shard_map.52 = (bf16[72,1024]{1,0:T(8,128)(2,1)}, bf16[72,1024]{1,0:T(8,128)(2,1)}, bf16[72,1024]{1,0:T(8,128)(2,1)}) custom-call(f32[8,1024]{1,0:T(8,128)S(1)} %get-tuple-element.42.rank_ref, bf16[1024,8]{1,0:T(8,128)(2,1)S(1)} %get-tuple-element.43.label_ref, bf16[1024,1024]{1,0:T(8,128)(2,1)S(1)} %copy-done.1), custom_call_target="tpu_custom_call" | custom-call | flops 402653184 | bytes 4194304 | tf_op jit(solution)/shard_map/pallas_call | solution.py:112
  16.4 1.6 %collective-permute-start.4 = (bf16[72,1024]{1,0:T(8,128)(2,1)}, bf16[72,1024]{1,0:T(8,128)(2,1)}, u32[]{:S(2)}, u32[]{:S(2)}) collective-permute-start(bf16[72,1024]{1,0:T(8,128)(2,1)} %get-tuple-element.48), channel_id=1, source_target_pairs={{0,8},{2,10},{4,12},{6,14},{8,0},{10,2},{12,4},{14,6},{16,24},{18,... | collective-permute-start | bytes 442376 | tf_op jit(solution)/shard_map/ppermute | solution.py:23
  18.0 2.2 %shard_map.50 = (bf16[72,1024]{1,0:T(8,128)(2,1)S(1)}, bf16[72,1024]{1,0:T(8,128)(2,1)}, bf16[72,1024]{1,0:T(8,128)(2,1)S(1)}, bf16[72,1024]{1,0:T(8,128)(2,1)S(...) custom-call(f32[8,1024]{1,0:T(8,128)S(1)} %get-tuple-element.38.rank, ...), custom_call_target="tpu_custom_call" | custom-call | flops 1073741824 | bytes 4194304 | tf_op jit(solution)/shard_map/pallas_call | solution.py:112
  22.3 4.1 %collective-permute-start = (bf16[72,1024]{1,0:T(8,128)(2,1)}, bf16[72,1024]{1,0:T(8,128)(2,1)S(1)}, u32[]{:S(2)}, u32[]{:S(2)}) collective-permute-start(bf16[72,1024]{1,0:T(8,128)(2,1)} %get-tuple-element.40), channel_id=1, source_target_pairs={{0,2},{2,0},{4,6},{6,4},{8,10},{10,8},{12,14},{14,12},{16,18},{18,... | collective-permute-start | bytes 442376 | tf_op jit(solution)/shard_map/ppermute | solution.py:23
  27.7 3.4 %collective-permute-start.12 = (bf16[72,1024]{1,0:T(8,128)(2,1)}, bf16[72,1024]{1,0:T(8,128)(2,1)}, u32[]{:S(2)}, u32[]{:S(2)}) collective-permute-start(bf16[72,1024]{1,0:T(8,128)(2,1)} %copy-done.18), channel_id=1, source_target_pairs={{0,10},{2,8},{4,14},{6,12},{8,2},{10,0},{12,6},{14,4},{16,26},{18,... | collective-permute-start | bytes 442376 | tf_op jit(solution)/shard_map/ppermute | solution.py:23
  32.0 2.2 %shard_map.53 = (f32[128,1024]{1,0:T(8,128)}, f32[8,128]{1,0:T(8,128)S(1)}) custom-call(bf16[72,1024]{1,0:T(8,128)(2,1)S(1)} %get-tuple-element.44.refs_0_, bf16[72,1024]{1,0:T(8,128)(2,1)} %collective-permute-done.1.refs_1_, bf16[72,1024]{1,0:T(8,128)(2,1)} %collective-permute-done.2.refs_2_, bf16[72,1024]{1,0:T(8,128)(2,1)S(1)} %collective-permute-done.3.refs_3_, ...), custom_call_target="tpu_custom_call" | custom-call | flops 134217728 | bytes 1572864 | tf_op jit(solution)/shard_map/pallas_call | solution.py:139
  34.2 2.6 %collective-permute-start.8 = (f32[128,1024]{1,0:T(8,128)}, f32[128,1024]{1,0:T(8,128)S(1)}, u32[]{:S(2)}, u32[]{:S(2)}) collective-permute-start(f32[128,1024]{1,0:T(8,128)} %get-tuple-element.52), channel_id=1, source_target_pairs={{0,16},{2,18},{4,20},{6,22},{8,24},{10,26},{12,28},{14,30},{16,0},... | collective-permute-start | bytes 1572872 | tf_op jit(solution)/shard_map/ppermute | solution.py:23
  36.8 2.5 %copy.8 = bf16[1024,1024]{0,1:T(8,128)(2,1)} copy(bf16[1024,1024]{1,0:T(8,128)(2,1)S(1)} %copy-done.1) | data formatting | bytes 4194304 | tf_op jit(solution)/shard_map/optimization_barrier | solution.py:323
  39.4 7.8 %first_lowest.1 = f32[8,1024]{1,0:T(8,128)} custom-call(bf16[2048,1024]{1,0:T(8,128)(2,1)} %cents_ref.1, bf16[1024,1024]{1,0:T(8,128)(2,1)} %bitcast.4), custom_call_target="tpu_custom_call" | custom-call | flops 4294967296 | bytes 4194304 | tf_op jit(solution)/shard_map/first_lowest/pallas_call | solution.py:190
  47.2 1.5 %collective-permute-start.14 = (bf16[72,1024]{1,0:T(8,128)(2,1)S(1)}, bf16[72,1024]{1,0:T(8,128)(2,1)S(1)}, u32[]{:S(2)}, u32[]{:S(2)}) collective-permute-start(bf16[72,1024]{1,0:T(8,128)(2,1)S(1)} %copy-done.16), channel_id=1, source_target_pairs={{0,14},{2,12},{4,10},{6,8},{8,6},{10,4},{12,2},{14,0},{16,30},{18,... | collective-permute-start | bytes 442376 | tf_op jit(solution)/shard_map/ppermute | solution.py:23
  51.1 7.2 %collective-permute-done.14.refs_7_ = bf16[72,1024]{1,0:T(8,128)(2,1)S(1)} collective-permute-done((bf16[72,1024]{1,0:T(8,128)(2,1)S(1)}, bf16[72,1024]{1,0:T(8,128)(2,1)S(1)}, u32[]{:S(2)}, u32[]{:S(2)}) %collective-permute-start.14) | collective-permute-done | bytes 147488 | tf_op jit(solution)/shard_map/ppermute | solution.py:23
  58.3 1.5 %shard_map.54 = (f32[128,1024]{1,0:T(8,128)S(1)}, f32[8,128]{1,0:T(8,128)S(1)}) custom-call(bf16[72,1024]{1,0:T(8,128)(2,1)S(1)} %get-tuple-element.55.refs_0_, bf16[72,1024]{1,0:T(8,128)(2,1)S(1)} %collective-permute-done.refs_1_, bf16[72,1024]{1,0:T(8,128)(2,1)S(1)} %collective-permute-done.9.refs_2_, bf16[72,1024]{1,0:T(8,128)(2,1)} %collective-permute-done.10.refs_3_, ...), custom_call_target="tpu_custom_call" | custom-call | flops 134217728 | bytes 1572864 | tf_op jit(solution)/shard_map/pallas_call | solution.py:139
  61.2 3.4 %collective-permute-start.28 = (bf16[128,1024]{1,0:T(8,128)(2,1)S(1)}, bf16[128,1024]{1,0:T(8,128)(2,1)S(1)}, u32[]{:S(2)}, u32[]{:S(2)}) collective-permute-start(bf16[128,1024]{1,0:T(8,128)(2,1)S(1)} %renew.1.refs_0_), channel_id=1, source_target_pairs={{0,2},{2,0},{4,6},{6,4},{8,10},{10,8},{12,14},{14,12},{16,18},{18,... | collective-permute-start | bytes 786440 | tf_op jit(solution)/shard_map/ppermute | solution.py:23
  64.6 3.5 %collective-permute-start.16 = (bf16[128,1024]{1,0:T(8,128)(2,1)S(1)}, bf16[128,1024]{1,0:T(8,128)(2,1)S(1)}, u32[]{:S(2)}, u32[]{:S(2)}) collective-permute-start(bf16[128,1024]{1,0:T(8,128)(2,1)S(1)} %renew.1.refs_0_), channel_id=1, source_target_pairs={{0,16},{2,18},{4,20},{6,22},{8,24},{10,26},{12,28},{14,30},{16,0},... | collective-permute-start | bytes 786440 | tf_op jit(solution)/shard_map/ppermute | solution.py:23
  73.3 1.9 %collective-permute-start.26 = (bf16[128,1024]{1,0:T(8,128)(2,1)S(1)}, bf16[128,1024]{1,0:T(8,128)(2,1)S(1)}, u32[]{:S(2)}, u32[]{:S(2)}) collective-permute-start(bf16[128,1024]{1,0:T(8,128)(2,1)S(1)} %collective-permute-done.24.refs_0_), channel_id=1, source_target_pairs={{0,4},{2,6},{4,0},{6,2},{8,12},{10,14},{12,8},{14,10},{16,20},{18,... | collective-permute-start | bytes 786440 | tf_op jit(solution)/shard_map/ppermute | solution.py:23
  75.2 2.8 %collective-permute-done.16.refs_4_ = bf16[128,1024]{1,0:T(8,128)(2,1)S(1)} collective-permute-done((bf16[128,1024]{1,0:T(8,128)(2,1)S(1)}, bf16[128,1024]{1,0:T(8,128)(2,1)S(1)}, u32[]{:S(2)}, u32[]{:S(2)}) %collective-permute-start.16) | collective-permute-done | bytes 262176 | tf_op jit(solution)/shard_map/ppermute | solution.py:23
  81.0 3.3 %collective-permute-done.30.refs_3_ = bf16[128,1024]{1,0:T(8,128)(2,1)S(1)} collective-permute-done((bf16[128,1024]{1,0:T(8,128)(2,1)S(1)}, bf16[128,1024]{1,0:T(8,128)(2,1)S(1)}, u32[]{:S(2)}, u32[]{:S(2)}) %collective-permute-start.30) | collective-permute-done | bytes 262176 | tf_op jit(solution)/shard_map/ppermute | solution.py:23
  94.0 1.9 %shard_map.55 = (f32[8,1024]{1,0:T(8,128)S(1)}, bf16[2048,1024]{1,0:T(8,128)(2,1)}) custom-call(bf16[128,1024]{1,0:T(8,128)(2,1)S(1)} %copy-done.6, bf16[128,1024]{1,0:T(8,128)(2,1)S(1)} %copy-done.10, bf16[128,1024]{1,0:T(8,128)(2,1)S(1)} %copy-done.8, bf16[128,1024]{1,0:T(8,128)(2,1)S(1)} %copy-done.12, bf16[1024,1024]{1,0:T(8,128)(2,1)S(1)} %bitcast.5), custom_call_target="tpu_custom_call" | custom-call | flops 1073741824 | bytes 2097152 | tf_op jit(solution)/shard_map/pallas_call | solution.py:291
  96.9 3.6 %shard_map.56 = (f32[8,1024]{1,0:T(8,128)S(1)}, bf16[2048,1024]{1,0:T(8,128)(2,1)}) custom-call(bf16[128,1024]{1,0:T(8,128)(2,1)S(1)} %collective-permute-done.24.refs_0_, bf16[128,1024]{1,0:T(8,128)(2,1)} %collective-permute-done.25.refs_1_, bf16[128,1024]{1,0:T(8,128)(2,1)S(1)} %copy-done.4, ...), custom_call_target="tpu_custom_call", output_to_operand_aliasing={{1}: (8, {})} | custom-call | flops 1610612736 | bytes 3145728 | tf_op jit(solution)/shard_map/pallas_call | solution.py:291
  100.5 3.1 %shard_map.57 = (f32[8,1024]{1,0:T(8,128)S(1)}, bf16[2048,1024]{1,0:T(8,128)(2,1)}) custom-call(bf16[128,1024]{1,0:T(8,128)(2,1)} %collective-permute-done.22.refs_0_, bf16[128,1024]{1,0:T(8,128)(2,1)} %collective-permute-done.17.refs_1_, bf16[128,1024]{1,0:T(8,128)(2,1)} %collective-permute-done.20.refs_2_, ...), custom_call_target="tpu_custom_call", output_to_operand_aliasing={{1}: (6, {})} | custom-call | flops 1073741824 | bytes 2097152 | tf_op jit(solution)/shard_map/pallas_call | solution.py:291
  (106 shorter events, 32.4 us)
Async XLA Ops:
  4.0 11.4 %collective-permute-start.3 = (bf16[72,1024]{1,0:T(8,128)(2,1)S(1)}, bf16[72,1024]{1,0:T(8,128)(2,1)S(1)}, u32[]{:S(2)}, u32[]{:S(2)}) collective-permute-start(bf16[72,1024]{1,0:T(8,128)(2,1)S(1)} %get-tuple-element.47), channel_id=1, source_target_pairs={{0,6},{2,4},{4,2},{6,0},{8,14},{10,12},{12,10},{14,8},{16,22},{18,... | collective-permute-start | bytes 442376 | tf_op jit(solution)/shard_map/ppermute | solution.py:23
  9.5 12.1 %collective-permute-start.6 = (bf16[72,1024]{1,0:T(8,128)(2,1)S(1)}, bf16[72,1024]{1,0:T(8,128)(2,1)S(1)}, u32[]{:S(2)}, u32[]{:S(2)}) collective-permute-start(bf16[72,1024]{1,0:T(8,128)(2,1)S(1)} %get-tuple-element.50), channel_id=1, source_target_pairs={{0,12},{2,14},{4,8},{6,10},{8,4},{10,6},{12,0},{14,2},{16,28},{18,... | collective-permute-start | bytes 442376 | tf_op jit(solution)/shard_map/ppermute | solution.py:23
  9.5 18.0 %collective-permute-start.7 = (bf16[72,1024]{1,0:T(8,128)(2,1)}, bf16[72,1024]{1,0:T(8,128)(2,1)S(1)}, u32[]{:S(2)}, u32[]{:S(2)}) collective-permute-start(bf16[72,1024]{1,0:T(8,128)(2,1)} %get-tuple-element.51), channel_id=1, source_target_pairs={{0,14},{2,12},{4,10},{6,8},{8,6},{10,4},{12,2},{14,0},{16,30},{18,... | collective-permute-start | bytes 442376 | tf_op jit(solution)/shard_map/ppermute | solution.py:23
  14.9 12.8 %collective-permute-start.1 = (bf16[72,1024]{1,0:T(8,128)(2,1)}, bf16[72,1024]{1,0:T(8,128)(2,1)}, u32[]{:S(2)}, u32[]{:S(2)}) collective-permute-start(bf16[72,1024]{1,0:T(8,128)(2,1)} %get-tuple-element.45), channel_id=1, source_target_pairs={{0,2},{2,0},{4,6},{6,4},{8,10},{10,8},{12,14},{14,12},{16,18},{18,... | collective-permute-start | bytes 442376 | tf_op jit(solution)/shard_map/ppermute | solution.py:23
  15.4 12.3 %collective-permute-start.2 = (bf16[72,1024]{1,0:T(8,128)(2,1)}, bf16[72,1024]{1,0:T(8,128)(2,1)}, u32[]{:S(2)}, u32[]{:S(2)}) collective-permute-start(bf16[72,1024]{1,0:T(8,128)(2,1)} %get-tuple-element.46), channel_id=1, source_target_pairs={{0,4},{2,6},{4,0},{6,2},{8,12},{10,14},{12,8},{14,10},{16,20},{18,... | collective-permute-start | bytes 442376 | tf_op jit(solution)/shard_map/ppermute | solution.py:23
  16.4 14.7 %collective-permute-start.4 = (bf16[72,1024]{1,0:T(8,128)(2,1)}, bf16[72,1024]{1,0:T(8,128)(2,1)}, u32[]{:S(2)}, u32[]{:S(2)}) collective-permute-start(bf16[72,1024]{1,0:T(8,128)(2,1)} %get-tuple-element.48), channel_id=1, source_target_pairs={{0,8},{2,10},{4,12},{6,14},{8,0},{10,2},{12,4},{14,6},{16,24},{18,... | collective-permute-start | bytes 442376 | tf_op jit(solution)/shard_map/ppermute | solution.py:23
  22.3 11.9 %collective-permute-start = (bf16[72,1024]{1,0:T(8,128)(2,1)}, bf16[72,1024]{1,0:T(8,128)(2,1)S(1)}, u32[]{:S(2)}, u32[]{:S(2)}) collective-permute-start(bf16[72,1024]{1,0:T(8,128)(2,1)} %get-tuple-element.40), channel_id=1, source_target_pairs={{0,2},{2,0},{4,6},{6,4},{8,10},{10,8},{12,14},{14,12},{16,18},{18,... | collective-permute-start | bytes 442376 | tf_op jit(solution)/shard_map/ppermute | solution.py:23
  27.5 19.7 %collective-permute-start.10 = (bf16[72,1024]{1,0:T(8,128)(2,1)}, bf16[72,1024]{1,0:T(8,128)(2,1)}, u32[]{:S(2)}, u32[]{:S(2)}) collective-permute-start(bf16[72,1024]{1,0:T(8,128)(2,1)} %copy-done.20), channel_id=1, source_target_pairs={{0,6},{2,4},{4,2},{6,0},{8,14},{10,12},{12,10},{14,8},{16,22},{18,... | collective-permute-start | bytes 442376 | tf_op jit(solution)/shard_map/ppermute | solution.py:23
  27.7 21.1 %collective-permute-start.11 = (bf16[72,1024]{1,0:T(8,128)(2,1)}, bf16[72,1024]{1,0:T(8,128)(2,1)}, u32[]{:S(2)}, u32[]{:S(2)}) collective-permute-start(bf16[72,1024]{1,0:T(8,128)(2,1)} %copy-done.19), channel_id=1, source_target_pairs={{0,8},{2,10},{4,12},{6,14},{8,0},{10,2},{12,4},{14,6},{16,24},{18,... | collective-permute-start | bytes 442376 | tf_op jit(solution)/shard_map/ppermute | solution.py:23
  27.7 23.0 %collective-permute-start.12 = (bf16[72,1024]{1,0:T(8,128)(2,1)}, bf16[72,1024]{1,0:T(8,128)(2,1)}, u32[]{:S(2)}, u32[]{:S(2)}) collective-permute-start(bf16[72,1024]{1,0:T(8,128)(2,1)} %copy-done.18), channel_id=1, source_target_pairs={{0,10},{2,8},{4,14},{6,12},{8,2},{10,0},{12,6},{14,4},{16,26},{18,... | collective-permute-start | bytes 442376 | tf_op jit(solution)/shard_map/ppermute | solution.py:23
  31.1 20.0 %collective-permute-start.13 = (bf16[72,1024]{1,0:T(8,128)(2,1)}, bf16[72,1024]{1,0:T(8,128)(2,1)}, u32[]{:S(2)}, u32[]{:S(2)}) collective-permute-start(bf16[72,1024]{1,0:T(8,128)(2,1)} %copy-done.17), channel_id=1, source_target_pairs={{0,12},{2,14},{4,8},{6,10},{8,4},{10,6},{12,0},{14,2},{16,28},{18,... | collective-permute-start | bytes 442376 | tf_op jit(solution)/shard_map/ppermute | solution.py:23
  34.2 25.6 %collective-permute-start.8 = (f32[128,1024]{1,0:T(8,128)}, f32[128,1024]{1,0:T(8,128)S(1)}, u32[]{:S(2)}, u32[]{:S(2)}) collective-permute-start(f32[128,1024]{1,0:T(8,128)} %get-tuple-element.52), channel_id=1, source_target_pairs={{0,16},{2,18},{4,20},{6,22},{8,24},{10,26},{12,28},{14,30},{16,0},... | collective-permute-start | bytes 1572872 | tf_op jit(solution)/shard_map/ppermute | solution.py:23
  47.2 11.1 %collective-permute-start.14 = (bf16[72,1024]{1,0:T(8,128)(2,1)S(1)}, bf16[72,1024]{1,0:T(8,128)(2,1)S(1)}, u32[]{:S(2)}, u32[]{:S(2)}) collective-permute-start(bf16[72,1024]{1,0:T(8,128)(2,1)S(1)} %copy-done.16), channel_id=1, source_target_pairs={{0,14},{2,12},{4,10},{6,8},{8,6},{10,4},{12,2},{14,0},{16,30},{18,... | collective-permute-start | bytes 442376 | tf_op jit(solution)/shard_map/ppermute | solution.py:23
  60.1 10.8 %collective-permute-start.29 = (bf16[128,1024]{1,0:T(8,128)(2,1)S(1)}, bf16[128,1024]{1,0:T(8,128)(2,1)S(1)}, u32[]{:S(2)}, u32[]{:S(2)}) collective-permute-start(bf16[128,1024]{1,0:T(8,128)(2,1)S(1)} %renew.1.refs_0_), channel_id=1, source_target_pairs={{0,4},{2,6},{4,0},{6,2},{8,12},{10,14},{12,8},{14,10},{16,20},{18,... | collective-permute-start | bytes 786440 | tf_op jit(solution)/shard_map/ppermute | solution.py:23
  61.2 11.4 %collective-permute-start.28 = (bf16[128,1024]{1,0:T(8,128)(2,1)S(1)}, bf16[128,1024]{1,0:T(8,128)(2,1)S(1)}, u32[]{:S(2)}, u32[]{:S(2)}) collective-permute-start(bf16[128,1024]{1,0:T(8,128)(2,1)S(1)} %renew.1.refs_0_), channel_id=1, source_target_pairs={{0,2},{2,0},{4,6},{6,4},{8,10},{10,8},{12,14},{14,12},{16,18},{18,... | collective-permute-start | bytes 786440 | tf_op jit(solution)/shard_map/ppermute | solution.py:23
  64.6 13.4 %collective-permute-start.16 = (bf16[128,1024]{1,0:T(8,128)(2,1)S(1)}, bf16[128,1024]{1,0:T(8,128)(2,1)S(1)}, u32[]{:S(2)}, u32[]{:S(2)}) collective-permute-start(bf16[128,1024]{1,0:T(8,128)(2,1)S(1)} %renew.1.refs_0_), channel_id=1, source_target_pairs={{0,16},{2,18},{4,20},{6,22},{8,24},{10,26},{12,28},{14,30},{16,0},... | collective-permute-start | bytes 786440 | tf_op jit(solution)/shard_map/ppermute | solution.py:23
  70.9 13.5 %collective-permute-start.30 = (bf16[128,1024]{1,0:T(8,128)(2,1)S(1)}, bf16[128,1024]{1,0:T(8,128)(2,1)S(1)}, u32[]{:S(2)}, u32[]{:S(2)}) collective-permute-start(bf16[128,1024]{1,0:T(8,128)(2,1)S(1)} %collective-permute-done.29.refs_2_), channel_id=1, source_target_pairs={{0,2},{2,0},{4,6},{6,4},{8,10},{10,8},{12,14},{14,12},{16,18},{18,... | collective-permute-start | bytes 786440 | tf_op jit(solution)/shard_map/ppermute | solution.py:23
  73.3 13.1 %collective-permute-start.26 = (bf16[128,1024]{1,0:T(8,128)(2,1)S(1)}, bf16[128,1024]{1,0:T(8,128)(2,1)S(1)}, u32[]{:S(2)}, u32[]{:S(2)}) collective-permute-start(bf16[128,1024]{1,0:T(8,128)(2,1)S(1)} %collective-permute-done.24.refs_0_), channel_id=1, source_target_pairs={{0,4},{2,6},{4,0},{6,2},{8,12},{10,14},{12,8},{14,10},{16,20},{18,... | collective-permute-start | bytes 786440 | tf_op jit(solution)/shard_map/ppermute | solution.py:23
  78.5 10.8 %collective-permute-start.20 = (bf16[128,1024]{1,0:T(8,128)(2,1)S(1)}, bf16[128,1024]{1,0:T(8,128)(2,1)}, u32[]{:S(2)}, u32[]{:S(2)}) collective-permute-start(bf16[128,1024]{1,0:T(8,128)(2,1)S(1)} %collective-permute-done.19.refs_5_), channel_id=1, source_target_pairs={{0,2},{2,0},{4,6},{6,4},{8,10},{10,8},{12,14},{14,12},{16,18},{18,... | collective-permute-start | bytes 786440 | tf_op jit(solution)/shard_map/ppermute | solution.py:23
  80.0 15.9 %collective-permute-start.27 = (bf16[128,1024]{1,0:T(8,128)(2,1)}, bf16[128,1024]{1,0:T(8,128)(2,1)}, u32[]{:S(2)}, u32[]{:S(2)}) collective-permute-start(bf16[128,1024]{1,0:T(8,128)(2,1)} %collective-permute-done.25.refs_1_), channel_id=1, source_target_pairs={{0,4},{2,6},{4,0},{6,2},{8,12},{10,14},{12,8},{14,10},{16,20},{18,... | collective-permute-start | bytes 786440 | tf_op jit(solution)/shard_map/ppermute | solution.py:23
  85.1 15.4 %collective-permute-start.22 = (bf16[128,1024]{1,0:T(8,128)(2,1)S(1)}, bf16[128,1024]{1,0:T(8,128)(2,1)}, u32[]{:S(2)}, u32[]{:S(2)}) collective-permute-start(bf16[128,1024]{1,0:T(8,128)(2,1)S(1)} %collective-permute-done.16.refs_4_), channel_id=1, source_target_pairs={{0,2},{2,0},{4,6},{6,4},{8,10},{10,8},{12,14},{14,12},{16,18},{18,... | collective-permute-start | bytes 786440 | tf_op jit(solution)/shard_map/ppermute | solution.py:23
  87.1 13.4 %collective-permute-start.23 = (bf16[128,1024]{1,0:T(8,128)(2,1)S(1)}, bf16[128,1024]{1,0:T(8,128)(2,1)}, u32[]{:S(2)}, u32[]{:S(2)}) collective-permute-start(bf16[128,1024]{1,0:T(8,128)(2,1)S(1)} %collective-permute-done.19.refs_5_), channel_id=1, source_target_pairs={{0,4},{2,6},{4,0},{6,2},{8,12},{10,14},{12,8},{14,10},{16,20},{18,... | collective-permute-start | bytes 786440 | tf_op jit(solution)/shard_map/ppermute | solution.py:23
  88.2 15.4 %collective-permute-start.18 = (bf16[128,1024]{1,0:T(8,128)(2,1)}, bf16[128,1024]{1,0:T(8,128)(2,1)S(1)}, u32[]{:S(2)}, u32[]{:S(2)}) collective-permute-start(bf16[128,1024]{1,0:T(8,128)(2,1)} %collective-permute-done.17.refs_1_), channel_id=1, source_target_pairs={{0,2},{2,0},{4,6},{6,4},{8,10},{10,8},{12,14},{14,12},{16,18},{18,... | collective-permute-start | bytes 786440 | tf_op jit(solution)/shard_map/ppermute | solution.py:23
  89.3 14.3 %collective-permute-start.21 = (bf16[128,1024]{1,0:T(8,128)(2,1)}, bf16[128,1024]{1,0:T(8,128)(2,1)S(1)}, u32[]{:S(2)}, u32[]{:S(2)}) collective-permute-start(bf16[128,1024]{1,0:T(8,128)(2,1)} %collective-permute-done.20.refs_2_), channel_id=1, source_target_pairs={{0,4},{2,6},{4,0},{6,2},{8,12},{10,14},{12,8},{14,10},{16,20},{18,... | collective-permute-start | bytes 786440 | tf_op jit(solution)/shard_map/ppermute | solution.py:23
  (31 other events, 204.3 us)

commit v5 on v4

--- a/solution.py
+++ b/solution.py
@@ -317,7 +317,10 @@
     far = place(far_rank, far_label, points, capacity, powers)
     far |= place(far_rank, far_label, points, capacity, others)
     far = [far[0]] + [swap(far[m], m) for m in range(1, half)]
-    near = place(near_rank, near_label, points, capacity, range(half))
+    early = [7, 6, 5] if half == 8 else [half - 1]
+    rest = [m for m in range(half) if m not in early]
+    near = place(near_rank, near_label, points, capacity, early)
+    near |= place(near_rank, near_label, points, capacity, rest)
     near = [near[0]] + [swap(near[m], m) for m in range(1, half)]
     far_sums, far_counts = add_up(far, share, capacity)
     near[1], late = lax.optimization_barrier((near[1], points))

time: 107 us -> 110 us (1.028)
  waiting for transfers between devices: 13.7 us -> 18.4 us
  Pallas kernels: 27.8 us -> 25.7 us
    ppermute x32, waiting for transfers between devices: 13.7 us -> 18.4 us  [swap(): return lax.ppermute(value, axis, [(i, i ^ mask) for i in range(size)])]
    pallas_call x3, Pallas kernels: 8.63 us -> 6.42 us  [arrive(): pl.pallas_call(functools.partial(arrive_kernel, share, places, fresh), ou...]
    pallas_call x3 -> x4, Pallas kernels: 5.56 us -> 5.81 us  [place(): pl.pallas_call(functools.partial(place_kernel, masks, capacity), out_shap...]
    unnamed x46 -> x38, local copies, waits for them, and re-layouts: 11.6 us -> 11.5 us
  transfers between devices with their start and end apart: 32 -> 32, of which waited for: 4 -> 6; matrix products, arithmetic and copies ran while one was open for 4% -> 4% of each run, Pallas kernels for 23% -> 21%
where the time goes in v5:
time: 110 us; the launch traced here: 108 us
  starting transfers between devices  47.2 us (43%)
  Pallas kernels  25.7 us (23%)
  waiting for transfers between devices  18.4 us (17%)
  local copies, waits for them, and re-layouts  15 us (14%)
  other arithmetic  1.13 us (1%)
    ppermute x32, starting transfers between devices, swap(): return lax.ppermute(value, axis, [(i, i ^ mask) for i in range(size)])  47.2 us
    ppermute x32, waiting for transfers between devices, swap(): return lax.ppermute(value, axis, [(i, i ^ mask) for i in range(size)])  18.4 us
    unnamed x38, local copies, waits for them, and re-layouts  11.5 us
    pallas_call x1, Pallas kernels, first_lowest(): pl.pallas_call(first_kernel, grid=(count // step,), out_shape=out, in_spe...  7.73 us
    pallas_call x3, Pallas kernels, arrive(): pl.pallas_call(functools.partial(arrive_kernel, share, places, fresh), ou...  6.42 us
    pallas_call x4, Pallas kernels, place(): pl.pallas_call(functools.partial(place_kernel, masks, capacity), out_shap...  5.81 us
    pallas_call x2, Pallas kernels, add_up(): pl.pallas_call(functools.partial(sum_kernel, share, capacity), out_shape=...  3.69 us
    optimization_barrier x1, local copies, waits for them, and re-layouts, halves(): near[1], late = lax.optimization_barrier((near[1], points))  2.56 us
  transfers between devices with their start and end apart: 32, of which 6 were waited for; matrix products, arithmetic and copies ran while one was open for 4% of the time, Pallas kernels for 21%

profile of v5, /device:TPU:0, one launch (start us, length us, event | category | flops | bytes accessed | tf_op | source)
XLA Modules:
  0.0 108.4 jit_solution(2719208333548262630)
XLA Ops:
  2.2 1.8 %shard_map.51 = (bf16[72,1024]{1,0:T(8,128)(2,1)S(1)}, bf16[72,1024]{1,0:T(8,128)(2,1)S(1)}, bf16[72,1024]{1,0:T(8,128)(2,1)S(1)}, bf16[72,1024]{1,0:T(8,128)(2,1)S(1)}, bf16[72,1024]{1,0:T(8,128)(2,1)}) custom-call(f32[8,1024]{1,0:T(8,128)S(1)} %get-tuple-element.42.rank_ref, bf16[1024,8]{1,0:T(8,128)(2,1)S(1)} %get-tuple-element.43.label_ref, ...), custom_call_target="tpu_custom_call" | custom-call | flops 671088640 | bytes 4194304 | tf_op jit(solution)/shard_map/pallas_call | solution.py:112
  4.0 3.9 %collective-permute-start.3 = (bf16[72,1024]{1,0:T(8,128)(2,1)S(1)}, bf16[72,1024]{1,0:T(8,128)(2,1)S(1)}, u32[]{:S(2)}, u32[]{:S(2)}) collective-permute-start(bf16[72,1024]{1,0:T(8,128)(2,1)S(1)} %get-tuple-element.47), channel_id=1, source_target_pairs={{0,6},{2,4},{4,2},{6,0},{8,14},{10,12},{12,10},{14,8},{16,22},{18,... | collective-permute-start | bytes 442376 | tf_op jit(solution)/shard_map/ppermute | solution.py:23
  8.0 1.5 %collective-permute-start.5 = (bf16[72,1024]{1,0:T(8,128)(2,1)S(1)}, bf16[72,1024]{1,0:T(8,128)(2,1)S(1)}, u32[]{:S(2)}, u32[]{:S(2)}) collective-permute-start(bf16[72,1024]{1,0:T(8,128)(2,1)S(1)} %get-tuple-element.49), channel_id=1, source_target_pairs={{0,10},{2,8},{4,14},{6,12},{8,2},{10,0},{12,6},{14,4},{16,26},{18,... | collective-permute-start | bytes 442376 | tf_op jit(solution)/shard_map/ppermute | solution.py:23
  9.5 3.8 %collective-permute-start.7 = (bf16[72,1024]{1,0:T(8,128)(2,1)}, bf16[72,1024]{1,0:T(8,128)(2,1)S(1)}, u32[]{:S(2)}, u32[]{:S(2)}) collective-permute-start(bf16[72,1024]{1,0:T(8,128)(2,1)} %get-tuple-element.51), channel_id=1, source_target_pairs={{0,14},{2,12},{4,10},{6,8},{8,6},{10,4},{12,2},{14,0},{16,30},{18,... | collective-permute-start | bytes 442376 | tf_op jit(solution)/shard_map/ppermute | solution.py:23
  15.4 1.7 %shard_map.50 = (bf16[72,1024]{1,0:T(8,128)(2,1)S(1)}, bf16[72,1024]{1,0:T(8,128)(2,1)}, bf16[72,1024]{1,0:T(8,128)(2,1)S(1)}, bf16[72,1024]{1,0:T(8,128)(2,1)S(1)}, bf16[72,1024]{1,0:T(8,128)(2,1)S(1)}) custom-call(f32[8,1024]{1,0:T(8,128)S(1)} %get-tuple-element.38.rank_ref, bf16[1024,8]{1,0:T(8,128)(2,1)S(1)} %get-tuple-element.39.label_ref, ...), custom_call_target="tpu_custom_call" | custom-call | flops 671088640 | bytes 4194304 | tf_op jit(solution)/shard_map/pallas_call | solution.py:112
  18.0 4.3 %collective-permute-start = (bf16[72,1024]{1,0:T(8,128)(2,1)}, bf16[72,1024]{1,0:T(8,128)(2,1)S(1)}, u32[]{:S(2)}, u32[]{:S(2)}) collective-permute-start(bf16[72,1024]{1,0:T(8,128)(2,1)} %get-tuple-element.40), channel_id=1, source_target_pairs={{0,2},{2,0},{4,6},{6,4},{8,10},{10,8},{12,14},{14,12},{16,18},{18,... | collective-permute-start | bytes 442376 | tf_op jit(solution)/shard_map/ppermute | solution.py:23
  27.7 3.4 %collective-permute-start.12 = (bf16[72,1024]{1,0:T(8,128)(2,1)}, bf16[72,1024]{1,0:T(8,128)(2,1)}, u32[]{:S(2)}, u32[]{:S(2)}) collective-permute-start(bf16[72,1024]{1,0:T(8,128)(2,1)} %copy-done.16), channel_id=1, source_target_pairs={{0,10},{2,8},{4,14},{6,12},{8,2},{10,0},{12,6},{14,4},{16,26},{18,... | collective-permute-start | bytes 442376 | tf_op jit(solution)/shard_map/ppermute | solution.py:23
  31.1 2.2 %shard_map.53 = (f32[128,1024]{1,0:T(8,128)}, f32[8,128]{1,0:T(8,128)S(1)}) custom-call(bf16[72,1024]{1,0:T(8,128)(2,1)S(1)} %get-tuple-element.44.refs_0_, bf16[72,1024]{1,0:T(8,128)(2,1)} %collective-permute-done.1.refs_1_, bf16[72,1024]{1,0:T(8,128)(2,1)} %collective-permute-done.2.refs_2_, bf16[72,1024]{1,0:T(8,128)(2,1)S(1)} %collective-permute-done.3.refs_3_, ...), custom_call_target="tpu_custom_call" | custom-call | flops 134217728 | bytes 1572864 | tf_op jit(solution)/shard_map/pallas_call | solution.py:139
  33.3 2.6 %collective-permute-start.8 = (f32[128,1024]{1,0:T(8,128)}, f32[128,1024]{1,0:T(8,128)S(1)}, u32[]{:S(2)}, u32[]{:S(2)}) collective-permute-start(f32[128,1024]{1,0:T(8,128)} %get-tuple-element.52), channel_id=1, source_target_pairs={{0,16},{2,18},{4,20},{6,22},{8,24},{10,26},{12,28},{14,30},{16,0},... | collective-permute-start | bytes 1572872 | tf_op jit(solution)/shard_map/ppermute | solution.py:23
  35.9 2.6 %copy.8 = bf16[1024,1024]{0,1:T(8,128)(2,1)} copy(bf16[1024,1024]{1,0:T(8,128)(2,1)S(1)} %copy-done) | data formatting | bytes 4194304 | tf_op jit(solution)/shard_map/optimization_barrier | solution.py:326
  38.4 7.7 %first_lowest.1 = f32[8,1024]{1,0:T(8,128)} custom-call(bf16[2048,1024]{1,0:T(8,128)(2,1)} %cents_ref.1, bf16[1024,1024]{1,0:T(8,128)(2,1)} %bitcast.4), custom_call_target="tpu_custom_call" | custom-call | flops 4294967296 | bytes 4194304 | tf_op jit(solution)/shard_map/first_lowest/pallas_call | solution.py:190
  46.6 2.0 %collective-permute-start.14 = (bf16[72,1024]{1,0:T(8,128)(2,1)S(1)}, bf16[72,1024]{1,0:T(8,128)(2,1)S(1)}, u32[]{:S(2)}, u32[]{:S(2)}) collective-permute-start(bf16[72,1024]{1,0:T(8,128)(2,1)S(1)} %copy-done.12), channel_id=1, source_target_pairs={{0,14},{2,12},{4,10},{6,8},{8,6},{10,4},{12,2},{14,0},{16,30},{18,... | collective-permute-start | bytes 442376 | tf_op jit(solution)/shard_map/ppermute | solution.py:23
  49.5 7.1 %collective-permute-done.13.refs_6_ = bf16[72,1024]{1,0:T(8,128)(2,1)S(1)} collective-permute-done((bf16[72,1024]{1,0:T(8,128)(2,1)S(1)}, bf16[72,1024]{1,0:T(8,128)(2,1)S(1)}, u32[]{:S(2)}, u32[]{:S(2)}) %collective-permute-start.13) | collective-permute-done | bytes 147488 | tf_op jit(solution)/shard_map/ppermute | solution.py:23
  56.6 1.6 %collective-permute-done.14.refs_7_ = bf16[72,1024]{1,0:T(8,128)(2,1)S(1)} collective-permute-done((bf16[72,1024]{1,0:T(8,128)(2,1)S(1)}, bf16[72,1024]{1,0:T(8,128)(2,1)S(1)}, u32[]{:S(2)}, u32[]{:S(2)}) %collective-permute-start.14) | collective-permute-done | bytes 147488 | tf_op jit(solution)/shard_map/ppermute | solution.py:23
  62.7 5.3 %collective-permute-start.16 = (bf16[128,1024]{1,0:T(8,128)(2,1)S(1)}, bf16[128,1024]{1,0:T(8,128)(2,1)S(1)}, u32[]{:S(2)}, u32[]{:S(2)}) collective-permute-start(bf16[128,1024]{1,0:T(8,128)(2,1)S(1)} %renew.1.refs_0_), channel_id=1, source_target_pairs={{0,16},{2,18},{4,20},{6,22},{8,24},{10,26},{12,28},{14,30},{16,0},... | collective-permute-start | bytes 786440 | tf_op jit(solution)/shard_map/ppermute | solution.py:23
  71.5 4.5 %collective-permute-start.26 = (bf16[128,1024]{1,0:T(8,128)(2,1)S(1)}, bf16[128,1024]{1,0:T(8,128)(2,1)S(1)}, u32[]{:S(2)}, u32[]{:S(2)}) collective-permute-start(bf16[128,1024]{1,0:T(8,128)(2,1)S(1)} %collective-permute-done.24.refs_0_), channel_id=1, source_target_pairs={{0,4},{2,6},{4,0},{6,2},{8,12},{10,14},{12,8},{14,10},{16,20},{18,... | collective-permute-start | bytes 786440 | tf_op jit(solution)/shard_map/ppermute | solution.py:23
  75.9 6.1 %collective-permute-done.16.refs_4_ = bf16[128,1024]{1,0:T(8,128)(2,1)S(1)} collective-permute-done((bf16[128,1024]{1,0:T(8,128)(2,1)S(1)}, bf16[128,1024]{1,0:T(8,128)(2,1)S(1)}, u32[]{:S(2)}, u32[]{:S(2)}) %collective-permute-start.16) | collective-permute-done | bytes 262176 | tf_op jit(solution)/shard_map/ppermute | solution.py:23
  83.6 1.6 %collective-permute-start.27 = (bf16[128,1024]{1,0:T(8,128)(2,1)S(1)}, bf16[128,1024]{1,0:T(8,128)(2,1)S(1)}, u32[]{:S(2)}, u32[]{:S(2)}) collective-permute-start(bf16[128,1024]{1,0:T(8,128)(2,1)S(1)} %collective-permute-done.25.refs_1_), channel_id=1, source_target_pairs={{0,4},{2,6},{4,0},{6,2},{8,12},{10,14},{12,8},{14,10},{16,20},{18,... | collective-permute-start | bytes 786440 | tf_op jit(solution)/shard_map/ppermute | solution.py:23
  88.3 2.9 %collective-permute-done.17.refs_1_ = bf16[128,1024]{1,0:T(8,128)(2,1)S(1)} collective-permute-done((bf16[128,1024]{1,0:T(8,128)(2,1)S(1)}, bf16[128,1024]{1,0:T(8,128)(2,1)S(1)}, u32[]{:S(2)}, u32[]{:S(2)}) %collective-permute-start.17) | collective-permute-done | bytes 262176 | tf_op jit(solution)/shard_map/ppermute | solution.py:23
  93.2 1.6 %copy-done.1 = bf16[1024,1024]{0,1:T(8,128)(2,1)S(1)} copy-done((bf16[1024,1024]{0,1:T(8,128)(2,1)S(1)}, bf16[1024,1024]{0,1:T(8,128)(2,1)}, u32[]{:S(2)}) %copy-start.1) | copy-done | bytes 2097176
  97.7 1.9 %shard_map.56 = (f32[8,1024]{1,0:T(8,128)S(1)}, bf16[2048,1024]{1,0:T(8,128)(2,1)}) custom-call(bf16[128,1024]{1,0:T(8,128)(2,1)S(1)} %renew.1.refs_0_, bf16[128,1024]{1,0:T(8,128)(2,1)S(1)} %copy-done.6, bf16[128,1024]{1,0:T(8,128)(2,1)S(1)} %copy-done.4, bf16[128,1024]{1,0:T(8,128)(2,1)S(1)} %copy-done.8, bf16[1024,1024]{1,0:T(8,128)(2,1)S(1)} %bitcast.5), custom_call_target="tpu_custom_call" | custom-call | flops 1073741824 | bytes 2097152 | tf_op jit(solution)/shard_map/pallas_call | solution.py:291
  99.6 1.6 %copy-done.2 = bf16[1024,1024]{0,1:T(8,128)(2,1)S(1)} copy-done((bf16[1024,1024]{0,1:T(8,128)(2,1)S(1)}, bf16[1024,1024]{0,1:T(8,128)(2,1)}, u32[]{:S(2)}) %copy-start.2) | copy-done | bytes 2097176
  101.2 2.6 %shard_map.57 = (f32[8,1024]{1,0:T(8,128)S(1)}, bf16[2048,1024]{1,0:T(8,128)(2,1)}) custom-call(bf16[128,1024]{1,0:T(8,128)(2,1)S(1)} %collective-permute-done.24.refs_0_, bf16[128,1024]{1,0:T(8,128)(2,1)S(1)} %collective-permute-done.25.refs_1_, bf16[128,1024]{1,0:T(8,128)(2,1)S(1)} %collective-permute-done.26.refs_2_, ...), custom_call_target="tpu_custom_call", output_to_operand_aliasing={{1}: (8, {})} | custom-call | flops 1610612736 | bytes 3145728 | tf_op jit(solution)/shard_map/pallas_call | solution.py:291
  103.8 1.9 %shard_map.58 = (f32[8,1024]{1,0:T(8,128)S(1)}, bf16[2048,1024]{1,0:T(8,128)(2,1)}) custom-call(bf16[128,1024]{1,0:T(8,128)(2,1)S(1)} %collective-permute-done.22.refs_0_, bf16[128,1024]{1,0:T(8,128)(2,1)S(1)} %collective-permute-done.17.refs_1_, bf16[128,1024]{1,0:T(8,128)(2,1)S(1)} %collective-permute-done.20.refs_2_, ...), custom_call_target="tpu_custom_call", output_to_operand_aliasing={{1}: (6, {})} | custom-call | flops 1073741824 | bytes 2097152 | tf_op jit(solution)/shard_map/pallas_call | solution.py:291
  (99 shorter events, 31.2 us)
Async XLA Ops:
  4.0 13.1 %collective-permute-start.3 = (bf16[72,1024]{1,0:T(8,128)(2,1)S(1)}, bf16[72,1024]{1,0:T(8,128)(2,1)S(1)}, u32[]{:S(2)}, u32[]{:S(2)}) collective-permute-start(bf16[72,1024]{1,0:T(8,128)(2,1)S(1)} %get-tuple-element.47), channel_id=1, source_target_pairs={{0,6},{2,4},{4,2},{6,0},{8,14},{10,12},{12,10},{14,8},{16,22},{18,... | collective-permute-start | bytes 442376 | tf_op jit(solution)/shard_map/ppermute | solution.py:23
  8.0 9.8 %collective-permute-start.5 = (bf16[72,1024]{1,0:T(8,128)(2,1)S(1)}, bf16[72,1024]{1,0:T(8,128)(2,1)S(1)}, u32[]{:S(2)}, u32[]{:S(2)}) collective-permute-start(bf16[72,1024]{1,0:T(8,128)(2,1)S(1)} %get-tuple-element.49), channel_id=1, source_target_pairs={{0,10},{2,8},{4,14},{6,12},{8,2},{10,0},{12,6},{14,4},{16,26},{18,... | collective-permute-start | bytes 442376 | tf_op jit(solution)/shard_map/ppermute | solution.py:23
  9.5 16.5 %collective-permute-start.7 = (bf16[72,1024]{1,0:T(8,128)(2,1)}, bf16[72,1024]{1,0:T(8,128)(2,1)S(1)}, u32[]{:S(2)}, u32[]{:S(2)}) collective-permute-start(bf16[72,1024]{1,0:T(8,128)(2,1)} %get-tuple-element.51), channel_id=1, source_target_pairs={{0,14},{2,12},{4,10},{6,8},{8,6},{10,4},{12,2},{14,0},{16,30},{18,... | collective-permute-start | bytes 442376 | tf_op jit(solution)/shard_map/ppermute | solution.py:23
  14.9 11.3 %collective-permute-start.1 = (bf16[72,1024]{1,0:T(8,128)(2,1)}, bf16[72,1024]{1,0:T(8,128)(2,1)}, u32[]{:S(2)}, u32[]{:S(2)}) collective-permute-start(bf16[72,1024]{1,0:T(8,128)(2,1)} %get-tuple-element.45), channel_id=1, source_target_pairs={{0,2},{2,0},{4,6},{6,4},{8,10},{10,8},{12,14},{14,12},{16,18},{18,... | collective-permute-start | bytes 442376 | tf_op jit(solution)/shard_map/ppermute | solution.py:23
  17.7 9.9 %collective-permute-start.4 = (bf16[72,1024]{1,0:T(8,128)(2,1)}, bf16[72,1024]{1,0:T(8,128)(2,1)}, u32[]{:S(2)}, u32[]{:S(2)}) collective-permute-start(bf16[72,1024]{1,0:T(8,128)(2,1)} %get-tuple-element.48), channel_id=1, source_target_pairs={{0,8},{2,10},{4,12},{6,14},{8,0},{10,2},{12,4},{14,6},{16,24},{18,... | collective-permute-start | bytes 442376 | tf_op jit(solution)/shard_map/ppermute | solution.py:23
  18.0 15.2 %collective-permute-start = (bf16[72,1024]{1,0:T(8,128)(2,1)}, bf16[72,1024]{1,0:T(8,128)(2,1)S(1)}, u32[]{:S(2)}, u32[]{:S(2)}) collective-permute-start(bf16[72,1024]{1,0:T(8,128)(2,1)} %get-tuple-element.40), channel_id=1, source_target_pairs={{0,2},{2,0},{4,6},{6,4},{8,10},{10,8},{12,14},{14,12},{16,18},{18,... | collective-permute-start | bytes 442376 | tf_op jit(solution)/shard_map/ppermute | solution.py:23
  26.0 20.1 %collective-permute-start.10 = (bf16[72,1024]{1,0:T(8,128)(2,1)}, bf16[72,1024]{1,0:T(8,128)(2,1)}, u32[]{:S(2)}, u32[]{:S(2)}) collective-permute-start(bf16[72,1024]{1,0:T(8,128)(2,1)} %copy-done.13), channel_id=1, source_target_pairs={{0,6},{2,4},{4,2},{6,0},{8,14},{10,12},{12,10},{14,8},{16,22},{18,... | collective-permute-start | bytes 442376 | tf_op jit(solution)/shard_map/ppermute | solution.py:23
  26.1 20.5 %collective-permute-start.11 = (bf16[72,1024]{1,0:T(8,128)(2,1)}, bf16[72,1024]{1,0:T(8,128)(2,1)}, u32[]{:S(2)}, u32[]{:S(2)}) collective-permute-start(bf16[72,1024]{1,0:T(8,128)(2,1)} %copy-done.10), channel_id=1, source_target_pairs={{0,8},{2,10},{4,12},{6,14},{8,0},{10,2},{12,4},{14,6},{16,24},{18,... | collective-permute-start | bytes 442376 | tf_op jit(solution)/shard_map/ppermute | solution.py:23
  26.6 22.5 %collective-permute-start.9 = (bf16[72,1024]{1,0:T(8,128)(2,1)}, bf16[72,1024]{1,0:T(8,128)(2,1)}, u32[]{:S(2)}, u32[]{:S(2)}) collective-permute-start(bf16[72,1024]{1,0:T(8,128)(2,1)} %copy-done.9), channel_id=1, source_target_pairs={{0,4},{2,6},{4,0},{6,2},{8,12},{10,14},{12,8},{14,10},{16,20},{18,... | collective-permute-start | bytes 442376 | tf_op jit(solution)/shard_map/ppermute | solution.py:23
  27.7 21.9 %collective-permute-start.12 = (bf16[72,1024]{1,0:T(8,128)(2,1)}, bf16[72,1024]{1,0:T(8,128)(2,1)}, u32[]{:S(2)}, u32[]{:S(2)}) collective-permute-start(bf16[72,1024]{1,0:T(8,128)(2,1)} %copy-done.16), channel_id=1, source_target_pairs={{0,10},{2,8},{4,14},{6,12},{8,2},{10,0},{12,6},{14,4},{16,26},{18,... | collective-permute-start | bytes 442376 | tf_op jit(solution)/shard_map/ppermute | solution.py:23
  33.3 26.4 %collective-permute-start.8 = (f32[128,1024]{1,0:T(8,128)}, f32[128,1024]{1,0:T(8,128)S(1)}, u32[]{:S(2)}, u32[]{:S(2)}) collective-permute-start(f32[128,1024]{1,0:T(8,128)} %get-tuple-element.52), channel_id=1, source_target_pairs={{0,16},{2,18},{4,20},{6,22},{8,24},{10,26},{12,28},{14,30},{16,0},... | collective-permute-start | bytes 1572872 | tf_op jit(solution)/shard_map/ppermute | solution.py:23
  46.2 10.4 %collective-permute-start.13 = (bf16[72,1024]{1,0:T(8,128)(2,1)S(1)}, bf16[72,1024]{1,0:T(8,128)(2,1)S(1)}, u32[]{:S(2)}, u32[]{:S(2)}) collective-permute-start(bf16[72,1024]{1,0:T(8,128)(2,1)S(1)} %copy-done.15), channel_id=1, source_target_pairs={{0,12},{2,14},{4,8},{6,10},{8,4},{10,6},{12,0},{14,2},{16,28},{18,... | collective-permute-start | bytes 442376 | tf_op jit(solution)/shard_map/ppermute | solution.py:23
  46.6 11.6 %collective-permute-start.14 = (bf16[72,1024]{1,0:T(8,128)(2,1)S(1)}, bf16[72,1024]{1,0:T(8,128)(2,1)S(1)}, u32[]{:S(2)}, u32[]{:S(2)}) collective-permute-start(bf16[72,1024]{1,0:T(8,128)(2,1)S(1)} %copy-done.12), channel_id=1, source_target_pairs={{0,14},{2,12},{4,10},{6,8},{8,6},{10,4},{12,2},{14,0},{16,30},{18,... | collective-permute-start | bytes 442376 | tf_op jit(solution)/shard_map/ppermute | solution.py:23
  49.1 10.6 %collective-permute-start.15 = (f32[8,128]{1,0:T(8,128)S(1)}, f32[8,128]{1,0:T(8,128)S(1)}, u32[]{:S(2)}, u32[]{:S(2)}) collective-permute-start(f32[8,128]{1,0:T(8,128)S(1)} %get-tuple-element.66), channel_id=1, source_target_pairs={{0,16},{2,18},{4,20},{6,22},{8,24},{10,26},{12,28},{14,30},{16,0},... | collective-permute-start | bytes 12296 | tf_op jit(solution)/shard_map/ppermute | solution.py:23
  62.7 19.4 %collective-permute-start.16 = (bf16[128,1024]{1,0:T(8,128)(2,1)S(1)}, bf16[128,1024]{1,0:T(8,128)(2,1)S(1)}, u32[]{:S(2)}, u32[]{:S(2)}) collective-permute-start(bf16[128,1024]{1,0:T(8,128)(2,1)S(1)} %renew.1.refs_0_), channel_id=1, source_target_pairs={{0,16},{2,18},{4,20},{6,22},{8,24},{10,26},{12,28},{14,30},{16,0},... | collective-permute-start | bytes 786440 | tf_op jit(solution)/shard_map/ppermute | solution.py:23
  68.0 15.5 %collective-permute-start.19 = (bf16[128,1024]{1,0:T(8,128)(2,1)S(1)}, bf16[128,1024]{1,0:T(8,128)(2,1)S(1)}, u32[]{:S(2)}, u32[]{:S(2)}) collective-permute-start(bf16[128,1024]{1,0:T(8,128)(2,1)S(1)} %renew.1.refs_0_), channel_id=1, source_target_pairs={{0,24},{2,26},{4,28},{6,30},{8,16},{10,18},{12,20},{14,22},{16,8},... | collective-permute-start | bytes 786440 | tf_op jit(solution)/shard_map/ppermute | solution.py:23
  68.0 15.6 %collective-permute-start.25 = (bf16[128,1024]{1,0:T(8,128)(2,1)S(1)}, bf16[128,1024]{1,0:T(8,128)(2,1)S(1)}, u32[]{:S(2)}, u32[]{:S(2)}) collective-permute-start(bf16[128,1024]{1,0:T(8,128)(2,1)S(1)} %collective-permute-done.24.refs_0_), channel_id=1, source_target_pairs={{0,2},{2,0},{4,6},{6,4},{8,10},{10,8},{12,14},{14,12},{16,18},{18,... | collective-permute-start | bytes 786440 | tf_op jit(solution)/shard_map/ppermute | solution.py:23
  69.1 16.1 %collective-permute-start.30 = (bf16[128,1024]{1,0:T(8,128)(2,1)S(1)}, bf16[128,1024]{1,0:T(8,128)(2,1)S(1)}, u32[]{:S(2)}, u32[]{:S(2)}) collective-permute-start(bf16[128,1024]{1,0:T(8,128)(2,1)S(1)} %collective-permute-done.29.refs_2_), channel_id=1, source_target_pairs={{0,2},{2,0},{4,6},{6,4},{8,10},{10,8},{12,14},{14,12},{16,18},{18,... | collective-permute-start | bytes 786440 | tf_op jit(solution)/shard_map/ppermute | solution.py:23
  71.5 15.3 %collective-permute-start.26 = (bf16[128,1024]{1,0:T(8,128)(2,1)S(1)}, bf16[128,1024]{1,0:T(8,128)(2,1)S(1)}, u32[]{:S(2)}, u32[]{:S(2)}) collective-permute-start(bf16[128,1024]{1,0:T(8,128)(2,1)S(1)} %collective-permute-done.24.refs_0_), channel_id=1, source_target_pairs={{0,4},{2,6},{4,0},{6,2},{8,12},{10,14},{12,8},{14,10},{16,20},{18,... | collective-permute-start | bytes 786440 | tf_op jit(solution)/shard_map/ppermute | solution.py:23
  83.6 16.0 %collective-permute-start.27 = (bf16[128,1024]{1,0:T(8,128)(2,1)S(1)}, bf16[128,1024]{1,0:T(8,128)(2,1)S(1)}, u32[]{:S(2)}, u32[]{:S(2)}) collective-permute-start(bf16[128,1024]{1,0:T(8,128)(2,1)S(1)} %collective-permute-done.25.refs_1_), channel_id=1, source_target_pairs={{0,4},{2,6},{4,0},{6,2},{8,12},{10,14},{12,8},{14,10},{16,20},{18,... | collective-permute-start | bytes 786440 | tf_op jit(solution)/shard_map/ppermute | solution.py:23
  85.9 17.9 %collective-permute-start.22 = (bf16[128,1024]{1,0:T(8,128)(2,1)S(1)}, bf16[128,1024]{1,0:T(8,128)(2,1)S(1)}, u32[]{:S(2)}, u32[]{:S(2)}) collective-permute-start(bf16[128,1024]{1,0:T(8,128)(2,1)S(1)} %collective-permute-done.16.refs_4_), channel_id=1, source_target_pairs={{0,2},{2,0},{4,6},{6,4},{8,10},{10,8},{12,14},{14,12},{16,18},{18,... | collective-permute-start | bytes 786440 | tf_op jit(solution)/shard_map/ppermute | solution.py:23
  86.8 17.0 %collective-permute-start.23 = (bf16[128,1024]{1,0:T(8,128)(2,1)S(1)}, bf16[128,1024]{1,0:T(8,128)(2,1)S(1)}, u32[]{:S(2)}, u32[]{:S(2)}) collective-permute-start(bf16[128,1024]{1,0:T(8,128)(2,1)S(1)} %collective-permute-done.19.refs_5_), channel_id=1, source_target_pairs={{0,4},{2,6},{4,0},{6,2},{8,12},{10,14},{12,8},{14,10},{16,20},{18,... | collective-permute-start | bytes 786440 | tf_op jit(solution)/shard_map/ppermute | solution.py:23
  91.2 14.5 %collective-permute-start.18 = (bf16[128,1024]{1,0:T(8,128)(2,1)S(1)}, bf16[128,1024]{1,0:T(8,128)(2,1)S(1)}, u32[]{:S(2)}, u32[]{:S(2)}) collective-permute-start(bf16[128,1024]{1,0:T(8,128)(2,1)S(1)} %collective-permute-done.17.refs_1_), channel_id=1, source_target_pairs={{0,2},{2,0},{4,6},{6,4},{8,10},{10,8},{12,14},{14,12},{16,18},{18,... | collective-permute-start | bytes 786440 | tf_op jit(solution)/shard_map/ppermute | solution.py:23
  92.7 13.1 %collective-permute-start.21 = (bf16[128,1024]{1,0:T(8,128)(2,1)S(1)}, bf16[128,1024]{1,0:T(8,128)(2,1)S(1)}, u32[]{:S(2)}, u32[]{:S(2)}) collective-permute-start(bf16[128,1024]{1,0:T(8,128)(2,1)S(1)} %collective-permute-done.20.refs_2_), channel_id=1, source_target_pairs={{0,4},{2,6},{4,0},{6,2},{8,12},{10,14},{12,8},{14,10},{16,20},{18,... | collective-permute-start | bytes 786440 | tf_op jit(solution)/shard_map/ppermute | solution.py:23
  (27 other events, 137.4 us)
